TPU v7x, 32 devices: a whole 2x2x4 slice. The times are simulated.
32 devices in a mesh: gx: 8 (over z, x), gy: 4 (over y, core).
Axes of the slice: x: 2, y: 2, z: 4, core: 2. Of those that a mesh axis runs over, the one named last changes fastest.
Arguments:
- ambient_compactness: float32 [16, 8, 6, 6, 6, 128], P('gx', 'gy'), may hold values from 0.5 to 2
- ambient_flow_knots: float32 [16, 8, 3, 6, 6, 6, 128], P('gx', 'gy'), may hold values from -5 to 5
- ambient_hotness_knots: float32 [16, 8, 6, 6, 6, 128], P('gx', 'gy'), may hold values from 0.5 to 2
- parent_subdomain: int32 [8192], P(('gx', 'gy')), may hold values from 0 to 4095, as said below
- parcel_membership: int32 [8192], P(('gx', 'gy')), may hold values from 1 to 128
- particle_basis_coefficients: float32 [8192, 3, 6, 128], P(('gx', 'gy')), may hold values from -0.1 to 0.4
- parcel_velocities_list: float32 [8192, 3, 128], P(('gx', 'gy')), may hold values from -3 to 3
- parcel_breadth: float32 [8192, 128], P(('gx', 'gy')), may hold values from 0.5 to 2
- parcel_hotness: float32 [8192, 128], P(('gx', 'gy')), may hold values from 0.5 to 2
Outputs:
- residual: float32 [16, 8, 5, 6, 6, 6, 128], P('gx', 'gy')
Inputs may be any that keep to these rules, and one draw needn't show every extreme that they name: parent_subdomain[b] = s * 512 + l names element l of streamwise slab s within bin b's own spanwise slab. Of the 256 bins of one device at most 64 have their host on any one streamwise slab; the same three cyclically neighbouring slabs take exactly 64 bins from every device.
All inputs are finite; a program needn't handle non-finite values.
Results may differ from a plain program's by a relative error of at most 0.0003.
Values sent between devices are 32-bit elements; how exact they have to be, the bound alone decides.
No kernel may reach another device: no remote copies, remote signals or barrier semaphores. Data moves between devices by JAX's collectives and lax.ppermute only.
A program may use at most 128 MiB of HBM per device.

v0:
```python
import math

import jax
import jax.numpy as jnp
import numpy as np
from jax import lax
from jax.sharding import PartitionSpec as P

SPECIFIC_CP = 2.5
MU_GAS = 0.2
CONDUCTANCE = 0.2
PRANDTL = 0.72


def padded_2(cells, sides, width, closed):
    for axis, dim in sides:
        count = lax.axis_size(axis)
        ends = count if closed else count - 1
        head = lax.slice_in_dim(cells, 0, width, axis=dim)
        tail = lax.slice_in_dim(cells, cells.shape[dim] - width, cells.shape[dim], axis=dim)
        cells = jnp.concatenate(
            [
                lax.ppermute(tail, axis, [(i, (i + 1) % count) for i in range(ends)]),
                cells,
                lax.ppermute(head, axis, [((i + 1) % count, i) for i in range(ends)]),
            ],
            axis=dim,
        )
    return cells


def gll_tables():
    root_seven = math.sqrt(7.0)
    outer_node = math.sqrt(1.0 / 3.0 + 2.0 * root_seven / 21.0)
    inner_node = math.sqrt(1.0 / 3.0 - 2.0 * root_seven / 21.0)
    points = np.array([-1.0, -outer_node, -inner_node, inner_node, outer_node, 1.0])
    outer_weight = (14.0 - root_seven) / 30.0
    inner_weight = (14.0 + root_seven) / 30.0
    quadrature = np.array(
        [1.0 / 15.0, outer_weight, inner_weight, inner_weight, outer_weight, 1.0 / 15.0]
    )
    barycentric = np.ones(6)
    for row_at in range(6):
        for col_at in range(6):
            if col_at != row_at:
                barycentric[row_at] = barycentric[row_at] / (points[row_at] - points[col_at])
    matrix = np.zeros((6, 6))
    for row_at in range(6):
        for col_at in range(6):
            if col_at != row_at:
                matrix[row_at, col_at] = (
                    barycentric[col_at] / barycentric[row_at] / (points[row_at] - points[col_at])
                )
        matrix[row_at, row_at] = -np.sum(matrix[row_at])
    volume = quadrature[:, None, None] * quadrature[None, :, None] * quadrature[None, None, :]
    return (jnp.asarray(matrix, dtype=jnp.float32), jnp.asarray(volume, dtype=jnp.float32))


def apply_along(knot_readings, matrix, direction):
    einsum_forms = ("ai,...ijkz->...ajkz", "aj,...ijkz->...iakz", "ak,...ijkz->...ijaz")
    return jnp.einsum(
        einsum_forms[direction], matrix, knot_readings, precision=lax.Precision.HIGHEST
    )


def ambient_coupling(compactness_measure, flow_vectors, hotness_listing):
    matrix, volume = gll_tables()
    thermodynamic_push = compactness_measure * hotness_listing
    momentum = compactness_measure[..., None, :, :, :, :] * flow_vectors
    thermal_forcing = compactness_measure * (
        SPECIFIC_CP * hotness_listing + 0.5 * jnp.sum(flow_vectors * flow_vectors, axis=-5)
    )
    divergence = None
    for direction in range(3):
        speed_dir = flow_vectors[..., direction, :, :, :, :]
        stress = momentum * speed_dir[..., None, :, :, :, :]
        stress = stress.at[..., direction, :, :, :, :].add(thermodynamic_push)
        flux_dir = jnp.concatenate(
            [
                momentum[..., direction : direction + 1, :, :, :, :],
                stress,
                ((thermal_forcing + thermodynamic_push) * speed_dir)[..., None, :, :, :, :],
            ],
            axis=-5,
        )
        term_dir = apply_along(flux_dir, matrix, direction)
        divergence = term_dir if divergence is None else divergence + term_dir
    return -volume[:, :, :, None] * divergence


def cell_feedback(
    parent_subdomain_condition,
    lagrange_factors,
    grain_speed,
    parcel_breadths,
    parcel_hotness_advanced,
    tally_occupancy,
):
    bin_rows = lagrange_factors.shape[0]
    slot_count = lagrange_factors.shape[-1]
    basis_table = (
        lagrange_factors[:, 0, :, None, None, :]
        * lagrange_factors[:, 1, None, :, None, :]
        * lagrange_factors[:, 2, None, None, :, :]
    )
    basis_table = basis_table.reshape(bin_rows, 216, slot_count)
    stacked = parent_subdomain_condition.reshape(bin_rows, 5, 216)
    computed_readings = jnp.einsum(
        "bcn,bns->bcs", stacked, basis_table, precision=lax.Precision.HIGHEST
    )
    gas_density = computed_readings[:, 0]
    gas_velocity = computed_readings[:, 1:4]
    queried_ambient_hotness = computed_readings[:, 4]
    relative = gas_velocity - grain_speed
    reynolds_sq = (gas_density * parcel_breadths / MU_GAS) ** 2 * jnp.sum(
        relative * relative, axis=1
    ) + 1.0
    drag_factor = 1.0 + 0.15 * jnp.power(reynolds_sq, 0.3435)
    drag_force = 3.0 * math.pi * MU_GAS * (parcel_breadths * drag_factor)[:, None, :] * relative
    transfer_quotient = 2.0 + 0.6 * PRANDTL ** (1.0 / 3.0) * jnp.power(reynolds_sq, 0.25)
    hotness_tendency = (
        math.pi
        * CONDUCTANCE
        * parcel_breadths
        * transfer_quotient
        * (queried_ambient_hotness - parcel_hotness_advanced)
    )
    coupled_work = jnp.sum(drag_force * grain_speed, axis=1) + hotness_tendency
    live_slots = (
        jnp.arange(slot_count, dtype=jnp.int32)[None, :] < tally_occupancy[:, None]
    ).astype(jnp.float32)
    coupling = (
        jnp.concatenate([drag_force, coupled_work[:, None, :]], axis=1) * live_slots[:, None, :]
    )
    mapped_forcing = jnp.einsum(
        "bqs,bns->bqn", coupling, basis_table, precision=lax.Precision.HIGHEST
    )
    return mapped_forcing.reshape(bin_rows, 4 * 216)


def source_term_blocks(
    parent_subdomain_condition,
    lagrange_factors,
    flow_vectors,
    parcel_breadths,
    hotness_listing,
    tally_occupancy,
):
    bin_total = lagrange_factors.shape[0]
    block_rows = math.gcd(bin_total, 64)

    def split_rows(field_values):
        return field_values.reshape((bin_total // block_rows, block_rows) + field_values.shape[1:])

    outcome = lax.map(
        lambda group_rows: cell_feedback(
            group_rows[0], group_rows[1], group_rows[2], group_rows[3], group_rows[4], group_rows[5]
        ),
        tuple(
            (
                split_rows(field_values)
                for field_values in (
                    parent_subdomain_condition,
                    lagrange_factors,
                    flow_vectors,
                    parcel_breadths,
                    hotness_listing,
                    tally_occupancy,
                )
            )
        ),
    )
    return outcome.reshape((bin_total,) + outcome.shape[2:])


def assemble(knot_readings):
    lower_face = knot_readings[:, :, :, 0]
    upper_face = knot_readings[:, :, :, 5]
    rim_faces = jnp.stack([lower_face[0], upper_face[-1]], axis=0)
    padded = padded_2(rim_faces, (("gx", 0),), 1, False)
    next_lower = jnp.concatenate([lower_face[1:], padded[3:4]], axis=0)
    prev_upper = jnp.concatenate([padded[0:1], upper_face[:-1]], axis=0)
    knot_readings = (
        knot_readings.at[:, :, :, 5]
        .set(upper_face + next_lower)
        .at[:, :, :, 0]
        .set(lower_face + prev_upper)
    )
    lower_face = knot_readings[:, :, :, :, 0]
    upper_face = knot_readings[:, :, :, :, 5]
    rim_faces = jnp.stack([lower_face[:, 0], upper_face[:, -1]], axis=1)
    padded = padded_2(rim_faces, (("gy", 1),), 1, True)
    next_lower = jnp.concatenate([lower_face[:, 1:], padded[:, 3:4]], axis=1)
    prev_upper = jnp.concatenate([padded[:, 0:1], upper_face[:, :-1]], axis=1)
    knot_readings = (
        knot_readings.at[:, :, :, :, 5]
        .set(upper_face + next_lower)
        .at[:, :, :, :, 0]
        .set(lower_face + prev_upper)
    )
    lower_face = knot_readings[..., 0, :]
    upper_face = knot_readings[..., 5, :]
    next_lower = jnp.roll(lower_face, -1, axis=-1)
    prev_upper = jnp.roll(upper_face, 1, axis=-1)
    return (
        knot_readings.at[..., 5, :]
        .set(upper_face + next_lower)
        .at[..., 0, :]
        .set(lower_face + prev_upper)
    )


def shards(
    ambient_compactness,
    ambient_flow_knots,
    ambient_hotness_knots,
    parent_subdomain,
    parcel_membership,
    particle_basis_coefficients,
    parcel_velocities_list,
    parcel_breadth,
    parcel_hotness,
):
    sheet_abscissa = ambient_compactness.shape[0]
    sheet_ordinate = ambient_compactness.shape[1]
    height_coordinate = ambient_compactness.shape[-1]
    elem_total = sheet_abscissa * sheet_ordinate * height_coordinate
    node_state = jnp.concatenate(
        [ambient_compactness[:, :, None], ambient_flow_knots, ambient_hotness_knots[:, :, None]],
        axis=2,
    )
    state_rows = jnp.moveaxis(node_state, -1, 2).reshape(elem_total, 5 * 216)
    groups = lax.axis_size("gx")
    bin_total = parent_subdomain.shape[0]
    capacity = bin_total // 4
    target = parent_subdomain // elem_total
    local_elem = parent_subdomain % elem_total
    onehot = (target[:, None] == jnp.arange(groups, dtype=jnp.int32)[None, :]).astype(jnp.int32)
    earlier = jnp.cumsum(onehot, axis=0) - onehot
    slot_index = target * capacity + jnp.sum(earlier * onehot, axis=1)
    ambient_fraction = ambient_coupling(
        ambient_compactness, ambient_flow_knots, ambient_hotness_knots
    )

    def allot_places(field_values):
        empty = jnp.zeros((groups * capacity,) + field_values.shape[1:], field_values.dtype)
        return (
            empty.at[slot_index]
            .set(field_values)
            .reshape((groups, capacity) + field_values.shape[1:])
        )

    wanted = allot_places(local_elem)
    requests = lax.all_to_all(wanted, "gx", split_axis=0, concat_axis=0, tiled=True)
    owning_mesh_ordinal = requests.reshape(-1)
    copies = state_rows[owning_mesh_ordinal]
    returned = lax.all_to_all(
        copies.reshape(groups, capacity, copies.shape[-1]),
        "gx",
        split_axis=0,
        concat_axis=0,
        tiled=True,
    )
    parent_subdomain_condition = returned.reshape(groups * capacity, copies.shape[-1])[slot_index]
    own_terms = source_term_blocks(
        parent_subdomain_condition,
        particle_basis_coefficients,
        parcel_velocities_list,
        parcel_breadth,
        parcel_hotness,
        parcel_membership,
    )
    outgoing = allot_places(own_terms)
    mapped_forcing = lax.all_to_all(outgoing, "gx", split_axis=0, concat_axis=0, tiled=True)
    mapped_forcing = mapped_forcing.reshape(-1, own_terms.shape[-1])
    force_rows = (
        jnp.zeros((elem_total, 4 * 216), jnp.float32).at[owning_mesh_ordinal].add(mapped_forcing)
    )
    drag_loads = jnp.moveaxis(
        force_rows.reshape(sheet_abscissa, sheet_ordinate, height_coordinate, 4, 6, 6, 6), 2, -1
    )
    subdomain_accumulation = ambient_fraction - jnp.concatenate(
        [jnp.zeros_like(drag_loads[:, :, :1]), drag_loads], axis=2
    )
    return assemble(subdomain_accumulation)


def solution(mesh):
    placed = (
        P("gx", "gy", None, None, None, None),
        P("gx", "gy", None, None, None, None, None),
        P("gx", "gy", None, None, None, None),
        P(("gx", "gy")),
        P(("gx", "gy")),
        P(("gx", "gy"), None, None, None),
        P(("gx", "gy"), None, None),
        P(("gx", "gy"), None),
        P(("gx", "gy"), None),
    )
    return jax.shard_map(
        shards,
        mesh=mesh,
        in_specs=placed,
        out_specs=P("gx", "gy", None, None, None, None, None),
        check_vma=False,
    )
```

profile of v0, /device:TPU:24, one launch (start us, length us, event | category | flops | bytes accessed | tf_op | source)
XLA Modules:
  0.0 352.8 jit_solution(14366132679899217867)
XLA Ops:
  3.7 6.0 %all-to-all-start = ((s32[8,1,64]{2,1,0:T(1,128)}), s32[8,1,64]{2,1,0:T(1,128)S(1)}, u32[]{:S(2)}, u32[]{:S(2)}) async-start(s32[8,1,64]{2,1,0:T(1,128)} %all_to_all.12), calls=%async_computation | async-start | bytes 8192 | tf_op jit(solution)/shard_map/all_to_all | solution.py:254
  22.2 6.0 %all-to-all-start.1 = ((f32[8,64,1080]{2,1,0:T(8,128)}), f32[8,64,1080]{2,1,0:T(8,128)S(1)}, u32[]{:S(2)}, u32[]{:S(2)}) async-start(f32[8,64,1080]{2,1,0:T(8,128)} %bitcast.227), calls=%async_computation.1 | async-start | bytes 4718592 | tf_op jit(solution)/shard_map/all_to_all | solution.py:257
  34.3 45.7 %all-to-all-done.1 = f32[8,64,1080]{2,1,0:T(8,128)S(1)} async-done(((f32[8,64,1080]{2,1,0:T(8,128)}), f32[8,64,1080]{2,1,0:T(8,128)S(1)}, u32[]{:S(2)}, u32[]{:S(2)}) %all-to-all-start.1) | async-done | bytes 2211872 | tf_op jit(solution)/shard_map/all_to_all | solution.py:257
  82.2 123.0 %while.19 = (s32[]{:T(128)}, f32[4,64,864]{2,1,0:T(8,128)}, f32[4,64,128]{2,1,0:T(8,128)S(1)}, f32[4,64,1080]{2,1,0:T(8,128)}, f32[4,64,3,6,128]{4,1,0,3,2:T(8,1...) while((s32[]{:T(128)}, f32[4,64,864]{2,1,0:T(8,128)}, ...), condition=%wide.region_8.9_spmd, body=%wide.region_5.8_spmd.sunk | while | flops 193576960 | bytes 30481284 | solution.py:155
  85.9 9.3 %fusion.76 = f32[64,5,128]{2,1,0:T(8,128)S(1)} fusion(f32[64,5,216]{2,1,0:T(8,128)S(1)} %reshape.673, f32[64,216,128]{2,0,1:T(8,128)S(1)} %bitcast.223), kind=kOutput, calls=%fused_computation.7.clone.1 | convolution fusion | flops 106168320 | bytes 7518208 | tf_op jit(solution)/shard_map/while/body/eval_jaxpr/bcn,bns->bcs/dot_general | solution.py:108
  96.4 13.8 %fusion.83 = f32[64,4,216]{2,1,0:T(4,128)S(1)} fusion(f32[64,216,128]{2,0,1:T(8,128)S(1)} %bitcast.224, f32[64,1,128]{2,1,0:T(1,128)S(1)} %bitcast.237, f32[64,3,128]{2,1,0:T(4,128)S(1)} %get-tuple-element.312, f32[64,128]{1,0:T(8,128)S(1)} %fusion.82), kind=kOutput, calls=%fused_computation.5.clone.1 | convolution fusion | flops 85000192 | bytes 7462912 | tf_op jit(solution)/shard_map/while/body/eval_jaxpr/bqs,bns->bqn/dot_general | solution.py:135
  114.7 9.3 %fusion.76 = f32[64,5,128]{2,1,0:T(8,128)S(1)} fusion(f32[64,5,216]{2,1,0:T(8,128)S(1)} %reshape.673, f32[64,216,128]{2,0,1:T(8,128)S(1)} %bitcast.223), kind=kOutput, calls=%fused_computation.7.clone.1 | convolution fusion | flops 106168320 | bytes 7518208 | tf_op jit(solution)/shard_map/while/body/eval_jaxpr/bcn,bns->bcs/dot_general | solution.py:108
  125.1 13.8 %fusion.83 = f32[64,4,216]{2,1,0:T(4,128)S(1)} fusion(f32[64,216,128]{2,0,1:T(8,128)S(1)} %bitcast.224, f32[64,1,128]{2,1,0:T(1,128)S(1)} %bitcast.237, f32[64,3,128]{2,1,0:T(4,128)S(1)} %get-tuple-element.312, f32[64,128]{1,0:T(8,128)S(1)} %fusion.82), kind=kOutput, calls=%fused_computation.5.clone.1 | convolution fusion | flops 85000192 | bytes 7462912 | tf_op jit(solution)/shard_map/while/body/eval_jaxpr/bqs,bns->bqn/dot_general | solution.py:135
  143.4 9.3 %fusion.76 = f32[64,5,128]{2,1,0:T(8,128)S(1)} fusion(f32[64,5,216]{2,1,0:T(8,128)S(1)} %reshape.673, f32[64,216,128]{2,0,1:T(8,128)S(1)} %bitcast.223), kind=kOutput, calls=%fused_computation.7.clone.1 | convolution fusion | flops 106168320 | bytes 7518208 | tf_op jit(solution)/shard_map/while/body/eval_jaxpr/bcn,bns->bcs/dot_general | solution.py:108
  153.8 13.8 %fusion.83 = f32[64,4,216]{2,1,0:T(4,128)S(1)} fusion(f32[64,216,128]{2,0,1:T(8,128)S(1)} %bitcast.224, f32[64,1,128]{2,1,0:T(1,128)S(1)} %bitcast.237, f32[64,3,128]{2,1,0:T(4,128)S(1)} %get-tuple-element.312, f32[64,128]{1,0:T(8,128)S(1)} %fusion.82), kind=kOutput, calls=%fused_computation.5.clone.1 | convolution fusion | flops 85000192 | bytes 7462912 | tf_op jit(solution)/shard_map/while/body/eval_jaxpr/bqs,bns->bqn/dot_general | solution.py:135
  172.1 9.3 %fusion.76 = f32[64,5,128]{2,1,0:T(8,128)S(1)} fusion(f32[64,5,216]{2,1,0:T(8,128)S(1)} %reshape.673, f32[64,216,128]{2,0,1:T(8,128)S(1)} %bitcast.223), kind=kOutput, calls=%fused_computation.7.clone.1 | convolution fusion | flops 106168320 | bytes 7518208 | tf_op jit(solution)/shard_map/while/body/eval_jaxpr/bcn,bns->bcs/dot_general | solution.py:108
  182.6 13.8 %fusion.83 = f32[64,4,216]{2,1,0:T(4,128)S(1)} fusion(f32[64,216,128]{2,0,1:T(8,128)S(1)} %bitcast.224, f32[64,1,128]{2,1,0:T(1,128)S(1)} %bitcast.237, f32[64,3,128]{2,1,0:T(4,128)S(1)} %get-tuple-element.312, f32[64,128]{1,0:T(8,128)S(1)} %fusion.82), kind=kOutput, calls=%fused_computation.5.clone.1 | convolution fusion | flops 85000192 | bytes 7462912 | tf_op jit(solution)/shard_map/while/body/eval_jaxpr/bqs,bns->bqn/dot_general | solution.py:135
  208.6 5.9 %all-to-all-start.2 = ((f32[8,64,864]{2,1,0:T(8,128)}), f32[8,64,864]{2,1,0:T(8,128)}, u32[]{:S(2)}, u32[]{:S(2)}) async-start(f32[8,64,864]{2,1,0:T(8,128)} %bitcast.230), calls=%async_computation.2 | async-start | bytes 3670016 | tf_op jit(solution)/shard_map/all_to_all | solution.py:274
  223.9 4.8 %fusion.29 = f32[2,2,5,6,6,128,6]{5,6,4,3,2,1,0:T(8,128)} fusion(f32[6,6,1,1,1,1,1]{1,0,6,5,4,3,2:T(8,128)S(1)} %copy-done.16, f32[2,2,5,6,6,6,128]{6,3,5,4,1,0,2:T(8,128)S(1)} %get-tuple-element.248), kind=kOutput, calls=%fused_computation.58 | convolution fusion | flops 39813120 | bytes 4423824 | tf_op jit(solution)/shard_map/aj,...ijkz->...iakz/dot_general | solution.py:61
  228.7 4.5 %fusion.27 = f32[2,2,5,6,6,128,6]{5,6,4,3,2,1,0:T(8,128)} fusion(f32[6,6,1,1,1,1,1]{1,0,6,5,4,3,2:T(8,128)S(1)} %copy-done.16, f32[2,2,5,6,6,6,128]{6,3,5,4,1,0,2:T(8,128)S(1)} %get-tuple-element.249), kind=kOutput, calls=%fused_computation.56 | convolution fusion | flops 39813120 | bytes 4423824 | tf_op jit(solution)/shard_map/ak,...ijkz->...ijaz/dot_general | solution.py:61
  233.1 21.7 %all-to-all-done.2 = f32[8,64,864]{2,1,0:T(8,128)} async-done(((f32[8,64,864]{2,1,0:T(8,128)}), f32[8,64,864]{2,1,0:T(8,128)}, u32[]{:S(2)}, u32[]{:S(2)}) %all-to-all-start.2) | async-done | bytes 1769504 | tf_op jit(solution)/shard_map/all_to_all | solution.py:274
  254.8 6.3 %scatter_custom_fusion.2 = f32[512,864]{1,0:T(8,128)S(1)} fusion(s32[512]{0:T(512)S(1)} %bitcast.250, f32[512,864]{1,0:T(8,128)} %bitcast.44, f32[]{:T(128)} %constant.317.clone.1), kind=kCustom, calls=%fused_computation.63 | custom fusion | flops 442368 | bytes 1769984 | tf_op jit(solution)/shard_map/scatter-add | solution.py:277
  267.3 6.4 %fusion.26 = f32[2,2,5,6,6,6,128]{6,3,5,4,2,1,0:T(8,128)S(1)} fusion(f32[2,2,5,6,6,128,6]{5,6,4,3,2,1,0:T(8,128)} %fusion.27, f32[2,2,5,6,6,128,6]{5,6,4,3,2,1,0:T(8,128)S(1)} %copy-done.3, f32[2,2,4,6,6,6,128]{6,3,5,4,2,1,0:T(8,128)S(1)} %bitcast.226, f32[6,6,1,1,1,1,1]{1,0,6,5,4,3,2:T(8,128)S(1)} %copy-done.16, ...), kind=kOutput, calls=%fused_computation.54 | convolution fusion | flops 43130880 | bytes 10617840 | tf_op jit(solution)/shard_map/ai,...ijkz->...ajkz/dot_general | solution.py:61
  277.2 4.0 %collective-permute-start = (f32[1,2,5,6,6,128]{5,0,4,3,2,1:T(1,128)S(1)}, f32[1,2,5,6,6,128]{5,0,4,3,2,1:T(1,128)S(1)}, u32[]{:S(2)}, u32[]{:S(2)}) collective-permute-start(f32[1,2,5,6,6,128]{5,0,4,3,2,1:T(1,128)S(1)} %get-tuple-element.223), channel_id=1, source_target_pairs={{4,0},{8,4},{12,8},{16,12},{20,16},{24,20},{28,24},{5,1},{9,5},{13... | collective-permute-start | bytes 552968 | tf_op jit(solution)/shard_map/ppermute | solution.py:25
  283.7 3.9 %collective-permute-done = f32[1,2,5,6,6,128]{5,0,4,3,2,1:T(1,128)S(1)} collective-permute-done((f32[1,2,5,6,6,128]{5,0,4,3,2,1:T(1,128)S(1)}, f32[1,2,5,6,6,128]{5,0,4,3,2,1:T(1,128)S(1)}, u32[]{:S(2)}, u32[]{:S(2)}) %collective-permute-start) | collective-permute-done | bytes 184352 | tf_op jit(solution)/shard_map/ppermute | solution.py:25
  289.3 16.9 %scatter.36 = f32[2,2,5,6,6,6,128]{6,3,5,4,2,1,0:T(8,128)S(1)} dynamic-update-slice(f32[2,2,5,6,6,6,128]{6,3,5,4,2,1,0:T(8,128)S(1)} %fusion.26, f32[2,2,5,1,6,6,128]{6,3,5,4,2,1,0:T(1,128)} %get-tuple-element.221, s32[]{:T(128)} %constant.315.clone.1, s32[]{:T(128)} %constant.315.clone.1, s32[]{:T(128)} %constant.315.clone.1, s32[]{:T(128)} %constant.326.clone.1, s32[]{:T(128)} %constant.315.clone.1, ...) | dynamic-update-slice | bytes 737284 | tf_op jit(solution)/shard_map/scatter | solution.py:185
  306.2 18.4 %scatter.39 = f32[2,2,5,6,6,6,128]{6,3,5,4,2,1,0:T(8,128)S(1)} dynamic-update-slice(f32[2,2,5,6,6,6,128]{6,3,5,4,2,1,0:T(8,128)S(1)} %scatter.36, f32[2,2,5,1,6,6,128]{6,3,5,4,2,1,0:T(1,128)S(1)} %get-tuple-element.220, s32[]{:T(128)} %constant.315.clone.1, s32[]{:T(128)} %constant.315.clone.1, s32[]{:T(128)} %constant.315.clone.1, s32[]{:T(128)} %constant.315.clone.1, s32[]{:T(128)} %constant.315.clone.1, ...) | dynamic-update-slice | bytes 737284 | tf_op jit(solution)/shard_map/scatter | solution.py:187
  326.2 3.5 collective-permute-done.2
  330.7 5.0 %collective-permute-done.3 = f32[2,1,5,6,6,128]{5,3,4,2,0,1:T(8,128)S(1)} collective-permute-done((f32[2,1,5,6,6,128]{5,3,4,2,0,1:T(8,128)S(1)}, f32[2,1,5,6,6,128]{5,3,4,2,0,1:T(8,128)S(1)}, u32[]{:S(2)}, u32[]{:S(2)}) %collective-permute-start.3) | collective-permute-done | bytes 184352 | tf_op jit(solution)/shard_map/ppermute | solution.py:23
  (162 shorter events, 92.4 us)
Async XLA Ops:
  3.7 14.3 %all-to-all-start = ((s32[8,1,64]{2,1,0:T(1,128)}), s32[8,1,64]{2,1,0:T(1,128)S(1)}, u32[]{:S(2)}, u32[]{:S(2)}) async-start(s32[8,1,64]{2,1,0:T(1,128)} %all_to_all.12), calls=%async_computation | async-start | bytes 8192 | tf_op jit(solution)/shard_map/all_to_all | solution.py:254
  22.2 57.7 %all-to-all-start.1 = ((f32[8,64,1080]{2,1,0:T(8,128)}), f32[8,64,1080]{2,1,0:T(8,128)S(1)}, u32[]{:S(2)}, u32[]{:S(2)}) async-start(f32[8,64,1080]{2,1,0:T(8,128)} %bitcast.227), calls=%async_computation.1 | async-start | bytes 4718592 | tf_op jit(solution)/shard_map/all_to_all | solution.py:257
  28.2 2.9 copy-start.17
  28.2 3.0 copy-start.14
  80.0 2.2 copy-start.13
  205.1 9.4 %copy-start = (f32[2,2,3,6,6,6,128]{6,1,5,4,3,2,0:T(2,128)S(1)}, f32[2,2,3,6,6,6,128]{6,1,5,4,3,2,0:T(2,128)}, u32[]{:S(2)}) copy-start(f32[2,2,3,6,6,6,128]{6,1,5,4,3,2,0:T(2,128)} %param.32) | copy-start | bytes 3981316
  208.6 6.6 %copy-start.2 = (f32[2,2,3,6,6,6,128]{6,3,5,4,1,0,2:T(8,128)S(1)}, f32[2,2,3,6,6,6,128]{6,3,5,4,1,0,2:T(8,128)}, u32[]{:S(2)}) copy-start(f32[2,2,3,6,6,6,128]{6,3,5,4,1,0,2:T(8,128)} %copy.175) | copy-start | bytes 3981316
  208.6 6.6 %copy-start.5 = (f32[2,2,6,6,6,128]{5,1,4,3,2,0:T(2,128)S(1)}, f32[2,2,6,6,6,128]{5,1,4,3,2,0:T(2,128)}, u32[]{:S(2)}) copy-start(f32[2,2,6,6,6,128]{5,1,4,3,2,0:T(2,128)} %param.33) | copy-start | bytes 1327108
  208.6 46.3 %all-to-all-start.2 = ((f32[8,64,864]{2,1,0:T(8,128)}), f32[8,64,864]{2,1,0:T(8,128)}, u32[]{:S(2)}, u32[]{:S(2)}) async-start(f32[8,64,864]{2,1,0:T(8,128)} %bitcast.230), calls=%async_computation.2 | async-start | bytes 3670016 | tf_op jit(solution)/shard_map/all_to_all | solution.py:274
  217.4 1.1 copy-start.9
  219.0 1.1 copy-start.7
  219.0 1.4 copy-start.8
  220.4 1.0 copy-start.6
  221.9 1.3 copy-start.4
  262.8 3.0 copy-start.15
  265.2 1.8 copy-start.3
  265.2 1.9 copy-start.10
  265.2 2.1 copy-start.11
  274.2 9.5 %collective-permute-start.1 = (f32[1,2,5,6,6,128]{5,0,4,3,2,1:T(1,128)S(1)}, f32[1,2,5,6,6,128]{5,0,4,3,2,1:T(1,128)S(1)}, u32[]{:S(2)}, u32[]{:S(2)}) collective-permute-start(f32[1,2,5,6,6,128]{5,0,4,3,2,1:T(1,128)S(1)} %get-tuple-element.222), channel_id=1, source_target_pairs={{0,4},{4,8},{8,12},{12,16},{16,20},{20,24},{24,28},{1,5},{5,9},{9,... | collective-permute-start | bytes 552968 | tf_op jit(solution)/shard_map/ppermute | solution.py:23
  277.2 10.3 %collective-permute-start = (f32[1,2,5,6,6,128]{5,0,4,3,2,1:T(1,128)S(1)}, f32[1,2,5,6,6,128]{5,0,4,3,2,1:T(1,128)S(1)}, u32[]{:S(2)}, u32[]{:S(2)}) collective-permute-start(f32[1,2,5,6,6,128]{5,0,4,3,2,1:T(1,128)S(1)} %get-tuple-element.223), channel_id=1, source_target_pairs={{4,0},{8,4},{12,8},{16,12},{20,16},{24,20},{28,24},{5,1},{9,5},{13... | collective-permute-start | bytes 552968 | tf_op jit(solution)/shard_map/ppermute | solution.py:25
  324.8 4.9 %collective-permute-start.2 = (f32[2,1,5,6,6,128]{5,3,4,2,0,1:T(8,128)S(1)}, f32[2,1,5,6,6,128]{5,3,4,2,0,1:T(8,128)S(1)}, u32[]{:S(2)}, u32[]{:S(2)}) collective-permute-start(f32[2,1,5,6,6,128]{5,3,4,2,0,1:T(8,128)S(1)} %get-tuple-element.244), channel_id=1, source_target_pairs={{1,0},{2,1},{3,2},{0,3},{5,4},{6,5},{7,6},{4,7},{9,8},{10,9},{11,1... | collective-permute-start | bytes 552968 | tf_op jit(solution)/shard_map/ppermute | solution.py:25
  329.8 5.8 %collective-permute-start.3 = (f32[2,1,5,6,6,128]{5,3,4,2,0,1:T(8,128)S(1)}, f32[2,1,5,6,6,128]{5,3,4,2,0,1:T(8,128)S(1)}, u32[]{:S(2)}, u32[]{:S(2)}) collective-permute-start(f32[2,1,5,6,6,128]{5,3,4,2,0,1:T(8,128)S(1)} %get-tuple-element.239), channel_id=1, source_target_pairs={{0,1},{1,2},{2,3},{3,0},{4,5},{5,6},{6,7},{7,4},{8,9},{9,10},{10,1... | collective-permute-start | bytes 552968 | tf_op jit(solution)/shard_map/ppermute | solution.py:23
  335.8 3.1 copy-start.1
  340.7 7.3 %copy-start.12 = (f32[2,2,5,6,6,1,127]{6,3,5,4,2,1,0:T(8,128)S(1)}, f32[2,2,5,6,6,1,127]{6,3,5,4,2,1,0:T(8,128)}, u32[]{:S(2)}) copy-start(f32[2,2,5,6,6,1,127]{6,3,5,4,2,1,0:T(8,128)} %slice_bitcast_fusion.7) | copy-start | bytes 1097284
  (1 other events, 0.7 us)
where the time goes:
time: 360 us; the launch traced here: 353 us
  matrix products  108 us (30%)
  local copies, waits for them, and re-layouts  97.2 us (27%)
  waiting for transfers between devices  82.2 us (23%)
  other arithmetic  29.4 us (8%)
  starting transfers between devices  26.9 us (7%)
  loops' own time  8.39 us (2%)
    dot_general x4, matrix products, cell_feedback(): jnp.einsum('bqs,bns->bqn', coupling, basis_table, precision=lax.Precision...  55.2 us
    all_to_all x1, waiting for transfers between devices, shards(): lax.all_to_all(copies.reshape(groups, capacity, copies.shape[-1]), 'gx',...  45.7 us
    dot_general x4, matrix products, cell_feedback(): jnp.einsum('bcn,bns->bcs', stacked, basis_table, precision=lax.Precision....  37.1 us
    scatter x2, local copies, waits for them, and re-layouts, assemble(): knot_readings = knot_readings.at[:, :, :, 5].set(upper_face + next_lower)...  35.3 us
    all_to_all x1, waiting for transfers between devices, shards(): lax.all_to_all(outgoing, 'gx', split_axis=0, concat_axis=0, tiled=True)  21.7 us
    dot_general x3, matrix products, apply_along(): jnp.einsum(einsum_forms[direction], matrix, knot_readings, precision=lax....  15.6 us
    unnamed x41, local copies, waits for them, and re-layouts  8.45 us
    another operation x1, loops' own time, source_term_blocks(): lax.map(lambda group_rows: cell_feedback(group_rows[0], group_rows[1], gr...  8.39 us
  transfers between devices with their start and end apart: 7, of which 6 were waited for; matrix products, arithmetic and copies ran while one was open for 8% of the time, Pallas kernels for 0%

commit v1 on v0

v1 whole, which is shorter than its diff:
```python
import functools
import math

import jax
import jax.numpy as jnp
import numpy as np
from jax import lax
from jax.experimental import pallas as pl
from jax.experimental.pallas import tpu as pltpu
from jax.sharding import PartitionSpec as P

SPECIFIC_CP = 2.5
MU_GAS = 0.2
CONDUCTANCE = 0.2
PRANDTL = 0.72

NODES = 216
LANES = 128
CHUNKS = 2
F32 = jnp.float32
BF16 = jnp.bfloat16
I32 = jnp.int32
NT = (((1,), (1,)), ((), ()))


def gll_operator():
    root_seven = math.sqrt(7.0)
    outer_node = math.sqrt(1.0 / 3.0 + 2.0 * root_seven / 21.0)
    inner_node = math.sqrt(1.0 / 3.0 - 2.0 * root_seven / 21.0)
    points = np.array([-1.0, -outer_node, -inner_node, inner_node, outer_node, 1.0])
    outer_weight = (14.0 - root_seven) / 30.0
    inner_weight = (14.0 + root_seven) / 30.0
    w = np.array([1.0 / 15.0, outer_weight, inner_weight, inner_weight, outer_weight, 1.0 / 15.0])
    bary = np.ones(6)
    for r in range(6):
        for c in range(6):
            if c != r:
                bary[r] = bary[r] / (points[r] - points[c])
    dm = np.zeros((6, 6))
    for r in range(6):
        for c in range(6):
            if c != r:
                dm[r, c] = bary[c] / bary[r] / (points[r] - points[c])
        dm[r, r] = -np.sum(dm[r])
    eye = np.eye(6)
    volume = np.kron(np.kron(w, w), w)
    blocks = [
        np.kron(np.kron(dm, eye), eye),
        np.kron(np.kron(eye, dm), eye),
        np.kron(np.kron(eye, eye), dm),
    ]
    return (-volume[:, None] * np.concatenate(blocks, axis=1)).astype(np.float32)


def halves(x):
    hi = x.astype(BF16)
    return hi, (x - hi.astype(F32)).astype(BF16)


def thirds(x):
    hi = x.astype(BF16)
    rest = x - hi.astype(F32)
    mid = rest.astype(BF16)
    return hi, mid, (rest - mid.astype(F32)).astype(BF16)


def pick(x, weights):
    hi, lo = halves(x)
    return jnp.dot(hi, weights, preferred_element_type=F32) + jnp.dot(
        lo, weights, preferred_element_type=F32
    )


def iota(shape, dim):
    return lax.broadcasted_iota(I32, shape, dim)


def sorted_places(ids, elems, groups):
    rows, bins = ids.shape
    shift = elems.bit_length() - 1
    assert elems == 1 << shift
    slab = jnp.right_shift(ids, shift)
    upper = (iota((bins, bins), 0) < iota((bins, bins), 1)).astype(F32).astype(BF16)
    places, firsts = [], []
    group_of = iota((groups, bins), 0)
    for d in range(rows):
        mine = jnp.broadcast_to(slab[d : d + 1], (groups, bins))
        hit = (mine == group_of).astype(F32)
        earlier = jnp.dot(hit.astype(BF16), upper, preferred_element_type=F32)
        first = jnp.sum((mine < group_of).astype(F32), axis=1, keepdims=True)
        places.append(jnp.sum(hit * (earlier + first), axis=0, keepdims=True).astype(I32))
        firsts.append(first.astype(I32))
    return places, slab, firsts


def state_columns(rho_ref, vel_ref, hot_ref, ex, ey):
    out = []
    for q in range(5):
        cols = []
        for x in range(ex):
            for y in range(ey):
                if q == 0 or q == 4:
                    ref, base = (rho_ref if q == 0 else hot_ref), x * NODES * ey + y
                else:
                    ref, base = vel_ref, (x * 3 + q - 1) * NODES * ey + y
                cols.append(ref[pl.ds(base, NODES, stride=ey), :])
        out.append(cols)
    return out


def gather_kernel(c, elems, ex, ey, me_ref, ids_ref, rho_ref, vel_ref, hot_ref, out_ref, req_ref, work):
    groups, bins = ids_ref.shape
    me = me_ref[0]
    cap = out_ref.shape[2] // 4
    slots = groups * cap
    ids = ids_ref[...]
    places, slab, firsts = sorted_places(ids, elems, groups)
    elem = jnp.bitwise_and(ids, elems - 1)
    sub = iota((LANES, bins), 0)
    slot_of = iota((slots, bins), 0)
    row_table = jnp.zeros((LANES, slots), F32)
    col_table = jnp.zeros((slots, LANES), F32)
    for d in range(groups):
        place = places[d]
        first = jnp.sum(
            jnp.where(iota((groups, 1), 0) == me, firsts[d], 0).astype(F32), axis=0, keepdims=True
        ).astype(I32)
        begin = jnp.right_shift(first - c + 1, 1)
        here = (slab[d : d + 1] == me) & (jnp.bitwise_and(place, 1) == c)
        slot = jnp.where(here, jnp.right_shift(place, 1) - begin + d * cap, -1)
        match = (jnp.broadcast_to(slot, (slots, bins)) == slot_of).astype(F32).astype(BF16)
        e = jnp.broadcast_to(elem[d : d + 1], (LANES, bins))
        parts = jnp.where(
            sub == 0,
            jnp.bitwise_and(e, 255),
            jnp.where(sub == 1, jnp.right_shift(e, 8), jnp.where(sub == 2, 1, 0)),
        )
        parts = parts.astype(F32).astype(BF16)
        row_table += lax.dot_general(parts, match, NT, preferred_element_type=F32)
        col_table += lax.dot_general(match, parts, NT, preferred_element_type=F32)
    wanted = jnp.where(row_table[2:3] > 0.5, row_table[0:1] + 256.0 * row_table[1:2], -1.0).astype(I32)
    wanted_col = jnp.where(
        col_table[:, 2:3] > 0.5, col_table[:, 0:1] + 256.0 * col_table[:, 1:2], -1.0
    ).astype(I32)
    req_ref[...] = jnp.broadcast_to(wanted_col, (slots, LANES))
    onehot = (jnp.broadcast_to(wanted, (elems, slots)) == iota((elems, slots), 0)).astype(F32).astype(BF16)
    state = state_columns(rho_ref, vel_ref, hot_ref, ex, ey)
    for q in range(5):
        work[q * NODES : (q + 1) * NODES, :] = pick(jnp.concatenate(state[q], axis=1), onehot)
    rows = out_ref.shape[1]
    pad = 4 * rows - 5 * NODES
    work[5 * NODES : 4 * rows, :] = jnp.zeros((pad, slots), F32)
    lane_group = iota((rows, LANES), 1) // cap
    for tile in range(slots // LANES):
        block = [
            work[g * rows : (g + 1) * rows, tile * LANES : (tile + 1) * LANES] for g in range(4)
        ]
        for at in range(4):
            total = None
            for g in range(4):
                turn = ((g - at) % 4) * cap
                moved = block[g] if turn == 0 else pltpu.roll(block[g], turn, 1)
                total = moved if total is None else jnp.where(lane_group == g, moved, total)
            out_ref[tile * 4 + at] = total


def arrange_kernel(elems, groups, ids_ref, count_ref, basis_ref, vel_ref, breadth_ref, hot_ref, out_ref, live_ref):
    bins = ids_ref.shape[1]
    half = bins // CHUNKS
    places, _, _ = sorted_places(ids_ref[...], elems, groups)
    place = places[0]
    target = jnp.bitwise_and(place, 1) * half + jnp.right_shift(place, 1)
    move = (jnp.broadcast_to(target, (bins, bins)) == iota((bins, bins), 0)).astype(F32).astype(BF16)
    count = jnp.broadcast_to(count_ref[...], (8, bins)).astype(F32).astype(BF16)
    live = lax.dot_general(count, move, NT, preferred_element_type=F32)
    for c in range(CHUNKS):
        live_ref[c] = live[:, c * half : (c + 1) * half].astype(I32)
    sources = [basis_ref.at[m] for m in range(18)] + [vel_ref.at[m] for m in range(3)]
    sources += [breadth_ref, hot_ref]
    for m, source in enumerate(sources):
        hi, mid, lo = thirds(source[...])
        moved = (
            jnp.dot(move, hi, preferred_element_type=F32)
            + jnp.dot(move, mid, preferred_element_type=F32)
            + jnp.dot(move, lo, preferred_element_type=F32)
        )
        for c in range(CHUNKS):
            out_ref[c, m] = moved[c * half : (c + 1) * half].T


def fluid_kernel(ex, ey, op_ref, rho_ref, vel_ref, hot_ref, out_ref, lead, flow, push):
    state = state_columns(rho_ref, vel_ref, hot_ref, ex, ey)
    for at in range(ex * ey):
        lanes = slice(at * LANES, (at + 1) * LANES)
        rho, hot = state[0][at], state[4][at]
        u = [state[1 + d][at] for d in range(3)]
        p = rho * hot
        energy = rho * (SPECIFIC_CP * hot + 0.5 * (u[0] * u[0] + u[1] * u[1] + u[2] * u[2]))
        push[:, lanes] = p
        lead[0, :, lanes] = rho
        lead[4, :, lanes] = energy + p
        for d in range(3):
            flow[d, :, lanes] = u[d]
            lead[1 + d, :, lanes] = rho * u[d]

    def component(q, _):
        parts = []
        for d in range(3):
            extra = jnp.where(q == d + 1, 1.0, 0.0).astype(F32)
            parts.append(lead[q] * flow[d] + extra * push[...])
        flux = jnp.concatenate(parts, axis=0)
        out_ref[q] = jnp.dot(
            op_ref[...], flux, preferred_element_type=F32, precision=lax.Precision.HIGHEST
        )
        return 0

    lax.fori_loop(0, 5, component, 0)


def particle_kernel(c, firsts_ref, recv_ref, data_ref, live_ref, out_ref, host, work, force):
    groups, rows, _ = recv_ref.shape
    cap = LANES // 4
    slots_t = data_ref.shape[1]
    width = data_ref.shape[2]
    begins = [jnp.right_shift(firsts_ref[g] - c + 1, 1) for g in range(groups + 1)]

    row = iota((LANES, width), 0)
    col = iota((LANES, width), 1)
    slot = jnp.bitwise_and(row, cap - 1)
    lane_group = jnp.right_shift(row, cap.bit_length() - 1)
    bases = [(col - slot == begins[d]) & (col < begins[d + 1]) for d in range(groups)]
    got_hi, got_lo = halves(jnp.concatenate([recv_ref[d] for d in range(groups)], axis=1))
    for g in range(4):
        weights = jnp.concatenate(
            [(bases[d] & (lane_group == g)).astype(F32).astype(BF16) for d in range(groups)], axis=0
        )
        host[g * rows : (g + 1) * rows, :] = jnp.dot(
            got_hi, weights, preferred_element_type=F32
        ) + jnp.dot(got_lo, weights, preferred_element_type=F32)

    step = 16
    live = live_ref[0:1, :]

    def sample(tb, _):
        at = pl.ds(pl.multiple_of(tb * step, step), step)
        b0 = [data_ref[i, at, :] for i in range(6)]
        b1 = [data_ref[6 + i, at, :] for i in range(6)]
        b2 = [data_ref[12 + i, at, :] for i in range(6)]
        sampled = []
        for q in range(5):
            over_i = None
            for i in range(6):
                over_j = None
                for j in range(6):
                    over_k = None
                    for k in range(6):
                        n = q * NODES + i * 36 + j * 6 + k
                        term = host[n : n + 1, :] * b2[k]
                        over_k = term if over_k is None else over_k + term
                    term = over_k * b1[j]
                    over_j = term if over_j is None else over_j + term
                term = over_j * b0[i]
                over_i = term if over_i is None else over_i + term
            sampled.append(over_i)
        v = [data_ref[18 + d, at, :] for d in range(3)]
        breadth, hot = data_ref[21, at, :], data_ref[22, at, :]
        rel = [sampled[1 + d] - v[d] for d in range(3)]
        ratio = sampled[0] * breadth * (1.0 / MU_GAS)
        reynolds = ratio * ratio * (rel[0] * rel[0] + rel[1] * rel[1] + rel[2] * rel[2]) + 1.0
        drag = (3.0 * math.pi * MU_GAS) * (breadth * (1.0 + 0.15 * jnp.exp(0.3435 * jnp.log(reynolds))))
        transfer = 2.0 + 0.6 * PRANDTL ** (1.0 / 3.0) * jnp.sqrt(jnp.sqrt(reynolds))
        heat = (math.pi * CONDUCTANCE) * breadth * transfer * (sampled[4] - hot)
        on = iota((step, width), 0) + tb * step < live
        pull = [drag * rel[d] for d in range(3)]
        power = pull[0] * v[0] + pull[1] * v[1] + pull[2] * v[2] + heat
        for r, value in enumerate(pull + [power]):
            force[r, at, :] = jnp.where(on, value, 0.0)
        return 0

    lax.fori_loop(0, slots_t // step, sample, 0)

    def project(ij, _):
        i, j = ij // 6, ij % 6
        acc = [[None] * 6 for _ in range(4)]
        for tb in range(slots_t // 8):
            at = slice(tb * 8, tb * 8 + 8)
            both = data_ref[i, at, :] * data_ref[6 + j, at, :]
            b2 = [data_ref[12 + k, at, :] for k in range(6)]
            for r in range(4):
                g = force[r, at, :] * both
                for k in range(6):
                    term = g * b2[k]
                    acc[r][k] = term if acc[r][k] is None else acc[r][k] + term
        for r in range(4):
            for k in range(6):
                work[pl.ds(r * NODES + ij * 6 + k, 1), :] = jnp.sum(acc[r][k], axis=0, keepdims=True)
        return 0

    lax.fori_loop(0, 36, project, 0)

    row = iota((width, LANES), 0)
    col = iota((width, LANES), 1)
    slot = jnp.bitwise_and(col, cap - 1)
    lane_group = jnp.right_shift(col, cap.bit_length() - 1)
    give_hi, give_lo = halves(
        jnp.concatenate([work[r * NODES : (r + 1) * NODES, :] for r in range(4)], axis=1)
    )
    for d in range(groups):
        base = (row - slot == begins[d]) & (row < begins[d + 1])
        weights = jnp.concatenate(
            [(base & (lane_group == r)).astype(F32).astype(BF16) for r in range(4)], axis=0
        )
        out_ref[d] = jnp.dot(give_hi, weights, preferred_element_type=F32) + jnp.dot(
            give_lo, weights, preferred_element_type=F32
        )


def collect(recv_ref, req_ref, elems):
    groups, rows, _ = recv_ref.shape
    cap = LANES // 4
    got = jnp.concatenate([recv_ref[d] for d in range(groups)], axis=1)
    lane_group = jnp.right_shift(jnp.bitwise_and(iota(got.shape, 1), LANES - 1), cap.bit_length() - 1)
    weights = []
    for d in range(groups):
        want = req_ref[d * cap : (d + 1) * cap, :]
        parts = [(want == iota(want.shape, 1) + t * LANES) for t in range(elems // LANES)]
        part = jnp.concatenate([p.astype(F32).astype(BF16) for p in parts], axis=1)
        weights += [part] * 4
    weights = jnp.concatenate(weights, axis=0)
    hi, lo = halves(got)
    zero = jnp.zeros_like(hi)
    out = []
    for r in range(4):
        mine = lane_group == r
        out.append(
            jnp.dot(jnp.where(mine, hi, zero), weights, preferred_element_type=F32)
            + jnp.dot(jnp.where(mine, lo, zero), weights, preferred_element_type=F32)
        )
    return out


def load_kernel(recv_ref, req_ref, fluid_ref, out_ref):
    loads = collect(recv_ref, req_ref, fluid_ref.shape[2])
    out_ref[0] = fluid_ref[0]
    for r in range(4):
        out_ref[1 + r] = fluid_ref[1 + r] - loads[r]


def join_kernel(ex, ey, recv_ref, req_ref, part_ref, out_ref, xlo_ref, xhi_ref, ylo_ref, yhi_ref, corner_ref):
    loads = collect(recv_ref, req_ref, part_ref.shape[2])
    out_ref[0] = part_ref[0]
    for r in range(4):
        out_ref[1 + r] = part_ref[1 + r] - loads[r]
    wide = ey * LANES
    for q in range(5):
        for x in range(ex - 1):
            a, b = slice(x * wide, (x + 1) * wide), slice((x + 1) * wide, (x + 2) * wide)
            total = out_ref[q, 180:216, a] + out_ref[q, 0:36, b]
            out_ref[q, 180:216, a] = total
            out_ref[q, 0:36, b] = total
        for x in range(ex):
            for y in range(ey - 1):
                base = x * wide + y * LANES
                a, b = slice(base, base + LANES), slice(base + LANES, base + 2 * LANES)
                for i in range(6):
                    total = out_ref[q, 36 * i + 30 : 36 * i + 36, a] + out_ref[q, 36 * i : 36 * i + 6, b]
                    out_ref[q, 36 * i + 30 : 36 * i + 36, a] = total
                    out_ref[q, 36 * i : 36 * i + 6, b] = total
        last = (ex - 1) * wide
        xlo_ref[q] = out_ref[q, 0:36, 0:wide]
        xhi_ref[q] = out_ref[q, 180:216, last : last + wide]
        for x in range(ex):
            dst = slice(x * LANES, (x + 1) * LANES)
            lo = slice(x * wide, x * wide + LANES)
            hi = slice((x + 1) * wide - LANES, (x + 1) * wide)
            for i in range(6):
                ylo_ref[q, 6 * i : 6 * i + 6, dst] = out_ref[q, 36 * i : 36 * i + 6, lo]
                yhi_ref[q, 6 * i : 6 * i + 6, dst] = out_ref[q, 36 * i + 30 : 36 * i + 36, hi]
        for at, (x, y) in enumerate(((0, 0), (0, 1), (1, 0), (1, 1))):
            start = 180 * x + 30 * y
            lanes = x * last + y * (wide - LANES)
            corner_ref[at, q] = jnp.zeros((8, LANES), F32)
            corner_ref[at, q, 0:6, :] = out_ref[q, start : start + 6, lanes : lanes + LANES]


def finish_kernel(ex, ey, part_ref, xl_ref, xr_ref, yl_ref, yr_ref, c00_ref, c01_ref, c10_ref, c11_ref, out_ref, work):
    for q in range(5):
        for at in range(ex * ey):
            work[at] = part_ref[q, :, at * LANES : (at + 1) * LANES]
        for y in range(ey):
            lanes = slice(y * LANES, (y + 1) * LANES)
            work[y, 0:36, :] += xl_ref[q, :, lanes]
            work[(ex - 1) * ey + y, 180:216, :] += xr_ref[q, :, lanes]
        for x in range(ex):
            lanes = slice(x * LANES, (x + 1) * LANES)
            for i in range(6):
                work[x * ey, 36 * i : 36 * i + 6, :] += yl_ref[q, 6 * i : 6 * i + 6, lanes]
                work[x * ey + ey - 1, 36 * i + 30 : 36 * i + 36, :] += yr_ref[q, 6 * i : 6 * i + 6, lanes]
        for ref, x, y in ((c00_ref, 0, 0), (c01_ref, 0, 1), (c10_ref, 1, 0), (c11_ref, 1, 1)):
            start = 180 * x + 30 * y
            work[x * (ex - 1) * ey + y * (ey - 1), start : start + 6, :] += ref[q, 0:6, :]
        for x in range(ex):
            for y in range(ey):
                at = x * ey + y
                lower = work[at, pl.ds(0, 36, stride=6), :]
                upper = work[at, pl.ds(5, 36, stride=6), :]
                work[at, pl.ds(5, 36, stride=6), :] = upper + pltpu.roll(lower, LANES - 1, 1)
                work[at, pl.ds(0, 36, stride=6), :] = lower + pltpu.roll(upper, 1, 1)
                out_ref[pl.ds((x * 5 + q) * NODES * ey + y, NODES, stride=ey), :] = work[at]


def call(kernel, out_shape, scratch=(), smem=0, flops=0, operands=()):
    n = len(operands)
    in_specs = [
        pl.BlockSpec(memory_space=pltpu.SMEM if at < smem else pltpu.VMEM) for at in range(n)
    ]
    outs = jax.tree.map(lambda s: pl.BlockSpec(memory_space=pltpu.VMEM), out_shape)
    moved = sum(x.size * 4 for x in operands)
    return pl.pallas_call(
        kernel,
        out_shape=out_shape,
        in_specs=in_specs,
        out_specs=outs,
        scratch_shapes=list(scratch),
        cost_estimate=pl.CostEstimate(flops=flops, bytes_accessed=moved, transcendentals=0),
        compiler_params=pltpu.CompilerParams(vmem_limit_bytes=48 << 20),
    )(*operands)


def shape(*dims, dtype=F32):
    return jax.ShapeDtypeStruct(dims, dtype)


def shards(rho, flow, hot, parent, count, basis, speed, breadth, heat):
    ex, ey, height = rho.shape[0], rho.shape[1], rho.shape[-1]
    elems = ex * ey * height
    groups, spans = lax.axis_size("gx"), lax.axis_size("gy")
    bins = parent.shape[0]
    half = bins // CHUNKS
    cap = bins // 4 // CHUNKS
    slots_t = basis.shape[-1]
    rows = -(-5 * NODES // 32) * 8
    me = lax.axis_index("gx").astype(I32).reshape(1)

    ids = lax.all_gather(parent, "gx")
    own = parent.reshape(1, bins)
    firsts = jnp.sum(
        (own // elems < jnp.arange(groups + 1, dtype=I32)[:, None]).astype(I32), axis=1
    )
    rho_v = rho.transpose(0, 2, 3, 4, 1, 5).reshape(-1, height)
    flow_v = flow.transpose(0, 2, 3, 4, 5, 1, 6).reshape(-1, height)
    hot_v = hot.transpose(0, 2, 3, 4, 1, 5).reshape(-1, height)
    basis_v = basis.transpose(1, 2, 0, 3).reshape(18, bins, slots_t)
    speed_v = speed.transpose(1, 0, 2)

    sent, wanted = [], []
    for c in range(CHUNKS):
        wire, req = call(
            functools.partial(gather_kernel, c, elems, ex, ey),
            (shape(groups, rows, 4 * cap), shape(groups * cap, LANES, dtype=I32)),
            [pltpu.VMEM((4 * rows, groups * cap), F32)],
            smem=1,
            flops=10_000_000,
            operands=(me, ids, rho_v, flow_v, hot_v),
        )
        sent.append(wire)
        wanted.append(req)
    exchange = functools.partial(lax.all_to_all, axis_name="gx", split_axis=0, concat_axis=0, tiled=True)
    states = [exchange(wire) for wire in sent]
    data, live = call(
        functools.partial(arrange_kernel, elems, groups),
        (shape(CHUNKS, 23, slots_t, half), shape(CHUNKS, 8, half, dtype=I32)),
        flops=10_000_000,
        operands=(own, count.reshape(1, bins), basis_v, speed_v, breadth, heat),
    )
    fluid = call(
        functools.partial(fluid_kernel, ex, ey),
        shape(5, NODES, elems),
        [
            pltpu.VMEM((5, NODES, elems), F32),
            pltpu.VMEM((3, NODES, elems), F32),
            pltpu.VMEM((NODES, elems), F32),
        ],
        flops=10_000_000,
        operands=(jnp.asarray(gll_operator()), rho_v, flow_v, hot_v),
    )
    given = []
    for c in range(CHUNKS):
        wire = call(
            functools.partial(particle_kernel, c),
            shape(groups, NODES, 4 * cap),
            [
                pltpu.VMEM((4 * rows, half), F32),
                pltpu.VMEM((4 * NODES, half), F32),
                pltpu.VMEM((4, slots_t, half), F32),
            ],
            smem=1,
            flops=20_000_000,
            operands=(firsts, states[c], data[c], live[c]),
        )
        given.append(exchange(wire))
    part = call(
        load_kernel, shape(5, NODES, elems), flops=5_000_000, operands=(given[0], wanted[0], fluid)
    )
    wide = ey * height
    part, xlo, xhi, ylo, yhi, corner = call(
        functools.partial(join_kernel, ex, ey),
        (
            shape(5, NODES, elems),
            shape(5, 36, wide),
            shape(5, 36, wide),
            shape(5, 36, ex * height),
            shape(5, 36, ex * height),
            shape(4, 5, 8, height),
        ),
        flops=5_000_000,
        operands=(given[1], wanted[1], part),
    )
    up_x = [(i, i + 1) for i in range(groups - 1)]
    down_x = [(i + 1, i) for i in range(groups - 1)]
    up_y = [(i, (i + 1) % spans) for i in range(spans)]
    down_y = [((i + 1) % spans, i) for i in range(spans)]

    def diagonal(xs, ys):
        return [(a * spans + c, b * spans + d) for a, b in xs for c, d in ys]

    both = ("gx", "gy")
    halos = (
        lax.ppermute(xhi, "gx", up_x),
        lax.ppermute(xlo, "gx", down_x),
        lax.ppermute(yhi, "gy", up_y),
        lax.ppermute(ylo, "gy", down_y),
        lax.ppermute(corner[3], both, diagonal(up_x, up_y)),
        lax.ppermute(corner[2], both, diagonal(up_x, down_y)),
        lax.ppermute(corner[1], both, diagonal(down_x, up_y)),
        lax.ppermute(corner[0], both, diagonal(down_x, down_y)),
    )
    out = call(
        functools.partial(finish_kernel, ex, ey),
        shape(ex * 5 * NODES * ey, height),
        [pltpu.VMEM((ex * ey, NODES, height), F32)],
        flops=5_000_000,
        operands=(part,) + halos,
    )
    out = out.reshape(ex, 5, 6, 6, 6, ey, height)
    return out.transpose(0, 5, 1, 2, 3, 4, 6)


def solution(mesh):
    placed = (
        P("gx", "gy", None, None, None, None),
        P("gx", "gy", None, None, None, None, None),
        P("gx", "gy", None, None, None, None),
        P(("gx", "gy")),
        P(("gx", "gy")),
        P(("gx", "gy"), None, None, None),
        P(("gx", "gy"), None, None),
        P(("gx", "gy"), None),
        P(("gx", "gy"), None),
    )
    return jax.shard_map(
        shards,
        mesh=mesh,
        in_specs=placed,
        out_specs=P("gx", "gy", None, None, None, None, None),
        check_vma=False,
    )
```

time: 360 us -> 177 us (0.49)
  matrix products: 108 us -> 0 us
  local copies, waits for them, and re-layouts: 97.2 us -> 14.9 us
  Pallas kernels: 0 us -> 52.6 us
  waiting for transfers between devices: 82.2 us -> 43.6 us
  other arithmetic: 29.4 us -> 0.12 us
  starting transfers between devices: 26.9 us -> 45.6 us
  blocking collectives: 0 us -> 16.2 us
  loops' own time: 8.39 us -> 0 us
    dot_general x11 -> x0, matrix products: 108 us -> none  [the longest x4 55.2 us: cell_feedback(): jnp.einsum('bqs,bns->bqn', coupling, basis_table, precision=lax.Precision...]
    pallas_call x0 -> x9, Pallas kernels: none -> 52.6 us  [call(): pl.pallas_call(kernel, out_shape=out_shape, in_specs=in_specs, out_specs=...]
    scatter x6 -> x0, local copies, waits for them, and re-layouts: 43.3 us -> none  [the longest x2 35.3 us: assemble(): knot_readings = knot_readings.at[:, :, :, 5].set(upper_face + next_lower)...]
    all_to_all x3 -> x4, waiting for transfers between devices: 67.4 us -> 28.4 us  [the longest x2 18.6 us: shards(): states = [exchange(wire) for wire in sent]]
    all_gather x0 -> x1, blocking collectives: none -> 16.2 us  [shards(): ids = lax.all_gather(parent, 'gx')]
    all_to_all x3 -> x4, starting transfers between devices: 17.9 us -> 28.3 us  [the longest x2 15.2 us: shards(): states = [exchange(wire) for wire in sent]]
    reshape x10 -> x0, local copies, waits for them, and re-layouts: 9.19 us -> none  [the longest x2 5.14 us: shards(): state_rows = jnp.moveaxis(node_state, -1, 2).reshape(elem_total, 5 * 216)]
    another operation x1 -> x0, loops' own time: 8.39 us -> none  [source_term_blocks(): lax.map(lambda group_rows: cell_feedback(group_rows[0], group_rows[1], gr...]
  transfers between devices with their start and end apart: 7 -> 12, of which waited for: 6 -> 8; matrix products, arithmetic and copies ran while one was open for 8% -> 0% of each run, Pallas kernels for 0% -> 26%
where the time goes in v1:
time: 177 us; the launch traced here: 173 us
  Pallas kernels  52.6 us (30%)
  starting transfers between devices  45.6 us (26%)
  waiting for transfers between devices  43.6 us (25%)
  blocking collectives  16.2 us (9%)
  local copies, waits for them, and re-layouts  14.9 us (8%)
    pallas_call x9, Pallas kernels, call(): pl.pallas_call(kernel, out_shape=out_shape, in_specs=in_specs, out_specs=...  52.6 us
    all_to_all x2, waiting for transfers between devices, shards(): states = [exchange(wire) for wire in sent]  18.6 us
    all_gather x1, blocking collectives, shards(): ids = lax.all_gather(parent, 'gx')  16.2 us
    all_to_all x2, starting transfers between devices, shards(): states = [exchange(wire) for wire in sent]  15.2 us
    unnamed x51, local copies, waits for them, and re-layouts  14.6 us
    all_to_all x2, starting transfers between devices, shards(): given.append(exchange(wire))  13.1 us
    all_to_all x2, waiting for transfers between devices, shards(): given.append(exchange(wire))  9.78 us
    ppermute x1, waiting for transfers between devices, shards(): lax.ppermute(corner[3], both, diagonal(up_x, up_y))  4.72 us
  transfers between devices with their start and end apart: 12, of which 8 were waited for; matrix products, arithmetic and copies ran while one was open for 0% of the time, Pallas kernels for 26%

profile of v1, /device:TPU:24, one launch (start us, length us, event | category | flops | bytes accessed | tf_op | source)
XLA Modules:
  0.0 173.4 jit_solution(14296494885967782355)
XLA Ops:
  0.0 16.2 %all-gather.1 = s32[8,1,256]{2,1,0:T(1,128)S(1)} all-gather(s32[1,1,256]{2,1,0:T(1,128)} %bitcast.52), channel_id=2, replica_groups=mesh['gx'=8,'gy'=4] {'gx'}, dimensions={0}, use_global_device_ids=true | all-gather | bytes 9216 | tf_op jit(solution)/shard_map/all_gather | solution.py:445
  19.6 2.2 %shard_map.103 = (f32[8,272,128]{2,1,0:T(8,128)S(1)}, s32[256,128]{1,0:T(8,128)S(1)}) custom-call(s32[1]{0:T(128)} %bitcast.me_ref, s32[8,256]{1,0:T(8,128)S(1)} %bitcast.50, f32[864,128]{1,0:T(8,128)S(1)} %bitcast.42, f32[2592,128]{1,0:T(8,128)S(1)} %bitcast.39, f32[864,128]{1,0:T(8,128)S(1)} %bitcast.45), custom_call_target="tpu_custom_call" | custom-call | flops 10000000 | bytes 2220036 | tf_op jit(solution)/shard_map/pallas_call | solution.py:419
  23.5 8.7 %all-to-all-start.2 = ((f32[8,272,128]{2,1,0:T(8,128)}), f32[8,272,128]{2,1,0:T(8,128)S(1)}, u32[]{:S(2)}, u32[]{:S(2)}) async-start(f32[8,272,128]{2,1,0:T(8,128)} %copy-done.14), calls=%async_computation.2 | async-start | bytes 2228224 | tf_op jit(solution)/shard_map/all_to_all | solution.py:469
  33.2 2.2 %shard_map.100 = (f32[8,272,128]{2,1,0:T(8,128)S(1)}, s32[256,128]{1,0:T(8,128)S(1)}) custom-call(s32[1]{0:T(128)} %bitcast.me_ref, s32[8,256]{1,0:T(8,128)S(1)} %bitcast.51, f32[864,128]{1,0:T(8,128)S(1)} %bitcast.43, f32[2592,128]{1,0:T(8,128)S(1)} %bitcast.40, f32[864,128]{1,0:T(8,128)S(1)} %bitcast.46), custom_call_target="tpu_custom_call" | custom-call | flops 10000000 | bytes 2220036 | tf_op jit(solution)/shard_map/pallas_call | solution.py:419
  37.1 16.6 %all-to-all-done.2.recv_ref = f32[8,272,128]{2,1,0:T(8,128)S(1)} async-done(((f32[8,272,128]{2,1,0:T(8,128)}), f32[8,272,128]{2,1,0:T(8,128)S(1)}, u32[]{:S(2)}, u32[]{:S(2)}) %all-to-all-start.2) | async-done | bytes 1114144 | tf_op jit(solution)/shard_map/all_to_all | solution.py:469
  53.7 6.5 %all-to-all-start = ((f32[8,272,128]{2,1,0:T(8,128)}), f32[8,272,128]{2,1,0:T(8,128)}, u32[]{:S(2)}, u32[]{:S(2)}) async-start(f32[8,272,128]{2,1,0:T(8,128)} %copy-done.13), calls=%async_computation | async-start | bytes 2228224 | tf_op jit(solution)/shard_map/all_to_all | solution.py:469
  61.9 2.8 %shard_map.101 = (f32[2,23,128,128]{3,2,1,0:T(8,128)S(1)}, s32[2,8,128]{2,1,0:T(8,128)S(1)}) custom-call(s32[1,256]{1,0:T(1,128)S(1)} %bitcast.53, s32[1,256]{1,0:T(1,128)S(1)} %bitcast.54, f32[18,256,128]{2,1,0:T(8,128)S(1)} %bitcast.48, f32[3,256,128]{2,1,0:T(8,128)S(1)} %bitcast.49, f32[256,128]{1,0:T(8,128)S(1)} %copy-done.17, f32[256,128]{1,0:T(8,128)S(1)} %copy-done.18), custom_call_target="tpu_custom_call" | custom-call | flops 10000000 | bytes 3016704 | tf_op jit(solution)/shard_map/pallas_call | solution.py:419
  66.1 14.0 %shard_map.104 = f32[8,216,128]{2,1,0:T(8,128)S(1)} custom-call(s32[9]{0:T(128)S(1)} %convert_reduce_fusion.firsts_ref, f32[8,272,128]{2,1,0:T(8,128)S(1)} %copy-done.4, f32[23,128,128]{2,1,0:T(8,128)S(1)} %get-tuple-element.29.data_ref, s32[8,128]{1,0:T(8,128)S(1)} %get-tuple-element.35.live_ref), custom_call_target="tpu_custom_call" | custom-call | flops 20000000 | bytes 2625572 | tf_op jit(solution)/shard_map/pallas_call | solution.py:419
  83.1 6.7 %all-to-all-start.3 = ((f32[8,216,128]{2,1,0:T(8,128)}), f32[8,216,128]{2,1,0:T(8,128)}, u32[]{:S(2)}, u32[]{:S(2)}) async-start(f32[8,216,128]{2,1,0:T(8,128)} %copy-done.11), calls=%async_computation.3 | async-start | bytes 1769472 | tf_op jit(solution)/shard_map/all_to_all | solution.py:501
  89.8 14.8 %shard_map.102 = f32[8,216,128]{2,1,0:T(8,128)S(1)} custom-call(s32[9]{0:T(128)S(1)} %convert_reduce_fusion.firsts_ref, f32[8,272,128]{2,1,0:T(8,128)} %all-to-all-done.recv_ref, f32[23,128,128]{2,1,0:T(8,128)S(1)} %get-tuple-element.30.data_ref, s32[8,128]{1,0:T(8,128)S(1)} %get-tuple-element.36.live_ref), custom_call_target="tpu_custom_call" | custom-call | flops 20000000 | bytes 2625572 | tf_op jit(solution)/shard_map/pallas_call | solution.py:419
  105.5 3.1 %all-to-all-done.3.recv_ref = f32[8,216,128]{2,1,0:T(8,128)} async-done(((f32[8,216,128]{2,1,0:T(8,128)}), f32[8,216,128]{2,1,0:T(8,128)}, u32[]{:S(2)}, u32[]{:S(2)}) %all-to-all-start.3) | async-done | bytes 884768 | tf_op jit(solution)/shard_map/all_to_all | solution.py:501
  108.6 6.4 %all-to-all-start.1 = ((f32[8,216,128]{2,1,0:T(8,128)}), f32[8,216,128]{2,1,0:T(8,128)S(1)}, u32[]{:S(2)}, u32[]{:S(2)}) async-start(f32[8,216,128]{2,1,0:T(8,128)} %copy-done.10), calls=%async_computation.1 | async-start | bytes 1769472 | tf_op jit(solution)/shard_map/all_to_all | solution.py:501
  116.1 7.3 %shard_map.105.fluid_ref = f32[5,216,512]{2,1,0:T(8,128)S(1)} custom-call(f32[216,648]{1,0:T(8,128)S(1)} %copy-done.15, f32[864,128]{1,0:T(8,128)S(1)} %bitcast.44, f32[2592,128]{1,0:T(8,128)S(1)} %bitcast.41, f32[864,128]{1,0:T(8,128)S(1)} %bitcast.47), custom_call_target="tpu_custom_call" | custom-call | flops 10000000 | bytes 2771712 | tf_op jit(solution)/shard_map/pallas_call | solution.py:419
  123.4 3.3 %shard_map.106.part_ref = f32[5,216,512]{2,1,0:T(8,128)S(1)} custom-call(f32[8,216,128]{2,1,0:T(8,128)} %all-to-all-done.3.recv_ref, s32[256,128]{1,0:T(8,128)S(1)} %copy-done.22, f32[5,216,512]{2,1,0:T(8,128)S(1)} %shard_map.105.fluid_ref), custom_call_target="tpu_custom_call" | custom-call | flops 5000000 | bytes 3227648 | tf_op jit(solution)/shard_map/pallas_call | solution.py:419
  128.1 6.6 %all-to-all-done.1.recv_ref = f32[8,216,128]{2,1,0:T(8,128)S(1)} async-done(((f32[8,216,128]{2,1,0:T(8,128)}), f32[8,216,128]{2,1,0:T(8,128)S(1)}, u32[]{:S(2)}, u32[]{:S(2)}) %all-to-all-start.1) | async-done | bytes 884768 | tf_op jit(solution)/shard_map/all_to_all | solution.py:501
  134.7 3.9 %shard_map.107 = (f32[5,216,512]{2,1,0:T(8,128)S(1)}, f32[5,36,256]{2,1,0:T(8,128)S(1)}, f32[5,36,256]{2,1,0:T(8,128)S(1)}, f32[5,36,256]{2,1,0:T(8,128)S(1)}, f...) custom-call(f32[8,216,128]{2,1,0:T(8,128)S(1)} %all-to-all-done.1.recv_ref, s32[256,128]{1,0:T(8,128)S(1)} %copy-done.20, ...), custom_call_target="tpu_custom_call" | custom-call | flops 5000000 | bytes 3227648 | tf_op jit(solution)/shard_map/pallas_call | solution.py:419
  138.6 3.6 %collective-permute-start = (f32[5,36,256]{2,1,0:T(8,128)S(1)}, f32[5,36,256]{2,1,0:T(8,128)S(1)}, u32[]{:S(2)}, u32[]{:S(2)}) collective-permute-start(f32[5,36,256]{2,1,0:T(8,128)S(1)} %get-tuple-element.24), channel_id=1, source_target_pairs={{0,4},{4,8},{8,12},{12,16},{16,20},{20,24},{24,28},{1,5},{5,9},{9,... | collective-permute-start | bytes 552968 | tf_op jit(solution)/shard_map/ppermute | solution.py:529
  142.2 3.1 %collective-permute-start.1 = (f32[5,36,256]{2,1,0:T(8,128)S(1)}, f32[5,36,256]{2,1,0:T(8,128)S(1)}, u32[]{:S(2)}, u32[]{:S(2)}) collective-permute-start(f32[5,36,256]{2,1,0:T(8,128)S(1)} %get-tuple-element.25), channel_id=1, source_target_pairs={{4,0},{8,4},{12,8},{16,12},{20,16},{24,20},{28,24},{5,1},{9,5},{13... | collective-permute-start | bytes 552968 | tf_op jit(solution)/shard_map/ppermute | solution.py:530
  147.1 2.3 %collective-permute-start.4 = (f32[5,8,128]{2,1,0:T(8,128)S(1)}, f32[5,8,128]{2,1,0:T(8,128)S(1)}, u32[]{:S(2)}, u32[]{:S(2)}) collective-permute-start(f32[5,8,128]{2,1,0:T(8,128)S(1)} %get-tuple-element.34), channel_id=1, source_target_pairs={{0,5},{1,6},{2,7},{3,4},{4,9},{5,10},{6,11},{7,8},{8,13},{9,14},{1... | collective-permute-start | bytes 61448 | tf_op jit(solution)/shard_map/ppermute | solution.py:533
  149.4 4.7 %collective-permute-done.4.c00_ref = f32[5,8,128]{2,1,0:T(8,128)S(1)} collective-permute-done((f32[5,8,128]{2,1,0:T(8,128)S(1)}, f32[5,8,128]{2,1,0:T(8,128)S(1)}, u32[]{:S(2)}, u32[]{:S(2)}) %collective-permute-start.4) | collective-permute-done | bytes 20512 | tf_op jit(solution)/shard_map/ppermute | solution.py:533
  156.0 4.1 %collective-permute-done.5.c01_ref = f32[5,8,128]{2,1,0:T(8,128)S(1)} collective-permute-done((f32[5,8,128]{2,1,0:T(8,128)S(1)}, f32[5,8,128]{2,1,0:T(8,128)S(1)}, u32[]{:S(2)}, u32[]{:S(2)}) %collective-permute-start.5) | collective-permute-done | bytes 20512 | tf_op jit(solution)/shard_map/ppermute | solution.py:534
  162.0 4.1 %collective-permute-done.6.c10_ref = f32[5,8,128]{2,1,0:T(8,128)S(1)} collective-permute-done((f32[5,8,128]{2,1,0:T(8,128)S(1)}, f32[5,8,128]{2,1,0:T(8,128)S(1)}, u32[]{:S(2)}, u32[]{:S(2)}) %collective-permute-start.6) | collective-permute-done | bytes 20512 | tf_op jit(solution)/shard_map/ppermute | solution.py:535
  166.1 2.8 %collective-permute-start.7 = (f32[5,8,128]{2,1,0:T(8,128)S(1)}, f32[5,8,128]{2,1,0:T(8,128)S(1)}, u32[]{:S(2)}, u32[]{:S(2)}) collective-permute-start(f32[5,8,128]{2,1,0:T(8,128)S(1)} %get-tuple-element.31), channel_id=1, source_target_pairs={{5,0},{6,1},{7,2},{4,3},{9,4},{10,5},{11,6},{8,7},{13,8},{14,9},{1... | collective-permute-start | bytes 61448 | tf_op jit(solution)/shard_map/ppermute | solution.py:536
  168.9 2.3 %collective-permute-done.7.c11_ref = f32[5,8,128]{2,1,0:T(8,128)S(1)} collective-permute-done((f32[5,8,128]{2,1,0:T(8,128)S(1)}, f32[5,8,128]{2,1,0:T(8,128)S(1)}, u32[]{:S(2)}, u32[]{:S(2)}) %collective-permute-start.7) | collective-permute-done | bytes 20512 | tf_op jit(solution)/shard_map/ppermute | solution.py:536
  (66 shorter events, 24.8 us)
Async XLA Ops:
  23.5 8.7 %copy-start.1 = (f32[2,2,3,6,6,6,128]{6,1,5,4,3,2,0:T(2,128)S(1)}, f32[2,2,3,6,6,6,128]{6,1,5,4,3,2,0:T(2,128)}, u32[]{:S(2)}) copy-start(f32[2,2,3,6,6,6,128]{6,1,5,4,3,2,0:T(2,128)} %param.11) | copy-start | bytes 3981316
  23.5 8.7 %copy-start.6 = (f32[2,2,6,6,6,128]{5,1,4,3,2,0:T(2,128)S(1)}, f32[2,2,6,6,6,128]{5,1,4,3,2,0:T(2,128)}, u32[]{:S(2)}) copy-start(f32[2,2,6,6,6,128]{5,1,4,3,2,0:T(2,128)} %param.10) | copy-start | bytes 1327108
  23.5 30.2 %all-to-all-start.2 = ((f32[8,272,128]{2,1,0:T(8,128)}), f32[8,272,128]{2,1,0:T(8,128)S(1)}, u32[]{:S(2)}, u32[]{:S(2)}) async-start(f32[8,272,128]{2,1,0:T(8,128)} %copy-done.14), calls=%async_computation.2 | async-start | bytes 2228224 | tf_op jit(solution)/shard_map/all_to_all | solution.py:469
  37.1 23.1 %copy-start.16 = (f32[256,3,128]{2,0,1:T(8,128)S(1)}, f32[256,3,128]{2,0,1:T(8,128)}, u32[]{:S(2)}) copy-start(f32[256,3,128]{2,0,1:T(8,128)} %param.16) | copy-start | bytes 1179652
  37.1 23.1 %copy-start.17 = (f32[256,128]{1,0:T(8,128)S(1)}, f32[256,128]{1,0:T(8,128)}, u32[]{:S(2)}) copy-start(f32[256,128]{1,0:T(8,128)} %breadth_ref.1) | copy-start | bytes 393220
  37.1 23.1 %copy-start.18 = (f32[256,128]{1,0:T(8,128)S(1)}, f32[256,128]{1,0:T(8,128)}, u32[]{:S(2)}) copy-start(f32[256,128]{1,0:T(8,128)} %hot_ref.1) | copy-start | bytes 393220
  37.1 23.1 %copy-start.23 = (s32[256]{0:T(256)S(1)}, s32[256]{0:T(256)}, u32[]{:S(2)}) copy-start(s32[256]{0:T(256)} %param.13) | copy-start | bytes 3076
  37.1 23.1 %copy-start.24 = (s32[256]{0:T(256)S(1)}, s32[256]{0:T(256)}, u32[]{:S(2)}) copy-start(s32[256]{0:T(256)} %param.14) | copy-start | bytes 3076
  53.7 11.0 %copy-start.3 = (f32[8,272,128]{2,1,0:T(8,128)}, f32[8,272,128]{2,1,0:T(8,128)S(1)}, u32[]{:S(2)}) copy-start(f32[8,272,128]{2,1,0:T(8,128)S(1)} %all-to-all-done.2.recv_ref) | copy-start | bytes 3342340
  53.7 29.4 %all-to-all-start = ((f32[8,272,128]{2,1,0:T(8,128)}), f32[8,272,128]{2,1,0:T(8,128)}, u32[]{:S(2)}, u32[]{:S(2)}) async-start(f32[8,272,128]{2,1,0:T(8,128)} %copy-done.13), calls=%async_computation | async-start | bytes 2228224 | tf_op jit(solution)/shard_map/all_to_all | solution.py:469
  60.2 1.7 copy-start.12
  83.1 25.5 %all-to-all-start.3 = ((f32[8,216,128]{2,1,0:T(8,128)}), f32[8,216,128]{2,1,0:T(8,128)}, u32[]{:S(2)}, u32[]{:S(2)}) async-start(f32[8,216,128]{2,1,0:T(8,128)} %copy-done.11), calls=%async_computation.3 | async-start | bytes 1769472 | tf_op jit(solution)/shard_map/all_to_all | solution.py:501
  105.5 9.5 %copy-start.9 = (f32[2,2,6,6,6,128]{5,1,4,3,2,0:T(2,128)S(1)}, f32[2,2,6,6,6,128]{5,1,4,3,2,0:T(2,128)}, u32[]{:S(2)}) copy-start(f32[2,2,6,6,6,128]{5,1,4,3,2,0:T(2,128)} %param.12) | copy-start | bytes 1327108
  108.6 26.1 %all-to-all-start.1 = ((f32[8,216,128]{2,1,0:T(8,128)}), f32[8,216,128]{2,1,0:T(8,128)S(1)}, u32[]{:S(2)}, u32[]{:S(2)}) async-start(f32[8,216,128]{2,1,0:T(8,128)} %copy-done.10), calls=%async_computation.1 | async-start | bytes 1769472 | tf_op jit(solution)/shard_map/all_to_all | solution.py:501
  116.1 7.3 %copy-start.22 = (s32[256,128]{1,0:T(8,128)S(1)}, s32[256,128]{1,0:T(8,128)}, u32[]{:S(2)}) copy-start(s32[256,128]{1,0:T(8,128)} %copy-done.21) | copy-start | bytes 393220
  123.4 11.3 %copy-start.20 = (s32[256,128]{1,0:T(8,128)S(1)}, s32[256,128]{1,0:T(8,128)}, u32[]{:S(2)}) copy-start(s32[256,128]{1,0:T(8,128)} %copy-done.19) | copy-start | bytes 393220
  138.6 32.6 %collective-permute-start = (f32[5,36,256]{2,1,0:T(8,128)S(1)}, f32[5,36,256]{2,1,0:T(8,128)S(1)}, u32[]{:S(2)}, u32[]{:S(2)}) collective-permute-start(f32[5,36,256]{2,1,0:T(8,128)S(1)} %get-tuple-element.24), channel_id=1, source_target_pairs={{0,4},{4,8},{8,12},{12,16},{16,20},{20,24},{24,28},{1,5},{5,9},{9,... | collective-permute-start | bytes 552968 | tf_op jit(solution)/shard_map/ppermute | solution.py:529
  142.2 29.0 %collective-permute-start.1 = (f32[5,36,256]{2,1,0:T(8,128)S(1)}, f32[5,36,256]{2,1,0:T(8,128)S(1)}, u32[]{:S(2)}, u32[]{:S(2)}) collective-permute-start(f32[5,36,256]{2,1,0:T(8,128)S(1)} %get-tuple-element.25), channel_id=1, source_target_pairs={{4,0},{8,4},{12,8},{16,12},{20,16},{24,20},{28,24},{5,1},{9,5},{13... | collective-permute-start | bytes 552968 | tf_op jit(solution)/shard_map/ppermute | solution.py:530
  145.3 25.9 %collective-permute-start.2 = (f32[5,36,256]{2,1,0:T(8,128)S(1)}, f32[5,36,256]{2,1,0:T(8,128)S(1)}, u32[]{:S(2)}, u32[]{:S(2)}) collective-permute-start(f32[5,36,256]{2,1,0:T(8,128)S(1)} %get-tuple-element.26), channel_id=1, source_target_pairs={{0,1},{1,2},{2,3},{3,0},{4,5},{5,6},{6,7},{7,4},{8,9},{9,10},{10,1... | collective-permute-start | bytes 552968 | tf_op jit(solution)/shard_map/ppermute | solution.py:531
  145.4 25.8 %collective-permute-start.3 = (f32[5,36,256]{2,1,0:T(8,128)S(1)}, f32[5,36,256]{2,1,0:T(8,128)S(1)}, u32[]{:S(2)}, u32[]{:S(2)}) collective-permute-start(f32[5,36,256]{2,1,0:T(8,128)S(1)} %get-tuple-element.27), channel_id=1, source_target_pairs={{1,0},{2,1},{3,2},{0,3},{5,4},{6,5},{7,6},{4,7},{9,8},{10,9},{11,1... | collective-permute-start | bytes 552968 | tf_op jit(solution)/shard_map/ppermute | solution.py:532
  147.1 7.0 %collective-permute-start.4 = (f32[5,8,128]{2,1,0:T(8,128)S(1)}, f32[5,8,128]{2,1,0:T(8,128)S(1)}, u32[]{:S(2)}, u32[]{:S(2)}) collective-permute-start(f32[5,8,128]{2,1,0:T(8,128)S(1)} %get-tuple-element.34), channel_id=1, source_target_pairs={{0,5},{1,6},{2,7},{3,4},{4,9},{5,10},{6,11},{7,8},{8,13},{9,14},{1... | collective-permute-start | bytes 61448 | tf_op jit(solution)/shard_map/ppermute | solution.py:533
  154.1 6.0 %collective-permute-start.5 = (f32[5,8,128]{2,1,0:T(8,128)S(1)}, f32[5,8,128]{2,1,0:T(8,128)S(1)}, u32[]{:S(2)}, u32[]{:S(2)}) collective-permute-start(f32[5,8,128]{2,1,0:T(8,128)S(1)} %get-tuple-element.33), channel_id=1, source_target_pairs={{1,4},{2,5},{3,6},{0,7},{5,8},{6,9},{7,10},{4,11},{9,12},{10,13},{... | collective-permute-start | bytes 61448 | tf_op jit(solution)/shard_map/ppermute | solution.py:534
  160.1 6.0 %collective-permute-start.6 = (f32[5,8,128]{2,1,0:T(8,128)S(1)}, f32[5,8,128]{2,1,0:T(8,128)S(1)}, u32[]{:S(2)}, u32[]{:S(2)}) collective-permute-start(f32[5,8,128]{2,1,0:T(8,128)S(1)} %get-tuple-element.32), channel_id=1, source_target_pairs={{4,1},{5,2},{6,3},{7,0},{8,5},{9,6},{10,7},{11,4},{12,9},{13,10},{... | collective-permute-start | bytes 61448 | tf_op jit(solution)/shard_map/ppermute | solution.py:535
  166.1 5.1 %collective-permute-start.7 = (f32[5,8,128]{2,1,0:T(8,128)S(1)}, f32[5,8,128]{2,1,0:T(8,128)S(1)}, u32[]{:S(2)}, u32[]{:S(2)}) collective-permute-start(f32[5,8,128]{2,1,0:T(8,128)S(1)} %get-tuple-element.31), channel_id=1, source_target_pairs={{5,0},{6,1},{7,2},{4,3},{9,4},{10,5},{11,6},{8,7},{13,8},{14,9},{1... | collective-permute-start | bytes 61448 | tf_op jit(solution)/shard_map/ppermute | solution.py:536
  (13 other events, 13.2 us)

commit v2 on v1

--- a/solution.py
+++ b/solution.py
@@ -8,6 +8,7 @@
 from jax.experimental import pallas as pl
 from jax.experimental.pallas import tpu as pltpu
 from jax.sharding import PartitionSpec as P
+
 
 SPECIFIC_CP = 2.5
 MU_GAS = 0.2
@@ -64,13 +65,6 @@
     return hi, mid, (rest - mid.astype(F32)).astype(BF16)
 
 
-def pick(x, weights):
-    hi, lo = halves(x)
-    return jnp.dot(hi, weights, preferred_element_type=F32) + jnp.dot(
-        lo, weights, preferred_element_type=F32
-    )
-
-
 def iota(shape, dim):
     return lax.broadcasted_iota(I32, shape, dim)
 
@@ -108,12 +102,32 @@
     return out
 
 
-def gather_kernel(c, elems, ex, ey, me_ref, ids_ref, rho_ref, vel_ref, hot_ref, out_ref, req_ref, work):
-    groups, bins = ids_ref.shape
+def split_kernel(ex, ey, rho_ref, vel_ref, hot_ref, hi_ref, lo_ref):
+    state = state_columns(rho_ref, vel_ref, hot_ref, ex, ey)
+    for q in range(5):
+        hi, lo = halves(jnp.concatenate(state[q], axis=1))
+        hi_ref[q * NODES : (q + 1) * NODES, :] = hi
+        lo_ref[q * NODES : (q + 1) * NODES, :] = lo
+
+
+def block_device(c, s, me, groups, sign):
+    return s if c == 0 else lax.rem(me + sign * s + groups, groups)
+
+
+def block_view(refs, s):
+    return refs[0].at[s] if len(refs) == 1 else refs[s]
+
+
+def gather_kernel(c, elems, groups, me_ref, ids_ref, hi_ref, lo_ref, after_ref, *refs):
+    out_refs, (req_ref, work) = refs[:-2], refs[-2:]
+    bins = ids_ref.shape[1]
     me = me_ref[0]
-    cap = out_ref.shape[2] // 4
+    rows = out_refs[0].shape[-2]
+    cap = LANES // 4
     slots = groups * cap
-    ids = ids_ref[...]
+    ids = jnp.concatenate(
+        [ids_ref[pl.ds(block_device(c, s, me, groups, 1), 1), :] for s in range(groups)], axis=0
+    )
     places, slab, firsts = sorted_places(ids, elems, groups)
     elem = jnp.bitwise_and(ids, elems - 1)
     sub = iota((LANES, bins), 0)
@@ -144,10 +158,9 @@
     ).astype(I32)
     req_ref[...] = jnp.broadcast_to(wanted_col, (slots, LANES))
     onehot = (jnp.broadcast_to(wanted, (elems, slots)) == iota((elems, slots), 0)).astype(F32).astype(BF16)
-    state = state_columns(rho_ref, vel_ref, hot_ref, ex, ey)
-    for q in range(5):
-        work[q * NODES : (q + 1) * NODES, :] = pick(jnp.concatenate(state[q], axis=1), onehot)
-    rows = out_ref.shape[1]
+    work[0 : 5 * NODES, :] = jnp.dot(
+        hi_ref[...], onehot, preferred_element_type=F32
+    ) + jnp.dot(lo_ref[...], onehot, preferred_element_type=F32)
     pad = 4 * rows - 5 * NODES
     work[5 * NODES : 4 * rows, :] = jnp.zeros((pad, slots), F32)
     lane_group = iota((rows, LANES), 1) // cap
@@ -161,10 +174,10 @@
                 turn = ((g - at) % 4) * cap
                 moved = block[g] if turn == 0 else pltpu.roll(block[g], turn, 1)
                 total = moved if total is None else jnp.where(lane_group == g, moved, total)
-            out_ref[tile * 4 + at] = total
-
-
-def arrange_kernel(elems, groups, ids_ref, count_ref, basis_ref, vel_ref, breadth_ref, hot_ref, out_ref, live_ref):
+            block_view(out_refs, tile * 4 + at)[...] = total
+
+
+def arrange_kernel(elems, groups, ids_ref, count_ref, basis_ref, vel_ref, breadth_ref, hot_ref, *out_refs):
     bins = ids_ref.shape[1]
     half = bins // CHUNKS
     places, _, _ = sorted_places(ids_ref[...], elems, groups)
@@ -174,7 +187,7 @@
     count = jnp.broadcast_to(count_ref[...], (8, bins)).astype(F32).astype(BF16)
     live = lax.dot_general(count, move, NT, preferred_element_type=F32)
     for c in range(CHUNKS):
-        live_ref[c] = live[:, c * half : (c + 1) * half].astype(I32)
+        out_refs[CHUNKS + c][...] = live[:, c * half : (c + 1) * half].astype(I32)
     sources = [basis_ref.at[m] for m in range(18)] + [vel_ref.at[m] for m in range(3)]
     sources += [breadth_ref, hot_ref]
     for m, source in enumerate(sources):
@@ -185,7 +198,7 @@
             + jnp.dot(move, lo, preferred_element_type=F32)
         )
         for c in range(CHUNKS):
-            out_ref[c, m] = moved[c * half : (c + 1) * half].T
+            out_refs[c][m] = moved[c * half : (c + 1) * half].T
 
 
 def fluid_kernel(ex, ey, op_ref, rho_ref, vel_ref, hot_ref, out_ref, lead, flow, push):
@@ -217,19 +230,27 @@
     lax.fori_loop(0, 5, component, 0)
 
 
-def particle_kernel(c, firsts_ref, recv_ref, data_ref, live_ref, out_ref, host, work, force):
-    groups, rows, _ = recv_ref.shape
+def particle_kernel(c, groups, me_ref, firsts_ref, data_ref, live_ref, after_ref, *refs):
+    host, work, force = refs[-3:]
+    blocks = 1 if c == 0 else groups
+    recv_refs, out_refs = refs[:blocks], refs[blocks:-3]
+    rows = recv_refs[0].shape[-2]
     cap = LANES // 4
+    me = me_ref[0]
     slots_t = data_ref.shape[1]
     width = data_ref.shape[2]
-    begins = [jnp.right_shift(firsts_ref[g] - c + 1, 1) for g in range(groups + 1)]
+    begins, ends = [], []
+    for s in range(groups):
+        g = block_device(c, s, me, groups, -1)
+        begins.append(jnp.right_shift(firsts_ref[g] - c + 1, 1))
+        ends.append(jnp.right_shift(firsts_ref[g + 1] - c + 1, 1))
 
     row = iota((LANES, width), 0)
     col = iota((LANES, width), 1)
     slot = jnp.bitwise_and(row, cap - 1)
     lane_group = jnp.right_shift(row, cap.bit_length() - 1)
-    bases = [(col - slot == begins[d]) & (col < begins[d + 1]) for d in range(groups)]
-    got_hi, got_lo = halves(jnp.concatenate([recv_ref[d] for d in range(groups)], axis=1))
+    bases = [(col - slot == begins[d]) & (col < ends[d]) for d in range(groups)]
+    got_hi, got_lo = halves(jnp.concatenate([block_view(recv_refs, s)[...] for s in range(groups)], axis=1))
     for g in range(4):
         weights = jnp.concatenate(
             [(bases[d] & (lane_group == g)).astype(F32).astype(BF16) for d in range(groups)], axis=0
@@ -306,19 +327,18 @@
         jnp.concatenate([work[r * NODES : (r + 1) * NODES, :] for r in range(4)], axis=1)
     )
     for d in range(groups):
-        base = (row - slot == begins[d]) & (row < begins[d + 1])
+        base = (row - slot == begins[d]) & (row < ends[d])
         weights = jnp.concatenate(
             [(base & (lane_group == r)).astype(F32).astype(BF16) for r in range(4)], axis=0
         )
-        out_ref[d] = jnp.dot(give_hi, weights, preferred_element_type=F32) + jnp.dot(
+        block_view(out_refs, d)[...] = jnp.dot(give_hi, weights, preferred_element_type=F32) + jnp.dot(
             give_lo, weights, preferred_element_type=F32
         )
 
 
-def collect(recv_ref, req_ref, elems):
-    groups, rows, _ = recv_ref.shape
+def collect(recv_refs, groups, req_ref, elems):
     cap = LANES // 4
-    got = jnp.concatenate([recv_ref[d] for d in range(groups)], axis=1)
+    got = jnp.concatenate([block_view(recv_refs, s)[...] for s in range(groups)], axis=1)
     lane_group = jnp.right_shift(jnp.bitwise_and(iota(got.shape, 1), LANES - 1), cap.bit_length() - 1)
     weights = []
     for d in range(groups):
@@ -339,15 +359,16 @@
     return out
 
 
-def load_kernel(recv_ref, req_ref, fluid_ref, out_ref):
-    loads = collect(recv_ref, req_ref, fluid_ref.shape[2])
+def load_kernel(groups, recv_ref, req_ref, fluid_ref, out_ref):
+    loads = collect([recv_ref], groups, req_ref, fluid_ref.shape[2])
     out_ref[0] = fluid_ref[0]
     for r in range(4):
         out_ref[1 + r] = fluid_ref[1 + r] - loads[r]
 
 
-def join_kernel(ex, ey, recv_ref, req_ref, part_ref, out_ref, xlo_ref, xhi_ref, ylo_ref, yhi_ref, corner_ref):
-    loads = collect(recv_ref, req_ref, part_ref.shape[2])
+def join_kernel(groups, ex, ey, *refs):
+    req_ref, part_ref, out_ref, xlo_ref, xhi_ref, ylo_ref, yhi_ref = refs[groups:]
+    loads = collect(refs[:groups], groups, req_ref, part_ref.shape[2])
     out_ref[0] = part_ref[0]
     for r in range(4):
         out_ref[1 + r] = part_ref[1 + r] - loads[r]
@@ -376,14 +397,16 @@
             for i in range(6):
                 ylo_ref[q, 6 * i : 6 * i + 6, dst] = out_ref[q, 36 * i : 36 * i + 6, lo]
                 yhi_ref[q, 6 * i : 6 * i + 6, dst] = out_ref[q, 36 * i + 30 : 36 * i + 36, hi]
-        for at, (x, y) in enumerate(((0, 0), (0, 1), (1, 0), (1, 1))):
-            start = 180 * x + 30 * y
-            lanes = x * last + y * (wide - LANES)
-            corner_ref[at, q] = jnp.zeros((8, LANES), F32)
-            corner_ref[at, q, 0:6, :] = out_ref[q, start : start + 6, lanes : lanes + LANES]
-
-
-def finish_kernel(ex, ey, part_ref, xl_ref, xr_ref, yl_ref, yr_ref, c00_ref, c01_ref, c10_ref, c11_ref, out_ref, work):
+
+
+def edge_kernel(ey, xl_ref, xr_ref, lo_ref, hi_ref):
+    last = (ey - 1) * LANES
+    for x, ref in enumerate((xl_ref, xr_ref)):
+        lo_ref[x] = ref[:, 0:6, 0:LANES]
+        hi_ref[x] = ref[:, 30:36, last : last + LANES]
+
+
+def finish_kernel(ex, ey, part_ref, xl_ref, xr_ref, yl_ref, yr_ref, el_ref, er_ref, out_ref, work):
     for q in range(5):
         for at in range(ex * ey):
             work[at] = part_ref[q, :, at * LANES : (at + 1) * LANES]
@@ -396,9 +419,10 @@
             for i in range(6):
                 work[x * ey, 36 * i : 36 * i + 6, :] += yl_ref[q, 6 * i : 6 * i + 6, lanes]
                 work[x * ey + ey - 1, 36 * i + 30 : 36 * i + 36, :] += yr_ref[q, 6 * i : 6 * i + 6, lanes]
-        for ref, x, y in ((c00_ref, 0, 0), (c01_ref, 0, 1), (c10_ref, 1, 0), (c11_ref, 1, 1)):
-            start = 180 * x + 30 * y
-            work[x * (ex - 1) * ey + y * (ey - 1), start : start + 6, :] += ref[q, 0:6, :]
+        for x in range(2):
+            start, at = 180 * x, x * (ex - 1) * ey
+            work[at, start : start + 6, :] += el_ref[x, q]
+            work[at + ey - 1, start + 30 : start + 36, :] += er_ref[x, q]
         for x in range(ex):
             for y in range(ey):
                 at = x * ey + y
@@ -409,21 +433,20 @@
                 out_ref[pl.ds((x * 5 + q) * NODES * ey + y, NODES, stride=ey), :] = work[at]
 
 
-def call(kernel, out_shape, scratch=(), smem=0, flops=0, operands=()):
-    n = len(operands)
-    in_specs = [
-        pl.BlockSpec(memory_space=pltpu.SMEM if at < smem else pltpu.VMEM) for at in range(n)
-    ]
-    outs = jax.tree.map(lambda s: pl.BlockSpec(memory_space=pltpu.VMEM), out_shape)
-    moved = sum(x.size * 4 for x in operands)
+def call(kernel, out_shape, scratch=(), smem=0, late=0, flops=0, operands=()):
+    spaces = [pltpu.SMEM if at < smem else pltpu.VMEM for at in range(len(operands))]
+    if late:
+        spaces[late] = pl.ANY
     return pl.pallas_call(
         kernel,
         out_shape=out_shape,
-        in_specs=in_specs,
-        out_specs=outs,
+        in_specs=[pl.BlockSpec(memory_space=space) for space in spaces],
+        out_specs=jax.tree.map(lambda s: pl.BlockSpec(memory_space=pltpu.VMEM), out_shape),
         scratch_shapes=list(scratch),
-        cost_estimate=pl.CostEstimate(flops=flops, bytes_accessed=moved, transcendentals=0),
-        compiler_params=pltpu.CompilerParams(vmem_limit_bytes=48 << 20),
+        cost_estimate=pl.CostEstimate(
+            flops=flops, bytes_accessed=sum(x.size * 4 for x in operands), transcendentals=0
+        ),
+        compiler_params=pltpu.CompilerParams(vmem_limit_bytes=16 << 20),
     )(*operands)
 
 
@@ -431,7 +454,7 @@
     return jax.ShapeDtypeStruct(dims, dtype)
 
 
-def shards(rho, flow, hot, parent, count, basis, speed, breadth, heat):
+def step(rho, flow, hot, parent, count, basis, speed, breadth, heat):
     ex, ey, height = rho.shape[0], rho.shape[1], rho.shape[-1]
     elems = ex * ey * height
     groups, spans = lax.axis_size("gx"), lax.axis_size("gy")
@@ -442,37 +465,57 @@
     rows = -(-5 * NODES // 32) * 8
     me = lax.axis_index("gx").astype(I32).reshape(1)
 
-    ids = lax.all_gather(parent, "gx")
     own = parent.reshape(1, bins)
     firsts = jnp.sum(
         (own // elems < jnp.arange(groups + 1, dtype=I32)[:, None]).astype(I32), axis=1
     )
+
+    def turn(x, by):
+        return lax.ppermute(x, "gx", [(i, (i + by) % groups) for i in range(groups)])
+
+    def spread(blocks, sign):
+        return [blocks[0]] + [turn(blocks[s], sign * s) for s in range(1, groups)]
+
+    def exchange(x):
+        return lax.all_to_all(x, "gx", 0, 0, tiled=True)
+
+    ids = exchange(jnp.broadcast_to(own, (groups, bins)))
     rho_v = rho.transpose(0, 2, 3, 4, 1, 5).reshape(-1, height)
     flow_v = flow.transpose(0, 2, 3, 4, 5, 1, 6).reshape(-1, height)
     hot_v = hot.transpose(0, 2, 3, 4, 1, 5).reshape(-1, height)
     basis_v = basis.transpose(1, 2, 0, 3).reshape(18, bins, slots_t)
     speed_v = speed.transpose(1, 0, 2)
 
-    sent, wanted = [], []
+    def turn_y(x, by):
+        return lax.ppermute(x, "gy", [(i, (i + by) % spans) for i in range(spans)])
+
+    high, low = call(
+        functools.partial(split_kernel, ex, ey),
+        [shape(5 * NODES, elems, dtype=BF16)] * 2,
+        flops=10_000_000,
+        operands=(rho_v, flow_v, hot_v),
+    )
+    arranged = call(
+        functools.partial(arrange_kernel, elems, groups),
+        [shape(23, slots_t, half)] * CHUNKS + [shape(8, half, dtype=I32)] * CHUNKS,
+        flops=10_000_000,
+        operands=(own, count.reshape(1, bins), basis_v, speed_v, breadth, heat),
+    )
+    data, live = arranged[:CHUNKS], arranged[CHUNKS:]
+    states, wanted = [], []
     for c in range(CHUNKS):
-        wire, req = call(
-            functools.partial(gather_kernel, c, elems, ex, ey),
-            (shape(groups, rows, 4 * cap), shape(groups * cap, LANES, dtype=I32)),
+        blocks = [shape(groups, rows, 4 * cap)] if c == 0 else [shape(rows, 4 * cap)] * groups
+        *wire, req = call(
+            functools.partial(gather_kernel, c, elems, groups),
+            blocks + [shape(groups * cap, LANES, dtype=I32)],
             [pltpu.VMEM((4 * rows, groups * cap), F32)],
             smem=1,
+            late=4,
             flops=10_000_000,
-            operands=(me, ids, rho_v, flow_v, hot_v),
-        )
-        sent.append(wire)
+            operands=(me, ids, high, low, ids if c == 0 else wanted[0]),
+        )
+        states.append([exchange(wire[0])] if c == 0 else spread(wire, 1))
         wanted.append(req)
-    exchange = functools.partial(lax.all_to_all, axis_name="gx", split_axis=0, concat_axis=0, tiled=True)
-    states = [exchange(wire) for wire in sent]
-    data, live = call(
-        functools.partial(arrange_kernel, elems, groups),
-        (shape(CHUNKS, 23, slots_t, half), shape(CHUNKS, 8, half, dtype=I32)),
-        flops=10_000_000,
-        operands=(own, count.reshape(1, bins), basis_v, speed_v, breadth, heat),
-    )
     fluid = call(
         functools.partial(fluid_kernel, ex, ey),
         shape(5, NODES, elems),
@@ -485,62 +528,54 @@
         operands=(jnp.asarray(gll_operator()), rho_v, flow_v, hot_v),
     )
     given = []
+    after = fluid
     for c in range(CHUNKS):
         wire = call(
-            functools.partial(particle_kernel, c),
-            shape(groups, NODES, 4 * cap),
+            functools.partial(particle_kernel, c, groups),
+            [shape(groups, NODES, 4 * cap)] if c == 0 else [shape(NODES, 4 * cap)] * groups,
             [
                 pltpu.VMEM((4 * rows, half), F32),
                 pltpu.VMEM((4 * NODES, half), F32),
                 pltpu.VMEM((4, slots_t, half), F32),
             ],
-            smem=1,
+            smem=2,
+            late=4,
             flops=20_000_000,
-            operands=(firsts, states[c], data[c], live[c]),
-        )
-        given.append(exchange(wire))
+            operands=(me, firsts, data[c], live[c], after, *states[c]),
+        )
+        after = wire[0]
+        given.append([exchange(wire[0])] if c == 0 else spread(wire, -1))
     part = call(
-        load_kernel, shape(5, NODES, elems), flops=5_000_000, operands=(given[0], wanted[0], fluid)
-    )
-    wide = ey * height
-    part, xlo, xhi, ylo, yhi, corner = call(
-        functools.partial(join_kernel, ex, ey),
+        functools.partial(load_kernel, groups),
+        shape(5, NODES, elems),
+        flops=5_000_000,
+        operands=(given[0][0], wanted[0], fluid),
+    )
+    part, xlo, xhi, ylo, yhi = call(
+        functools.partial(join_kernel, groups, ex, ey),
         (
             shape(5, NODES, elems),
-            shape(5, 36, wide),
-            shape(5, 36, wide),
+            shape(5, 36, ey * height),
+            shape(5, 36, ey * height),
             shape(5, 36, ex * height),
             shape(5, 36, ex * height),
-            shape(4, 5, 8, height),
         ),
         flops=5_000_000,
-        operands=(given[1], wanted[1], part),
-    )
-    up_x = [(i, i + 1) for i in range(groups - 1)]
-    down_x = [(i + 1, i) for i in range(groups - 1)]
-    up_y = [(i, (i + 1) % spans) for i in range(spans)]
-    down_y = [((i + 1) % spans, i) for i in range(spans)]
-
-    def diagonal(xs, ys):
-        return [(a * spans + c, b * spans + d) for a, b in xs for c, d in ys]
-
-    both = ("gx", "gy")
-    halos = (
-        lax.ppermute(xhi, "gx", up_x),
-        lax.ppermute(xlo, "gx", down_x),
-        lax.ppermute(yhi, "gy", up_y),
-        lax.ppermute(ylo, "gy", down_y),
-        lax.ppermute(corner[3], both, diagonal(up_x, up_y)),
-        lax.ppermute(corner[2], both, diagonal(up_x, down_y)),
-        lax.ppermute(corner[1], both, diagonal(down_x, up_y)),
-        lax.ppermute(corner[0], both, diagonal(down_x, down_y)),
-    )
+        operands=(*given[1], wanted[1], part),
+    )
+    xl = lax.ppermute(xhi, "gx", [(i, i + 1) for i in range(groups - 1)])
+    xr = lax.ppermute(xlo, "gx", [(i + 1, i) for i in range(groups - 1)])
+    yl, yr = turn_y(yhi, 1), turn_y(ylo, -1)
+    elo, ehi = call(
+        functools.partial(edge_kernel, ey), [shape(2, 5, 6, height)] * 2, flops=1_000_000, operands=(xl, xr)
+    )
+    el, er = turn_y(ehi, 1), turn_y(elo, -1)
     out = call(
         functools.partial(finish_kernel, ex, ey),
         shape(ex * 5 * NODES * ey, height),
         [pltpu.VMEM((ex * ey, NODES, height), F32)],
         flops=5_000_000,
-        operands=(part,) + halos,
+        operands=(part, xl, xr, yl, yr, el, er),
     )
     out = out.reshape(ex, 5, 6, 6, 6, ey, height)
     return out.transpose(0, 5, 1, 2, 3, 4, 6)
@@ -559,7 +594,7 @@
         P(("gx", "gy"), None),
     )
     return jax.shard_map(
-        shards,
+        step,
         mesh=mesh,
         in_specs=placed,
         out_specs=P("gx", "gy", None, None, None, None, None),

time: 177 us -> 178 us (level)
  the two profiles are of different devices: /device:TPU:24 before, /device:TPU:17 now
where the time goes in v2:
time: 178 us; the launch traced here: 177 us
  waiting for transfers between devices  60.7 us (34%)
  Pallas kernels  53.1 us (30%)
  starting transfers between devices  47.8 us (27%)
  local copies, waits for them, and re-layouts  15 us (8%)
    pallas_call x11, Pallas kernels, call(): pl.pallas_call(kernel, out_shape=out_shape, in_specs=[pl.BlockSpec(memory...  53.1 us
    ppermute x14, waiting for transfers between devices, turn(): lax.ppermute(x, 'gx', [(i, (i + by) % groups) for i in range(groups)])  43.7 us
    all_to_all x3, starting transfers between devices, exchange(): return lax.all_to_all(x, 'gx', 0, 0, tiled=True)  19.1 us
    ppermute x14, starting transfers between devices, turn(): lax.ppermute(x, 'gx', [(i, (i + by) % groups) for i in range(groups)])  18.6 us
    unnamed x53, local copies, waits for them, and re-layouts  13.7 us
    all_to_all x3, waiting for transfers between devices, exchange(): return lax.all_to_all(x, 'gx', 0, 0, tiled=True)  7.84 us
    ppermute x1, starting transfers between devices, step(): xr = lax.ppermute(xlo, 'gx', [(i + 1, i) for i in range(groups - 1)])  4.26 us
    ppermute x4, starting transfers between devices, turn_y(): return lax.ppermute(x, 'gy', [(i, (i + by) % spans) for i in range(spans)])  3.93 us
  transfers between devices with their start and end apart: 23, of which 12 were waited for; matrix products, arithmetic and copies ran while one was open for 0% of the time, Pallas kernels for 17%

profile of v2, /device:TPU:17, one launch (start us, length us, event | category | flops | bytes accessed | tf_op | source)
XLA Modules:
  0.0 177.0 jit_solution(1118077341791938787)
XLA Ops:
  1.3 5.6 %all-to-all-start = ((s32[8,1,256]{2,1,0:T(1,128)}), s32[8,1,256]{2,1,0:T(1,128)S(1)}, u32[]{:S(2)}, u32[]{:S(2)}) async-start(s32[8,1,256]{2,1,0:T(1,128)} %broadcast_in_dim.2), calls=%async_computation | async-start | bytes 16384 | tf_op jit(solution)/shard_map/all_to_all | solution.py:480
  10.6 2.3 %shard_map.103 = (f32[8,272,128]{2,1,0:T(8,128)S(1)}, s32[256,128]{1,0:T(8,128)S(1)}) custom-call(s32[1]{0:T(128)} %bitcast.me_ref, s32[8,256]{1,0:T(8,128)S(1)} %bitcast.30, bf16[1080,512]{1,0:T(8,128)(2,1)S(1)} %get-tuple-element.41.hi_ref, bf16[1080,512]{1,0:T(8,128)(2,1)S(1)} %get-tuple-element.42.lo_ref, s32[8,256]{1,0:T(8,128)S(1)} %bitcast.31), custom_call_target="tpu_custom_call" | custom-call | flops 10000000 | bytes 4440068 | tf_op jit(solution)/shard_map/pallas_call | solution.py:440
  14.6 5.9 %all-to-all-start.1 = ((f32[8,272,128]{2,1,0:T(8,128)}), f32[8,272,128]{2,1,0:T(8,128)}, u32[]{:S(2)}, u32[]{:S(2)}) async-start(f32[8,272,128]{2,1,0:T(8,128)} %copy-done.15), calls=%async_computation.1 | async-start | bytes 2228224 | tf_op jit(solution)/shard_map/all_to_all | solution.py:480
  23.6 7.3 %shard_map.101.after_ref.fluid_ref = f32[5,216,512]{2,1,0:T(8,128)S(1)} custom-call(f32[216,648]{1,0:T(8,128)S(1)} %copy-done.16, f32[864,128]{1,0:T(8,128)S(1)} %bitcast.26, f32[2592,128]{1,0:T(8,128)S(1)} %bitcast.23, f32[864,128]{1,0:T(8,128)S(1)} %bitcast.28), custom_call_target="tpu_custom_call" | custom-call | flops 10000000 | bytes 2771712 | tf_op jit(solution)/shard_map/pallas_call | solution.py:440
  30.9 2.8 %shard_map.100 = (f32[23,128,128]{2,1,0:T(8,128)S(1)}, f32[23,128,128]{2,1,0:T(8,128)S(1)}, s32[8,128]{1,0:T(8,128)S(1)}, s32[8,128]{1,0:T(8,128)S(1)}) custom-call(s32[1,256]{1,0:T(1,128)S(1)} %bitcast.33, s32[1,256]{1,0:T(1,128)S(1)} %bitcast.34, f32[18,256,128]{2,1,0:T(8,128)S(1)} %bitcast.24, f32[3,256,128]{2,1,0:T(8,128)S(1)} %bitcast.29, ...), custom_call_target="tpu_custom_call" | custom-call | flops 10000000 | bytes 3016704 | tf_op jit(solution)/shard_map/pallas_call | solution.py:440
  36.1 7.8 %all-to-all-done.1.refs_0_ = f32[8,272,128]{2,1,0:T(8,128)} async-done(((f32[8,272,128]{2,1,0:T(8,128)}), f32[8,272,128]{2,1,0:T(8,128)}, u32[]{:S(2)}, u32[]{:S(2)}) %all-to-all-start.1) | async-done | bytes 1114144 | tf_op jit(solution)/shard_map/all_to_all | solution.py:480
  45.4 15.7 %shard_map.104.after_ref = f32[8,216,128]{2,1,0:T(8,128)} custom-call(s32[1]{0:T(128)} %bitcast.me_ref, s32[9]{0:T(128)S(1)} %convert_reduce_fusion.firsts_ref, f32[23,128,128]{2,1,0:T(8,128)S(1)} %copy-done.14, s32[8,128]{1,0:T(8,128)S(1)} %get-tuple-element.40.live_ref, f32[5,216,512]{2,1,0:T(8,128)S(1)} %shard_map.101.after_ref.fluid_ref, ...), custom_call_target="tpu_custom_call" | custom-call | flops 20000000 | bytes 4837416 | tf_op jit(solution)/shard_map/pallas_call | solution.py:440
  61.1 7.7 %all-to-all-start.2 = ((f32[8,216,128]{2,1,0:T(8,128)}), f32[8,216,128]{2,1,0:T(8,128)}, u32[]{:S(2)}, u32[]{:S(2)}) async-start(f32[8,216,128]{2,1,0:T(8,128)} %shard_map.104.after_ref), calls=%async_computation.2 | async-start | bytes 1769472 | tf_op jit(solution)/shard_map/all_to_all | solution.py:480
  70.0 2.3 %shard_map.105 = (f32[272,128]{1,0:T(8,128)S(1)}, f32[272,128]{1,0:T(8,128)S(1)}, f32[272,128]{1,0:T(8,128)S(1)}, f32[272,128]{1,0:T(8,128)S(1)}, f32[272,128]{1...) custom-call(s32[1]{0:T(128)} %bitcast.me_ref, ...), custom_call_target="tpu_custom_call" | custom-call | flops 10000000 | bytes 4562948 | tf_op jit(solution)/shard_map/pallas_call | solution.py:440
  78.8 26.4 %collective-permute-done.refs_1_ = f32[272,128]{1,0:T(8,128)S(1)} collective-permute-done((f32[272,128]{1,0:T(8,128)S(1)}, f32[272,128]{1,0:T(8,128)S(1)}, u32[]{:S(2)}, u32[]{:S(2)}) %collective-permute-start) | collective-permute-done | bytes 139296 | tf_op jit(solution)/shard_map/ppermute | solution.py:474
  105.2 2.2 %collective-permute-start.6 = (f32[272,128]{1,0:T(8,128)S(1)}, f32[272,128]{1,0:T(8,128)S(1)}, u32[]{:S(2)}, u32[]{:S(2)}) collective-permute-start(f32[272,128]{1,0:T(8,128)S(1)} %get-tuple-element.52), channel_id=1, source_target_pairs={{0,28},{4,0},{8,4},{12,8},{16,12},{20,16},{24,20},{28,24},{1,29},{... | collective-permute-start | bytes 417800 | tf_op jit(solution)/shard_map/ppermute | solution.py:474
  107.4 2.4 %collective-permute-done.5.refs_6_ = f32[272,128]{1,0:T(8,128)S(1)} collective-permute-done((f32[272,128]{1,0:T(8,128)S(1)}, f32[272,128]{1,0:T(8,128)S(1)}, u32[]{:S(2)}, u32[]{:S(2)}) %collective-permute-start.5) | collective-permute-done | bytes 139296 | tf_op jit(solution)/shard_map/ppermute | solution.py:474
  111.9 14.7 %shard_map.106 = (f32[216,128]{1,0:T(8,128)S(1)}, f32[216,128]{1,0:T(8,128)S(1)}, f32[216,128]{1,0:T(8,128)S(1)}, f32[216,128]{1,0:T(8,128)}, f32[216,128]{1,0:T...) custom-call(s32[1]{0:T(128)} %bitcast.me_ref, s32[9]{0:T(128)S(1)} %convert_reduce_fusion.firsts_ref, ...), custom_call_target="tpu_custom_call" | custom-call | flops 20000000 | bytes 3510312 | tf_op jit(solution)/shard_map/pallas_call | solution.py:440
  126.6 2.8 %collective-permute-start.7 = (f32[216,128]{1,0:T(8,128)S(1)}, f32[216,128]{1,0:T(8,128)S(1)}, u32[]{:S(2)}, u32[]{:S(2)}) collective-permute-start(f32[216,128]{1,0:T(8,128)S(1)} %get-tuple-element.54), channel_id=1, source_target_pairs={{0,28},{4,0},{8,4},{12,8},{16,12},{20,16},{24,20},{28,24},{1,29},{... | collective-permute-start | bytes 331784 | tf_op jit(solution)/shard_map/ppermute | solution.py:474
  129.5 3.6 %collective-permute-start.9 = (f32[216,128]{1,0:T(8,128)}, f32[216,128]{1,0:T(8,128)S(1)}, u32[]{:S(2)}, u32[]{:S(2)}) collective-permute-start(f32[216,128]{1,0:T(8,128)} %get-tuple-element.56), channel_id=1, source_target_pairs={{0,20},{4,24},{8,28},{12,0},{16,4},{20,8},{24,12},{28,16},{1,21},{... | collective-permute-start | bytes 331784 | tf_op jit(solution)/shard_map/ppermute | solution.py:474
  134.5 2.4 %collective-permute-start.12 = (f32[216,128]{1,0:T(8,128)}, f32[216,128]{1,0:T(8,128)S(1)}, u32[]{:S(2)}, u32[]{:S(2)}) collective-permute-start(f32[216,128]{1,0:T(8,128)} %get-tuple-element.59), channel_id=1, source_target_pairs={{0,8},{4,12},{8,16},{12,20},{16,24},{20,28},{24,0},{28,4},{1,9},{5... | collective-permute-start | bytes 331784 | tf_op jit(solution)/shard_map/ppermute | solution.py:474
  137.1 3.3 %shard_map.107.refs_9_ = f32[5,216,512]{2,1,0:T(8,128)S(1)} custom-call(f32[8,216,128]{2,1,0:T(8,128)} %all-to-all-done.2.recv_ref, s32[256,128]{1,0:T(8,128)S(1)} %copy-done.18, f32[5,216,512]{2,1,0:T(8,128)S(1)} %shard_map.101.after_ref.fluid_ref), custom_call_target="tpu_custom_call" | custom-call | flops 5000000 | bytes 3227648 | tf_op jit(solution)/shard_map/pallas_call | solution.py:440
  140.4 4.9 %collective-permute-done.9.refs_3_ = f32[216,128]{1,0:T(8,128)S(1)} collective-permute-done((f32[216,128]{1,0:T(8,128)}, f32[216,128]{1,0:T(8,128)S(1)}, u32[]{:S(2)}, u32[]{:S(2)}) %collective-permute-start.9) | collective-permute-done | bytes 110624 | tf_op jit(solution)/shard_map/ppermute | solution.py:474
  145.4 2.4 %collective-permute-done.10.refs_4_ = f32[216,128]{1,0:T(8,128)S(1)} collective-permute-done((f32[216,128]{1,0:T(8,128)}, f32[216,128]{1,0:T(8,128)S(1)}, u32[]{:S(2)}, u32[]{:S(2)}) %collective-permute-start.10) | collective-permute-done | bytes 110624 | tf_op jit(solution)/shard_map/ppermute | solution.py:474
  147.7 4.6 %collective-permute-done.12.refs_6_ = f32[216,128]{1,0:T(8,128)S(1)} collective-permute-done((f32[216,128]{1,0:T(8,128)}, f32[216,128]{1,0:T(8,128)S(1)}, u32[]{:S(2)}, u32[]{:S(2)}) %collective-permute-start.12) | collective-permute-done | bytes 110624 | tf_op jit(solution)/shard_map/ppermute | solution.py:474
  153.3 2.2 %shard_map.108 = (f32[5,216,512]{2,1,0:T(8,128)S(1)}, f32[5,36,256]{2,1,0:T(8,128)S(1)}, f32[5,36,256]{2,1,0:T(8,128)S(1)}, f32[5,36,256]{2,1,0:T(8,128)S(1)}, f32[5,36,256]{2,1,0:T(8,128)S(1)}) custom-call(f32[216,128]{1,0:T(8,128)S(1)} %get-tuple-element.53.refs_0_, f32[216,128]{1,0:T(8,128)S(1)} %collective-permute-done.7.refs_1_, ...), custom_call_target="tpu_custom_call" | custom-call | flops 5000000 | bytes 3227648 | tf_op jit(solution)/shard_map/pallas_call | solution.py:440
  157.5 4.3 %collective-permute-start.15 = (f32[5,36,256]{2,1,0:T(8,128)S(1)}, f32[5,36,256]{2,1,0:T(8,128)S(1)}, u32[]{:S(2)}, u32[]{:S(2)}) collective-permute-start(f32[5,36,256]{2,1,0:T(8,128)S(1)} %get-tuple-element.64), channel_id=1, source_target_pairs={{4,0},{8,4},{12,8},{16,12},{20,16},{24,20},{28,24},{5,1},{9,5},{13... | collective-permute-start | bytes 552968 | tf_op jit(solution)/shard_map/ppermute | solution.py:567
  166.0 3.7 %collective-permute-done.15.xr_ref = f32[5,36,256]{2,1,0:T(8,128)S(1)} collective-permute-done((f32[5,36,256]{2,1,0:T(8,128)S(1)}, f32[5,36,256]{2,1,0:T(8,128)S(1)}, u32[]{:S(2)}, u32[]{:S(2)}) %collective-permute-start.15) | collective-permute-done | bytes 184352 | tf_op jit(solution)/shard_map/ppermute | solution.py:567
  172.5 2.3 %collective-permute-done.19.er_ref = f32[2,5,6,128]{3,2,1,0:T(8,128)S(1)} collective-permute-done((f32[2,5,6,128]{3,2,1,0:T(8,128)S(1)}, f32[2,5,6,128]{3,2,1,0:T(8,128)S(1)}, u32[]{:S(2)}, u32[]{:S(2)}) %collective-permute-start.19) | collective-permute-done | bytes 30752 | tf_op jit(solution)/shard_map/ppermute | solution.py:490
  (89 shorter events, 37.3 us)
Async XLA Ops:
  1.3 9.3 %all-to-all-start = ((s32[8,1,256]{2,1,0:T(1,128)}), s32[8,1,256]{2,1,0:T(1,128)S(1)}, u32[]{:S(2)}, u32[]{:S(2)}) async-start(s32[8,1,256]{2,1,0:T(1,128)} %broadcast_in_dim.2), calls=%async_computation | async-start | bytes 16384 | tf_op jit(solution)/shard_map/all_to_all | solution.py:480
  14.6 29.4 %all-to-all-start.1 = ((f32[8,272,128]{2,1,0:T(8,128)}), f32[8,272,128]{2,1,0:T(8,128)}, u32[]{:S(2)}, u32[]{:S(2)}) async-start(f32[8,272,128]{2,1,0:T(8,128)} %copy-done.15), calls=%async_computation.1 | async-start | bytes 2228224 | tf_op jit(solution)/shard_map/all_to_all | solution.py:480
  61.1 76.1 %all-to-all-start.2 = ((f32[8,216,128]{2,1,0:T(8,128)}), f32[8,216,128]{2,1,0:T(8,128)}, u32[]{:S(2)}, u32[]{:S(2)}) async-start(f32[8,216,128]{2,1,0:T(8,128)} %shard_map.104.after_ref), calls=%async_computation.2 | async-start | bytes 1769472 | tf_op jit(solution)/shard_map/all_to_all | solution.py:480
  70.0 41.9 %copy-start.12 = (f32[23,128,128]{2,1,0:T(8,128)S(1)}, f32[23,128,128]{2,1,0:T(8,128)}, u32[]{:S(2)}) copy-start(f32[23,128,128]{2,1,0:T(8,128)} %copy-done.11) | copy-start | bytes 4521988
  72.9 32.3 %collective-permute-start = (f32[272,128]{1,0:T(8,128)S(1)}, f32[272,128]{1,0:T(8,128)S(1)}, u32[]{:S(2)}, u32[]{:S(2)}) collective-permute-start(f32[272,128]{1,0:T(8,128)S(1)} %get-tuple-element.46), channel_id=1, source_target_pairs={{0,4},{4,8},{8,12},{12,16},{16,20},{20,24},{24,28},{28,0},{1,5},{5... | collective-permute-start | bytes 417800 | tf_op jit(solution)/shard_map/ppermute | solution.py:474
  74.1 31.1 %collective-permute-start.1 = (f32[272,128]{1,0:T(8,128)S(1)}, f32[272,128]{1,0:T(8,128)S(1)}, u32[]{:S(2)}, u32[]{:S(2)}) collective-permute-start(f32[272,128]{1,0:T(8,128)S(1)} %get-tuple-element.47), channel_id=1, source_target_pairs={{0,8},{4,12},{8,16},{12,20},{16,24},{20,28},{24,0},{28,4},{1,9},{5... | collective-permute-start | bytes 417800 | tf_op jit(solution)/shard_map/ppermute | solution.py:474
  75.3 32.2 %collective-permute-start.2 = (f32[272,128]{1,0:T(8,128)S(1)}, f32[272,128]{1,0:T(8,128)S(1)}, u32[]{:S(2)}, u32[]{:S(2)}) collective-permute-start(f32[272,128]{1,0:T(8,128)S(1)} %get-tuple-element.48), channel_id=1, source_target_pairs={{0,12},{4,16},{8,20},{12,24},{16,28},{20,0},{24,4},{28,8},{1,13},{... | collective-permute-start | bytes 417800 | tf_op jit(solution)/shard_map/ppermute | solution.py:474
  76.4 31.0 %collective-permute-start.3 = (f32[272,128]{1,0:T(8,128)S(1)}, f32[272,128]{1,0:T(8,128)S(1)}, u32[]{:S(2)}, u32[]{:S(2)}) collective-permute-start(f32[272,128]{1,0:T(8,128)S(1)} %get-tuple-element.49), channel_id=1, source_target_pairs={{0,16},{4,20},{8,24},{12,28},{16,0},{20,4},{24,8},{28,12},{1,17},{... | collective-permute-start | bytes 417800 | tf_op jit(solution)/shard_map/ppermute | solution.py:474
  77.6 29.8 %collective-permute-start.4 = (f32[272,128]{1,0:T(8,128)S(1)}, f32[272,128]{1,0:T(8,128)S(1)}, u32[]{:S(2)}, u32[]{:S(2)}) collective-permute-start(f32[272,128]{1,0:T(8,128)S(1)} %get-tuple-element.50), channel_id=1, source_target_pairs={{0,20},{4,24},{8,28},{12,0},{16,4},{20,8},{24,12},{28,16},{1,21},{... | collective-permute-start | bytes 417800 | tf_op jit(solution)/shard_map/ppermute | solution.py:474
  105.2 4.6 %collective-permute-start.5 = (f32[272,128]{1,0:T(8,128)S(1)}, f32[272,128]{1,0:T(8,128)S(1)}, u32[]{:S(2)}, u32[]{:S(2)}) collective-permute-start(f32[272,128]{1,0:T(8,128)S(1)} %get-tuple-element.51), channel_id=1, source_target_pairs={{0,24},{4,28},{8,0},{12,4},{16,8},{20,12},{24,16},{28,20},{1,25},{... | collective-permute-start | bytes 417800 | tf_op jit(solution)/shard_map/ppermute | solution.py:474
  105.2 6.7 %collective-permute-start.6 = (f32[272,128]{1,0:T(8,128)S(1)}, f32[272,128]{1,0:T(8,128)S(1)}, u32[]{:S(2)}, u32[]{:S(2)}) collective-permute-start(f32[272,128]{1,0:T(8,128)S(1)} %get-tuple-element.52), channel_id=1, source_target_pairs={{0,28},{4,0},{8,4},{12,8},{16,12},{20,16},{24,20},{28,24},{1,29},{... | collective-permute-start | bytes 417800 | tf_op jit(solution)/shard_map/ppermute | solution.py:474
  126.6 7.9 %collective-permute-start.7 = (f32[216,128]{1,0:T(8,128)S(1)}, f32[216,128]{1,0:T(8,128)S(1)}, u32[]{:S(2)}, u32[]{:S(2)}) collective-permute-start(f32[216,128]{1,0:T(8,128)S(1)} %get-tuple-element.54), channel_id=1, source_target_pairs={{0,28},{4,0},{8,4},{12,8},{16,12},{20,16},{24,20},{28,24},{1,29},{... | collective-permute-start | bytes 331784 | tf_op jit(solution)/shard_map/ppermute | solution.py:474
  129.5 7.4 %collective-permute-start.8 = (f32[216,128]{1,0:T(8,128)S(1)}, f32[216,128]{1,0:T(8,128)S(1)}, u32[]{:S(2)}, u32[]{:S(2)}) collective-permute-start(f32[216,128]{1,0:T(8,128)S(1)} %get-tuple-element.55), channel_id=1, source_target_pairs={{0,24},{4,28},{8,0},{12,4},{16,8},{20,12},{24,16},{28,20},{1,25},{... | collective-permute-start | bytes 331784 | tf_op jit(solution)/shard_map/ppermute | solution.py:474
  129.5 15.9 %collective-permute-start.9 = (f32[216,128]{1,0:T(8,128)}, f32[216,128]{1,0:T(8,128)S(1)}, u32[]{:S(2)}, u32[]{:S(2)}) collective-permute-start(f32[216,128]{1,0:T(8,128)} %get-tuple-element.56), channel_id=1, source_target_pairs={{0,20},{4,24},{8,28},{12,0},{16,4},{20,8},{24,12},{28,16},{1,21},{... | collective-permute-start | bytes 331784 | tf_op jit(solution)/shard_map/ppermute | solution.py:474
  133.1 14.6 %collective-permute-start.10 = (f32[216,128]{1,0:T(8,128)}, f32[216,128]{1,0:T(8,128)S(1)}, u32[]{:S(2)}, u32[]{:S(2)}) collective-permute-start(f32[216,128]{1,0:T(8,128)} %get-tuple-element.57), channel_id=1, source_target_pairs={{0,16},{4,20},{8,24},{12,28},{16,0},{20,4},{24,8},{28,12},{1,17},{... | collective-permute-start | bytes 331784 | tf_op jit(solution)/shard_map/ppermute | solution.py:474
  133.1 14.6 %collective-permute-start.11 = (f32[216,128]{1,0:T(8,128)}, f32[216,128]{1,0:T(8,128)S(1)}, u32[]{:S(2)}, u32[]{:S(2)}) collective-permute-start(f32[216,128]{1,0:T(8,128)} %get-tuple-element.58), channel_id=1, source_target_pairs={{0,12},{4,16},{8,20},{12,24},{16,28},{20,0},{24,4},{28,8},{1,13},{... | collective-permute-start | bytes 331784 | tf_op jit(solution)/shard_map/ppermute | solution.py:474
  134.5 17.8 %collective-permute-start.12 = (f32[216,128]{1,0:T(8,128)}, f32[216,128]{1,0:T(8,128)S(1)}, u32[]{:S(2)}, u32[]{:S(2)}) collective-permute-start(f32[216,128]{1,0:T(8,128)} %get-tuple-element.59), channel_id=1, source_target_pairs={{0,8},{4,12},{8,16},{12,20},{16,24},{20,28},{24,0},{28,4},{1,9},{5... | collective-permute-start | bytes 331784 | tf_op jit(solution)/shard_map/ppermute | solution.py:474
  136.9 16.4 %collective-permute-start.13 = (f32[216,128]{1,0:T(8,128)}, f32[216,128]{1,0:T(8,128)S(1)}, u32[]{:S(2)}, u32[]{:S(2)}) collective-permute-start(f32[216,128]{1,0:T(8,128)} %get-tuple-element.60), channel_id=1, source_target_pairs={{0,4},{4,8},{8,12},{12,16},{16,20},{20,24},{24,28},{28,0},{1,5},{5... | collective-permute-start | bytes 331784 | tf_op jit(solution)/shard_map/ppermute | solution.py:474
  155.5 10.5 %collective-permute-start.14 = (f32[5,36,256]{2,1,0:T(8,128)S(1)}, f32[5,36,256]{2,1,0:T(8,128)S(1)}, u32[]{:S(2)}, u32[]{:S(2)}) collective-permute-start(f32[5,36,256]{2,1,0:T(8,128)S(1)} %get-tuple-element.63), channel_id=1, source_target_pairs={{0,4},{4,8},{8,12},{12,16},{16,20},{20,24},{24,28},{1,5},{5,9},{9,... | collective-permute-start | bytes 552968 | tf_op jit(solution)/shard_map/ppermute | solution.py:566
  157.5 12.3 %collective-permute-start.15 = (f32[5,36,256]{2,1,0:T(8,128)S(1)}, f32[5,36,256]{2,1,0:T(8,128)S(1)}, u32[]{:S(2)}, u32[]{:S(2)}) collective-permute-start(f32[5,36,256]{2,1,0:T(8,128)S(1)} %get-tuple-element.64), channel_id=1, source_target_pairs={{4,0},{8,4},{12,8},{16,12},{20,16},{24,20},{28,24},{5,1},{9,5},{13... | collective-permute-start | bytes 552968 | tf_op jit(solution)/shard_map/ppermute | solution.py:567
  161.7 9.7 %collective-permute-start.16 = (f32[5,36,256]{2,1,0:T(8,128)S(1)}, f32[5,36,256]{2,1,0:T(8,128)S(1)}, u32[]{:S(2)}, u32[]{:S(2)}) collective-permute-start(f32[5,36,256]{2,1,0:T(8,128)S(1)} %get-tuple-element.65), channel_id=1, source_target_pairs={{0,1},{1,2},{2,3},{3,0},{4,5},{5,6},{6,7},{7,4},{8,9},{9,10},{10,1... | collective-permute-start | bytes 552968 | tf_op jit(solution)/shard_map/ppermute | solution.py:490
  164.0 7.5 %collective-permute-start.17 = (f32[5,36,256]{2,1,0:T(8,128)S(1)}, f32[5,36,256]{2,1,0:T(8,128)S(1)}, u32[]{:S(2)}, u32[]{:S(2)}) collective-permute-start(f32[5,36,256]{2,1,0:T(8,128)S(1)} %get-tuple-element.66), channel_id=1, source_target_pairs={{0,3},{1,0},{2,1},{3,2},{4,7},{5,4},{6,5},{7,6},{8,11},{9,8},{10,9... | collective-permute-start | bytes 552968 | tf_op jit(solution)/shard_map/ppermute | solution.py:490
  169.7 2.8 %collective-permute-start.18 = (f32[2,5,6,128]{3,2,1,0:T(8,128)S(1)}, f32[2,5,6,128]{3,2,1,0:T(8,128)S(1)}, u32[]{:S(2)}, u32[]{:S(2)}) collective-permute-start(f32[2,5,6,128]{3,2,1,0:T(8,128)S(1)} %get-tuple-element.67), channel_id=1, source_target_pairs={{0,1},{1,2},{2,3},{3,0},{4,5},{5,6},{6,7},{7,4},{8,9},{9,10},{10,1... | collective-permute-start | bytes 92168 | tf_op jit(solution)/shard_map/ppermute | solution.py:490
  171.4 3.4 %collective-permute-start.19 = (f32[2,5,6,128]{3,2,1,0:T(8,128)S(1)}, f32[2,5,6,128]{3,2,1,0:T(8,128)S(1)}, u32[]{:S(2)}, u32[]{:S(2)}) collective-permute-start(f32[2,5,6,128]{3,2,1,0:T(8,128)S(1)} %get-tuple-element.68), channel_id=1, source_target_pairs={{0,3},{1,0},{2,1},{3,2},{4,7},{5,4},{6,5},{7,6},{8,11},{9,8},{10,9... | collective-permute-start | bytes 92168 | tf_op jit(solution)/shard_map/ppermute | solution.py:490
  (25 other events, 103.3 us)

commit v3 on v2

--- a/solution.py
+++ b/solution.py
@@ -18,6 +18,7 @@
 NODES = 216
 LANES = 128
 CHUNKS = 2
+WHOLE = (True, False)
 F32 = jnp.float32
 BF16 = jnp.bfloat16
 I32 = jnp.int32
@@ -102,7 +103,16 @@
     return out
 
 
-def split_kernel(ex, ey, rho_ref, vel_ref, hot_ref, hi_ref, lo_ref):
+def fetch(pairs, sems):
+    copies = [pltpu.make_async_copy(a, b, sems.at[n]) for n, (a, b) in enumerate(pairs)]
+    for copy in copies:
+        copy.start()
+    for copy in copies:
+        copy.wait()
+
+
+def split_kernel(ex, ey, rho_in, vel_in, hot_in, hi_ref, lo_ref, rho_ref, vel_ref, hot_ref, sems):
+    fetch(((rho_in, rho_ref), (vel_in, vel_ref), (hot_in, hot_ref)), sems)
     state = state_columns(rho_ref, vel_ref, hot_ref, ex, ey)
     for q in range(5):
         hi, lo = halves(jnp.concatenate(state[q], axis=1))
@@ -110,8 +120,8 @@
         lo_ref[q * NODES : (q + 1) * NODES, :] = lo
 
 
-def block_device(c, s, me, groups, sign):
-    return s if c == 0 else lax.rem(me + sign * s + groups, groups)
+def block_device(c, s, me):
+    return s if WHOLE[c] else jnp.bitwise_xor(me, s)
 
 
 def block_view(refs, s):
@@ -126,7 +136,7 @@
     cap = LANES // 4
     slots = groups * cap
     ids = jnp.concatenate(
-        [ids_ref[pl.ds(block_device(c, s, me, groups, 1), 1), :] for s in range(groups)], axis=0
+        [ids_ref[pl.ds(block_device(c, s, me), 1), :] for s in range(groups)], axis=0
     )
     places, slab, firsts = sorted_places(ids, elems, groups)
     elem = jnp.bitwise_and(ids, elems - 1)
@@ -232,7 +242,7 @@
 
 def particle_kernel(c, groups, me_ref, firsts_ref, data_ref, live_ref, after_ref, *refs):
     host, work, force = refs[-3:]
-    blocks = 1 if c == 0 else groups
+    blocks = 1 if WHOLE[c] else groups
     recv_refs, out_refs = refs[:blocks], refs[blocks:-3]
     rows = recv_refs[0].shape[-2]
     cap = LANES // 4
@@ -241,7 +251,7 @@
     width = data_ref.shape[2]
     begins, ends = [], []
     for s in range(groups):
-        g = block_device(c, s, me, groups, -1)
+        g = block_device(c, s, me)
         begins.append(jnp.right_shift(firsts_ref[g] - c + 1, 1))
         ends.append(jnp.right_shift(firsts_ref[g + 1] - c + 1, 1))
 
@@ -359,16 +369,17 @@
     return out
 
 
-def load_kernel(groups, recv_ref, req_ref, fluid_ref, out_ref):
-    loads = collect([recv_ref], groups, req_ref, fluid_ref.shape[2])
+def load_kernel(groups, *refs):
+    req_ref, fluid_ref, out_ref = refs[-3:]
+    loads = collect(refs[:-3], groups, req_ref, fluid_ref.shape[2])
     out_ref[0] = fluid_ref[0]
     for r in range(4):
         out_ref[1 + r] = fluid_ref[1 + r] - loads[r]
 
 
 def join_kernel(groups, ex, ey, *refs):
-    req_ref, part_ref, out_ref, xlo_ref, xhi_ref, ylo_ref, yhi_ref = refs[groups:]
-    loads = collect(refs[:groups], groups, req_ref, part_ref.shape[2])
+    req_ref, part_ref, out_ref, xlo_ref, xhi_ref, ylo_ref, yhi_ref = refs[-7:]
+    loads = collect(refs[:-7], groups, req_ref, part_ref.shape[2])
     out_ref[0] = part_ref[0]
     for r in range(4):
         out_ref[1 + r] = part_ref[1 + r] - loads[r]
@@ -433,10 +444,12 @@
                 out_ref[pl.ds((x * 5 + q) * NODES * ey + y, NODES, stride=ey), :] = work[at]
 
 
-def call(kernel, out_shape, scratch=(), smem=0, late=0, flops=0, operands=()):
+def call(kernel, out_shape, scratch=(), smem=0, late=0, hbm=(), flops=0, operands=()):
     spaces = [pltpu.SMEM if at < smem else pltpu.VMEM for at in range(len(operands))]
     if late:
         spaces[late] = pl.ANY
+    for at in hbm:
+        spaces[at] = pltpu.HBM
     return pl.pallas_call(
         kernel,
         out_shape=out_shape,
@@ -470,14 +483,17 @@
         (own // elems < jnp.arange(groups + 1, dtype=I32)[:, None]).astype(I32), axis=1
     )
 
-    def turn(x, by):
-        return lax.ppermute(x, "gx", [(i, (i + by) % groups) for i in range(groups)])
-
-    def spread(blocks, sign):
-        return [blocks[0]] + [turn(blocks[s], sign * s) for s in range(1, groups)]
+    def swap(x, by):
+        return lax.ppermute(x, "gx", [(i, i ^ by) for i in range(groups)])
 
     def exchange(x):
         return lax.all_to_all(x, "gx", 0, 0, tiled=True)
+
+    def send(c, blocks):
+        if WHOLE[c]:
+            return [exchange(blocks[0])]
+        got = {s: swap(blocks[s], s) for s in range(groups - 1, 0, -1)}
+        return [blocks[0]] + [got[s] for s in range(1, groups)]
 
     ids = exchange(jnp.broadcast_to(own, (groups, bins)))
     rho_v = rho.transpose(0, 2, 3, 4, 1, 5).reshape(-1, height)
@@ -492,6 +508,8 @@
     high, low = call(
         functools.partial(split_kernel, ex, ey),
         [shape(5 * NODES, elems, dtype=BF16)] * 2,
+        [pltpu.VMEM(x.shape, F32) for x in (rho_v, flow_v, hot_v)] + [pltpu.SemaphoreType.DMA((3,))],
+        hbm=(0, 1, 2),
         flops=10_000_000,
         operands=(rho_v, flow_v, hot_v),
     )
@@ -504,7 +522,7 @@
     data, live = arranged[:CHUNKS], arranged[CHUNKS:]
     states, wanted = [], []
     for c in range(CHUNKS):
-        blocks = [shape(groups, rows, 4 * cap)] if c == 0 else [shape(rows, 4 * cap)] * groups
+        blocks = [shape(groups, rows, 4 * cap)] if WHOLE[c] else [shape(rows, 4 * cap)] * groups
         *wire, req = call(
             functools.partial(gather_kernel, c, elems, groups),
             blocks + [shape(groups * cap, LANES, dtype=I32)],
@@ -514,7 +532,7 @@
             flops=10_000_000,
             operands=(me, ids, high, low, ids if c == 0 else wanted[0]),
         )
-        states.append([exchange(wire[0])] if c == 0 else spread(wire, 1))
+        states.append(send(c, wire))
         wanted.append(req)
     fluid = call(
         functools.partial(fluid_kernel, ex, ey),
@@ -528,11 +546,11 @@
         operands=(jnp.asarray(gll_operator()), rho_v, flow_v, hot_v),
     )
     given = []
-    after = fluid
+    after = wanted[1]
     for c in range(CHUNKS):
         wire = call(
             functools.partial(particle_kernel, c, groups),
-            [shape(groups, NODES, 4 * cap)] if c == 0 else [shape(NODES, 4 * cap)] * groups,
+            [shape(groups, NODES, 4 * cap)] if WHOLE[c] else [shape(NODES, 4 * cap)] * groups,
             [
                 pltpu.VMEM((4 * rows, half), F32),
                 pltpu.VMEM((4 * NODES, half), F32),
@@ -544,12 +562,12 @@
             operands=(me, firsts, data[c], live[c], after, *states[c]),
         )
         after = wire[0]
-        given.append([exchange(wire[0])] if c == 0 else spread(wire, -1))
+        given.append(send(c, wire))
     part = call(
         functools.partial(load_kernel, groups),
         shape(5, NODES, elems),
         flops=5_000_000,
-        operands=(given[0][0], wanted[0], fluid),
+        operands=(*given[0], wanted[0], fluid),
     )
     part, xlo, xhi, ylo, yhi = call(
         functools.partial(join_kernel, groups, ex, ey),

time: 178 us -> 183 us (1.028)
  the two profiles are of different devices: /device:TPU:17 before, /device:TPU:9 now
where the time goes in v3:
time: 183 us; the launch traced here: 182 us
  starting transfers between devices  59 us (32%)
  Pallas kernels  53 us (29%)
  waiting for transfers between devices  49.1 us (27%)
  local copies, waits for them, and re-layouts  20.7 us (11%)
    pallas_call x11, Pallas kernels, call(): pl.pallas_call(kernel, out_shape=out_shape, in_specs=[pl.BlockSpec(memory...  53 us
    ppermute x14, waiting for transfers between devices, swap(): return lax.ppermute(x, 'gx', [(i, i ^ by) for i in range(groups)])  34 us
    ppermute x14, starting transfers between devices, swap(): return lax.ppermute(x, 'gx', [(i, i ^ by) for i in range(groups)])  28.9 us
    unnamed x73, local copies, waits for them, and re-layouts  19.4 us
    all_to_all x3, starting transfers between devices, exchange(): return lax.all_to_all(x, 'gx', 0, 0, tiled=True)  18.4 us
    all_to_all x3, waiting for transfers between devices, exchange(): return lax.all_to_all(x, 'gx', 0, 0, tiled=True)  7.64 us
    ppermute x4, starting transfers between devices, turn_y(): return lax.ppermute(x, 'gy', [(i, (i + by) % spans) for i in range(spans)])  5.56 us
    ppermute x1, starting transfers between devices, step(): xr = lax.ppermute(xlo, 'gx', [(i + 1, i) for i in range(groups - 1)])  4.26 us
  transfers between devices with their start and end apart: 23, of which 11 were waited for; matrix products, arithmetic and copies ran while one was open for 0% of the time, Pallas kernels for 17%

profile of v3, /device:TPU:9, one launch (start us, length us, event | category | flops | bytes accessed | tf_op | source)
XLA Modules:
  0.0 182.2 jit_solution(16596554035989362313)
XLA Ops:
  1.3 5.7 %all-to-all-start = ((s32[8,1,256]{2,1,0:T(1,128)}), s32[8,1,256]{2,1,0:T(1,128)S(1)}, u32[]{:S(2)}, u32[]{:S(2)}) async-start(s32[8,1,256]{2,1,0:T(1,128)} %broadcast_in_dim.2), calls=%async_computation | async-start | bytes 16384 | tf_op jit(solution)/shard_map/all_to_all | solution.py:490
  15.3 5.6 %all-to-all-start.1 = ((f32[8,272,128]{2,1,0:T(8,128)}), f32[8,272,128]{2,1,0:T(8,128)S(1)}, u32[]{:S(2)}, u32[]{:S(2)}) async-start(f32[8,272,128]{2,1,0:T(8,128)} %copy-done.11), calls=%async_computation.1 | async-start | bytes 2228224 | tf_op jit(solution)/shard_map/all_to_all | solution.py:490
  24.5 2.8 %shard_map.100 = (f32[23,128,128]{2,1,0:T(8,128)S(1)}, f32[23,128,128]{2,1,0:T(8,128)S(1)}, s32[8,128]{1,0:T(8,128)S(1)}, s32[8,128]{1,0:T(8,128)S(1)}) custom-call(s32[1,256]{1,0:T(1,128)S(1)} %bitcast.33, s32[1,256]{1,0:T(1,128)S(1)} %bitcast.34, f32[18,256,128]{2,1,0:T(8,128)S(1)} %bitcast.24, f32[3,256,128]{2,1,0:T(8,128)S(1)} %bitcast.29, ...), custom_call_target="tpu_custom_call" | custom-call | flops 10000000 | bytes 3016704 | tf_op jit(solution)/shard_map/pallas_call | solution.py:453
  37.2 7.6 %all-to-all-done.1.refs_0_ = f32[8,272,128]{2,1,0:T(8,128)S(1)} async-done(((f32[8,272,128]{2,1,0:T(8,128)}), f32[8,272,128]{2,1,0:T(8,128)S(1)}, u32[]{:S(2)}, u32[]{:S(2)}) %all-to-all-start.1) | async-done | bytes 1114144 | tf_op jit(solution)/shard_map/all_to_all | solution.py:490
  46.2 15.0 %shard_map.104.after_ref = f32[8,216,128]{2,1,0:T(8,128)} custom-call(s32[1]{0:T(128)} %bitcast.me_ref, s32[9]{0:T(128)S(1)} %convert_reduce_fusion.firsts_ref, f32[23,128,128]{2,1,0:T(8,128)S(1)} %copy-done.8, s32[8,128]{1,0:T(8,128)S(1)} %get-tuple-element.40.live_ref, s32[256,128]{1,0:T(8,128)S(1)} %get-tuple-element.44.after_ref.refs_8_, ...), custom_call_target="tpu_custom_call" | custom-call | flops 20000000 | bytes 2756648 | tf_op jit(solution)/shard_map/pallas_call | solution.py:453
  61.2 7.1 %all-to-all-start.2 = ((f32[8,216,128]{2,1,0:T(8,128)}), f32[8,216,128]{2,1,0:T(8,128)S(1)}, u32[]{:S(2)}, u32[]{:S(2)}) async-start(f32[8,216,128]{2,1,0:T(8,128)} %shard_map.104.after_ref), calls=%async_computation.2 | async-start | bytes 1769472 | tf_op jit(solution)/shard_map/all_to_all | solution.py:490
  74.3 4.0 %collective-permute-done.refs_1_ = f32[272,128]{1,0:T(8,128)S(1)} collective-permute-done((f32[272,128]{1,0:T(8,128)}, f32[272,128]{1,0:T(8,128)S(1)}, u32[]{:S(2)}, u32[]{:S(2)}) %collective-permute-start) | collective-permute-done | bytes 139296 | tf_op jit(solution)/shard_map/ppermute | solution.py:487
  78.3 2.3 %collective-permute-start.5 = (f32[272,128]{1,0:T(8,128)}, f32[272,128]{1,0:T(8,128)S(1)}, u32[]{:S(2)}, u32[]{:S(2)}) collective-permute-start(f32[272,128]{1,0:T(8,128)} %copy-done.30), channel_id=1, source_target_pairs={{0,24},{4,28},{8,16},{12,20},{16,8},{20,12},{24,0},{28,4},{1,25},{... | collective-permute-start | bytes 417800 | tf_op jit(solution)/shard_map/ppermute | solution.py:487
  80.5 5.2 %collective-permute-done.1.refs_2_ = f32[272,128]{1,0:T(8,128)S(1)} collective-permute-done((f32[272,128]{1,0:T(8,128)}, f32[272,128]{1,0:T(8,128)S(1)}, u32[]{:S(2)}, u32[]{:S(2)}) %collective-permute-start.1) | collective-permute-done | bytes 139296 | tf_op jit(solution)/shard_map/ppermute | solution.py:487
  85.7 3.3 %collective-permute-start.6 = (f32[272,128]{1,0:T(8,128)}, f32[272,128]{1,0:T(8,128)S(1)}, u32[]{:S(2)}, u32[]{:S(2)}) collective-permute-start(f32[272,128]{1,0:T(8,128)} %copy-done.29), channel_id=1, source_target_pairs={{0,28},{4,24},{8,20},{12,16},{16,12},{20,8},{24,4},{28,0},{1,29},{... | collective-permute-start | bytes 417800 | tf_op jit(solution)/shard_map/ppermute | solution.py:487
  89.9 12.7 %collective-permute-done.3.refs_4_ = f32[272,128]{1,0:T(8,128)S(1)} collective-permute-done((f32[272,128]{1,0:T(8,128)}, f32[272,128]{1,0:T(8,128)S(1)}, u32[]{:S(2)}, u32[]{:S(2)}) %collective-permute-start.3) | collective-permute-done | bytes 139296 | tf_op jit(solution)/shard_map/ppermute | solution.py:487
  102.6 3.0 %collective-permute-done.4.refs_5_ = f32[272,128]{1,0:T(8,128)S(1)} collective-permute-done((f32[272,128]{1,0:T(8,128)}, f32[272,128]{1,0:T(8,128)S(1)}, u32[]{:S(2)}, u32[]{:S(2)}) %collective-permute-start.4) | collective-permute-done | bytes 139296 | tf_op jit(solution)/shard_map/ppermute | solution.py:487
  105.6 4.4 %collective-permute-done.5.refs_6_ = f32[272,128]{1,0:T(8,128)S(1)} collective-permute-done((f32[272,128]{1,0:T(8,128)}, f32[272,128]{1,0:T(8,128)S(1)}, u32[]{:S(2)}, u32[]{:S(2)}) %collective-permute-start.5) | collective-permute-done | bytes 139296 | tf_op jit(solution)/shard_map/ppermute | solution.py:487
  109.9 3.8 %collective-permute-done.6.refs_7_ = f32[272,128]{1,0:T(8,128)S(1)} collective-permute-done((f32[272,128]{1,0:T(8,128)}, f32[272,128]{1,0:T(8,128)S(1)}, u32[]{:S(2)}, u32[]{:S(2)}) %collective-permute-start.6) | collective-permute-done | bytes 139296 | tf_op jit(solution)/shard_map/ppermute | solution.py:487
  113.8 14.7 %shard_map.105 = (f32[216,128]{1,0:T(8,128)S(1)}, f32[216,128]{1,0:T(8,128)}, f32[216,128]{1,0:T(8,128)}, f32[216,128]{1,0:T(8,128)}, f32[216,128]{1,0:T(8,128)S...) custom-call(s32[1]{0:T(128)} %bitcast.me_ref, s32[9]{0:T(128)S(1)} %convert_reduce_fusion.firsts_ref, ...), custom_call_target="tpu_custom_call" | custom-call | flops 20000000 | bytes 3510312 | tf_op jit(solution)/shard_map/pallas_call | solution.py:453
  129.2 2.4 %collective-permute-start.11 = (f32[216,128]{1,0:T(8,128)S(1)}, f32[216,128]{1,0:T(8,128)S(1)}, u32[]{:S(2)}, u32[]{:S(2)}) collective-permute-start(f32[216,128]{1,0:T(8,128)S(1)} %get-tuple-element.59), channel_id=1, source_target_pairs={{0,20},{4,16},{8,28},{12,24},{16,4},{20,0},{24,12},{28,8},{1,21},{... | collective-permute-start | bytes 331784 | tf_op jit(solution)/shard_map/ppermute | solution.py:487
  134.9 9.8 %collective-permute-start.8 = (f32[216,128]{1,0:T(8,128)}, f32[216,128]{1,0:T(8,128)}, u32[]{:S(2)}, u32[]{:S(2)}) collective-permute-start(f32[216,128]{1,0:T(8,128)} %get-tuple-element.56), channel_id=1, source_target_pairs={{0,8},{4,12},{8,0},{12,4},{16,24},{20,28},{24,16},{28,20},{1,9},{5... | collective-permute-start | bytes 331784 | tf_op jit(solution)/shard_map/ppermute | solution.py:487
  145.4 2.5 %collective-permute-start.9 = (f32[216,128]{1,0:T(8,128)}, f32[216,128]{1,0:T(8,128)}, u32[]{:S(2)}, u32[]{:S(2)}) collective-permute-start(f32[216,128]{1,0:T(8,128)} %get-tuple-element.57), channel_id=1, source_target_pairs={{0,12},{4,8},{8,4},{12,0},{16,28},{20,24},{24,20},{28,16},{1,13},{... | collective-permute-start | bytes 331784 | tf_op jit(solution)/shard_map/ppermute | solution.py:487
  147.9 7.3 %shard_map.106.refs_2_ = f32[5,216,512]{2,1,0:T(8,128)S(1)} custom-call(f32[216,648]{1,0:T(8,128)S(1)} %copy-done.12, f32[864,128]{1,0:T(8,128)S(1)} %bitcast.26, f32[2592,128]{1,0:T(8,128)S(1)} %bitcast.23, f32[864,128]{1,0:T(8,128)S(1)} %bitcast.28), custom_call_target="tpu_custom_call" | custom-call | flops 10000000 | bytes 2771712 | tf_op jit(solution)/shard_map/pallas_call | solution.py:453
  157.4 3.4 %shard_map.108 = (f32[5,216,512]{2,1,0:T(8,128)S(1)}, f32[5,36,256]{2,1,0:T(8,128)S(1)}, f32[5,36,256]{2,1,0:T(8,128)S(1)}, f32[5,36,256]{2,1,0:T(8,128)S(1)}, f32[5,36,256]{2,1,0:T(8,128)S(1)}) custom-call(f32[216,128]{1,0:T(8,128)S(1)} %copy-done.22, f32[216,128]{1,0:T(8,128)} %collective-permute-done.7.refs_1_, ...), custom_call_target="tpu_custom_call" | custom-call | flops 5000000 | bytes 3227648 | tf_op jit(solution)/shard_map/pallas_call | solution.py:453
  162.7 4.3 %collective-permute-start.15 = (f32[5,36,256]{2,1,0:T(8,128)S(1)}, f32[5,36,256]{2,1,0:T(8,128)S(1)}, u32[]{:S(2)}, u32[]{:S(2)}) collective-permute-start(f32[5,36,256]{2,1,0:T(8,128)S(1)} %get-tuple-element.64), channel_id=1, source_target_pairs={{4,0},{8,4},{12,8},{16,12},{20,16},{24,20},{28,24},{5,1},{9,5},{13... | collective-permute-start | bytes 552968 | tf_op jit(solution)/shard_map/ppermute | solution.py:585
  167.0 3.7 %collective-permute-start.16 = (f32[5,36,256]{2,1,0:T(8,128)S(1)}, f32[5,36,256]{2,1,0:T(8,128)S(1)}, u32[]{:S(2)}, u32[]{:S(2)}) collective-permute-start(f32[5,36,256]{2,1,0:T(8,128)S(1)} %get-tuple-element.65), channel_id=1, source_target_pairs={{0,1},{1,2},{2,3},{3,0},{4,5},{5,6},{6,7},{7,4},{8,9},{9,10},{10,1... | collective-permute-start | bytes 552968 | tf_op jit(solution)/shard_map/ppermute | solution.py:506
  170.7 4.1 %collective-permute-done.15.xr_ref = f32[5,36,256]{2,1,0:T(8,128)S(1)} collective-permute-done((f32[5,36,256]{2,1,0:T(8,128)S(1)}, f32[5,36,256]{2,1,0:T(8,128)S(1)}, u32[]{:S(2)}, u32[]{:S(2)}) %collective-permute-start.15) | collective-permute-done | bytes 184352 | tf_op jit(solution)/shard_map/ppermute | solution.py:585
  177.7 2.3 %collective-permute-done.19.er_ref = f32[2,5,6,128]{3,2,1,0:T(8,128)S(1)} collective-permute-done((f32[2,5,6,128]{3,2,1,0:T(8,128)S(1)}, f32[2,5,6,128]{3,2,1,0:T(8,128)S(1)}, u32[]{:S(2)}, u32[]{:S(2)}) %collective-permute-start.19) | collective-permute-done | bytes 30752 | tf_op jit(solution)/shard_map/ppermute | solution.py:506
  (109 shorter events, 44.9 us)
Async XLA Ops:
  1.3 10.1 %all-to-all-start = ((s32[8,1,256]{2,1,0:T(1,128)}), s32[8,1,256]{2,1,0:T(1,128)S(1)}, u32[]{:S(2)}, u32[]{:S(2)}) async-start(s32[8,1,256]{2,1,0:T(1,128)} %broadcast_in_dim.2), calls=%async_computation | async-start | bytes 16384 | tf_op jit(solution)/shard_map/all_to_all | solution.py:490
  15.3 29.5 %all-to-all-start.1 = ((f32[8,272,128]{2,1,0:T(8,128)}), f32[8,272,128]{2,1,0:T(8,128)S(1)}, u32[]{:S(2)}, u32[]{:S(2)}) async-start(f32[8,272,128]{2,1,0:T(8,128)} %copy-done.11), calls=%async_computation.1 | async-start | bytes 2228224 | tf_op jit(solution)/shard_map/all_to_all | solution.py:490
  61.2 52.5 %copy-start.18 = (f32[272,128]{1,0:T(8,128)S(1)}, f32[272,128]{1,0:T(8,128)}, u32[]{:S(2)}) copy-start(f32[272,128]{1,0:T(8,128)} %copy-done.17) | copy-start | bytes 417796
  61.2 94.0 %all-to-all-start.2 = ((f32[8,216,128]{2,1,0:T(8,128)}), f32[8,216,128]{2,1,0:T(8,128)S(1)}, u32[]{:S(2)}, u32[]{:S(2)}) async-start(f32[8,216,128]{2,1,0:T(8,128)} %shard_map.104.after_ref), calls=%async_computation.2 | async-start | bytes 1769472 | tf_op jit(solution)/shard_map/all_to_all | solution.py:490
  68.3 9.9 %collective-permute-start = (f32[272,128]{1,0:T(8,128)}, f32[272,128]{1,0:T(8,128)S(1)}, u32[]{:S(2)}, u32[]{:S(2)}) collective-permute-start(f32[272,128]{1,0:T(8,128)} %copy-done.35), channel_id=1, source_target_pairs={{0,4},{4,0},{8,12},{12,8},{16,20},{20,16},{24,28},{28,24},{1,5},{5... | collective-permute-start | bytes 417800 | tf_op jit(solution)/shard_map/ppermute | solution.py:487
  69.5 16.2 %collective-permute-start.1 = (f32[272,128]{1,0:T(8,128)}, f32[272,128]{1,0:T(8,128)S(1)}, u32[]{:S(2)}, u32[]{:S(2)}) collective-permute-start(f32[272,128]{1,0:T(8,128)} %copy-done.34), channel_id=1, source_target_pairs={{0,8},{4,12},{8,0},{12,4},{16,24},{20,28},{24,16},{28,20},{1,9},{5... | collective-permute-start | bytes 417800 | tf_op jit(solution)/shard_map/ppermute | solution.py:487
  69.8 20.1 %collective-permute-start.2 = (f32[272,128]{1,0:T(8,128)}, f32[272,128]{1,0:T(8,128)S(1)}, u32[]{:S(2)}, u32[]{:S(2)}) collective-permute-start(f32[272,128]{1,0:T(8,128)} %copy-done.33), channel_id=1, source_target_pairs={{0,12},{4,8},{8,4},{12,0},{16,28},{20,24},{24,20},{28,16},{1,13},{... | collective-permute-start | bytes 417800 | tf_op jit(solution)/shard_map/ppermute | solution.py:487
  71.0 31.6 %collective-permute-start.3 = (f32[272,128]{1,0:T(8,128)}, f32[272,128]{1,0:T(8,128)S(1)}, u32[]{:S(2)}, u32[]{:S(2)}) collective-permute-start(f32[272,128]{1,0:T(8,128)} %copy-done.32), channel_id=1, source_target_pairs={{0,16},{4,20},{8,24},{12,28},{16,0},{20,4},{24,8},{28,12},{1,17},{... | collective-permute-start | bytes 417800 | tf_op jit(solution)/shard_map/ppermute | solution.py:487
  73.1 32.5 %collective-permute-start.4 = (f32[272,128]{1,0:T(8,128)}, f32[272,128]{1,0:T(8,128)S(1)}, u32[]{:S(2)}, u32[]{:S(2)}) collective-permute-start(f32[272,128]{1,0:T(8,128)} %copy-done.31), channel_id=1, source_target_pairs={{0,20},{4,16},{8,28},{12,24},{16,4},{20,0},{24,12},{28,8},{1,21},{... | collective-permute-start | bytes 417800 | tf_op jit(solution)/shard_map/ppermute | solution.py:487
  78.3 31.7 %collective-permute-start.5 = (f32[272,128]{1,0:T(8,128)}, f32[272,128]{1,0:T(8,128)S(1)}, u32[]{:S(2)}, u32[]{:S(2)}) collective-permute-start(f32[272,128]{1,0:T(8,128)} %copy-done.30), channel_id=1, source_target_pairs={{0,24},{4,28},{8,16},{12,20},{16,8},{20,12},{24,0},{28,4},{1,25},{... | collective-permute-start | bytes 417800 | tf_op jit(solution)/shard_map/ppermute | solution.py:487
  85.7 28.0 %collective-permute-start.6 = (f32[272,128]{1,0:T(8,128)}, f32[272,128]{1,0:T(8,128)S(1)}, u32[]{:S(2)}, u32[]{:S(2)}) collective-permute-start(f32[272,128]{1,0:T(8,128)} %copy-done.29), channel_id=1, source_target_pairs={{0,28},{4,24},{8,20},{12,16},{16,12},{20,8},{24,4},{28,0},{1,29},{... | collective-permute-start | bytes 417800 | tf_op jit(solution)/shard_map/ppermute | solution.py:487
  129.2 5.1 %collective-permute-start.10 = (f32[216,128]{1,0:T(8,128)S(1)}, f32[216,128]{1,0:T(8,128)S(1)}, u32[]{:S(2)}, u32[]{:S(2)}) collective-permute-start(f32[216,128]{1,0:T(8,128)S(1)} %get-tuple-element.58), channel_id=1, source_target_pairs={{0,16},{4,20},{8,24},{12,28},{16,0},{20,4},{24,8},{28,12},{1,17},{... | collective-permute-start | bytes 331784 | tf_op jit(solution)/shard_map/ppermute | solution.py:487
  129.2 15.6 %collective-permute-start.11 = (f32[216,128]{1,0:T(8,128)S(1)}, f32[216,128]{1,0:T(8,128)S(1)}, u32[]{:S(2)}, u32[]{:S(2)}) collective-permute-start(f32[216,128]{1,0:T(8,128)S(1)} %get-tuple-element.59), channel_id=1, source_target_pairs={{0,20},{4,16},{8,28},{12,24},{16,4},{20,0},{24,12},{28,8},{1,21},{... | collective-permute-start | bytes 331784 | tf_op jit(solution)/shard_map/ppermute | solution.py:487
  131.6 25.7 %collective-permute-start.12 = (f32[216,128]{1,0:T(8,128)}, f32[216,128]{1,0:T(8,128)}, u32[]{:S(2)}, u32[]{:S(2)}) collective-permute-start(f32[216,128]{1,0:T(8,128)} %get-tuple-element.60), channel_id=1, source_target_pairs={{0,24},{4,28},{8,16},{12,20},{16,8},{20,12},{24,0},{28,4},{1,25},{... | collective-permute-start | bytes 331784 | tf_op jit(solution)/shard_map/ppermute | solution.py:487
  132.3 25.0 %collective-permute-start.13 = (f32[216,128]{1,0:T(8,128)}, f32[216,128]{1,0:T(8,128)}, u32[]{:S(2)}, u32[]{:S(2)}) collective-permute-start(f32[216,128]{1,0:T(8,128)} %get-tuple-element.61), channel_id=1, source_target_pairs={{0,28},{4,24},{8,20},{12,16},{16,12},{20,8},{24,4},{28,0},{1,29},{... | collective-permute-start | bytes 331784 | tf_op jit(solution)/shard_map/ppermute | solution.py:487
  133.9 23.5 %collective-permute-start.7 = (f32[216,128]{1,0:T(8,128)}, f32[216,128]{1,0:T(8,128)}, u32[]{:S(2)}, u32[]{:S(2)}) collective-permute-start(f32[216,128]{1,0:T(8,128)} %get-tuple-element.55), channel_id=1, source_target_pairs={{0,4},{4,0},{8,12},{12,8},{16,20},{20,16},{24,28},{28,24},{1,5},{5... | collective-permute-start | bytes 331784 | tf_op jit(solution)/shard_map/ppermute | solution.py:487
  134.9 22.5 %collective-permute-start.8 = (f32[216,128]{1,0:T(8,128)}, f32[216,128]{1,0:T(8,128)}, u32[]{:S(2)}, u32[]{:S(2)}) collective-permute-start(f32[216,128]{1,0:T(8,128)} %get-tuple-element.56), channel_id=1, source_target_pairs={{0,8},{4,12},{8,0},{12,4},{16,24},{20,28},{24,16},{28,20},{1,9},{5... | collective-permute-start | bytes 331784 | tf_op jit(solution)/shard_map/ppermute | solution.py:487
  145.4 12.0 %collective-permute-start.9 = (f32[216,128]{1,0:T(8,128)}, f32[216,128]{1,0:T(8,128)}, u32[]{:S(2)}, u32[]{:S(2)}) collective-permute-start(f32[216,128]{1,0:T(8,128)} %get-tuple-element.57), channel_id=1, source_target_pairs={{0,12},{4,8},{8,4},{12,0},{16,28},{20,24},{24,20},{28,16},{1,13},{... | collective-permute-start | bytes 331784 | tf_op jit(solution)/shard_map/ppermute | solution.py:487
  160.8 9.9 %collective-permute-start.14 = (f32[5,36,256]{2,1,0:T(8,128)S(1)}, f32[5,36,256]{2,1,0:T(8,128)S(1)}, u32[]{:S(2)}, u32[]{:S(2)}) collective-permute-start(f32[5,36,256]{2,1,0:T(8,128)S(1)} %get-tuple-element.63), channel_id=1, source_target_pairs={{0,4},{4,8},{8,12},{12,16},{16,20},{20,24},{24,28},{1,5},{5,9},{9,... | collective-permute-start | bytes 552968 | tf_op jit(solution)/shard_map/ppermute | solution.py:584
  162.7 12.1 %collective-permute-start.15 = (f32[5,36,256]{2,1,0:T(8,128)S(1)}, f32[5,36,256]{2,1,0:T(8,128)S(1)}, u32[]{:S(2)}, u32[]{:S(2)}) collective-permute-start(f32[5,36,256]{2,1,0:T(8,128)S(1)} %get-tuple-element.64), channel_id=1, source_target_pairs={{4,0},{8,4},{12,8},{16,12},{20,16},{24,20},{28,24},{5,1},{9,5},{13... | collective-permute-start | bytes 552968 | tf_op jit(solution)/shard_map/ppermute | solution.py:585
  167.0 9.6 %collective-permute-start.16 = (f32[5,36,256]{2,1,0:T(8,128)S(1)}, f32[5,36,256]{2,1,0:T(8,128)S(1)}, u32[]{:S(2)}, u32[]{:S(2)}) collective-permute-start(f32[5,36,256]{2,1,0:T(8,128)S(1)} %get-tuple-element.65), channel_id=1, source_target_pairs={{0,1},{1,2},{2,3},{3,0},{4,5},{5,6},{6,7},{7,4},{8,9},{9,10},{10,1... | collective-permute-start | bytes 552968 | tf_op jit(solution)/shard_map/ppermute | solution.py:506
  170.7 5.9 %collective-permute-start.17 = (f32[5,36,256]{2,1,0:T(8,128)S(1)}, f32[5,36,256]{2,1,0:T(8,128)S(1)}, u32[]{:S(2)}, u32[]{:S(2)}) collective-permute-start(f32[5,36,256]{2,1,0:T(8,128)S(1)} %get-tuple-element.66), channel_id=1, source_target_pairs={{0,3},{1,0},{2,1},{3,2},{4,7},{5,4},{6,5},{7,6},{8,11},{9,8},{10,9... | collective-permute-start | bytes 552968 | tf_op jit(solution)/shard_map/ppermute | solution.py:506
  174.8 2.9 %collective-permute-start.18 = (f32[2,5,6,128]{3,2,1,0:T(8,128)S(1)}, f32[2,5,6,128]{3,2,1,0:T(8,128)S(1)}, u32[]{:S(2)}, u32[]{:S(2)}) collective-permute-start(f32[2,5,6,128]{3,2,1,0:T(8,128)S(1)} %get-tuple-element.67), channel_id=1, source_target_pairs={{0,1},{1,2},{2,3},{3,0},{4,5},{5,6},{6,7},{7,4},{8,9},{9,10},{10,1... | collective-permute-start | bytes 92168 | tf_op jit(solution)/shard_map/ppermute | solution.py:506
  176.6 3.4 %collective-permute-start.19 = (f32[2,5,6,128]{3,2,1,0:T(8,128)S(1)}, f32[2,5,6,128]{3,2,1,0:T(8,128)S(1)}, u32[]{:S(2)}, u32[]{:S(2)}) collective-permute-start(f32[2,5,6,128]{3,2,1,0:T(8,128)S(1)} %get-tuple-element.68), channel_id=1, source_target_pairs={{0,3},{1,0},{2,1},{3,2},{4,7},{5,4},{6,5},{7,6},{8,11},{9,8},{10,9... | collective-permute-start | bytes 92168 | tf_op jit(solution)/shard_map/ppermute | solution.py:506
  (35 other events, 246.7 us)

commit v4 on v3

--- a/solution.py
+++ b/solution.py
@@ -399,22 +399,25 @@
                     out_ref[q, 36 * i + 30 : 36 * i + 36, a] = total
                     out_ref[q, 36 * i : 36 * i + 6, b] = total
         last = (ex - 1) * wide
-        xlo_ref[q] = out_ref[q, 0:36, 0:wide]
-        xhi_ref[q] = out_ref[q, 180:216, last : last + wide]
+        face = slice(36 * q, 36 * q + 36)
+        xlo_ref[face, :] = out_ref[q, 0:36, 0:wide]
+        xhi_ref[face, :] = out_ref[q, 180:216, last : last + wide]
         for x in range(ex):
             dst = slice(x * LANES, (x + 1) * LANES)
             lo = slice(x * wide, x * wide + LANES)
             hi = slice((x + 1) * wide - LANES, (x + 1) * wide)
             for i in range(6):
-                ylo_ref[q, 6 * i : 6 * i + 6, dst] = out_ref[q, 36 * i : 36 * i + 6, lo]
-                yhi_ref[q, 6 * i : 6 * i + 6, dst] = out_ref[q, 36 * i + 30 : 36 * i + 36, hi]
+                ylo_ref[36 * q + 6 * i : 36 * q + 6 * i + 6, dst] = out_ref[q, 36 * i : 36 * i + 6, lo]
+                yhi_ref[36 * q + 6 * i : 36 * q + 6 * i + 6, dst] = out_ref[q, 36 * i + 30 : 36 * i + 36, hi]
 
 
 def edge_kernel(ey, xl_ref, xr_ref, lo_ref, hi_ref):
     last = (ey - 1) * LANES
     for x, ref in enumerate((xl_ref, xr_ref)):
-        lo_ref[x] = ref[:, 0:6, 0:LANES]
-        hi_ref[x] = ref[:, 30:36, last : last + LANES]
+        for q in range(5):
+            at = slice((x * 5 + q) * 6, (x * 5 + q) * 6 + 6)
+            lo_ref[at, :] = ref[36 * q : 36 * q + 6, 0:LANES]
+            hi_ref[at, :] = ref[36 * q + 30 : 36 * q + 36, last : last + LANES]
 
 
 def finish_kernel(ex, ey, part_ref, xl_ref, xr_ref, yl_ref, yr_ref, el_ref, er_ref, out_ref, work):
@@ -423,17 +426,18 @@
             work[at] = part_ref[q, :, at * LANES : (at + 1) * LANES]
         for y in range(ey):
             lanes = slice(y * LANES, (y + 1) * LANES)
-            work[y, 0:36, :] += xl_ref[q, :, lanes]
-            work[(ex - 1) * ey + y, 180:216, :] += xr_ref[q, :, lanes]
+            work[y, 0:36, :] += xl_ref[36 * q : 36 * q + 36, lanes]
+            work[(ex - 1) * ey + y, 180:216, :] += xr_ref[36 * q : 36 * q + 36, lanes]
         for x in range(ex):
             lanes = slice(x * LANES, (x + 1) * LANES)
             for i in range(6):
-                work[x * ey, 36 * i : 36 * i + 6, :] += yl_ref[q, 6 * i : 6 * i + 6, lanes]
-                work[x * ey + ey - 1, 36 * i + 30 : 36 * i + 36, :] += yr_ref[q, 6 * i : 6 * i + 6, lanes]
+                work[x * ey, 36 * i : 36 * i + 6, :] += yl_ref[36 * q + 6 * i : 36 * q + 6 * i + 6, lanes]
+                work[x * ey + ey - 1, 36 * i + 30 : 36 * i + 36, :] += yr_ref[36 * q + 6 * i : 36 * q + 6 * i + 6, lanes]
         for x in range(2):
             start, at = 180 * x, x * (ex - 1) * ey
-            work[at, start : start + 6, :] += el_ref[x, q]
-            work[at + ey - 1, start + 30 : start + 36, :] += er_ref[x, q]
+            edge = slice((x * 5 + q) * 6, (x * 5 + q) * 6 + 6)
+            work[at, start : start + 6, :] += el_ref[edge, :]
+            work[at + ey - 1, start + 30 : start + 36, :] += er_ref[edge, :]
         for x in range(ex):
             for y in range(ey):
                 at = x * ey + y
@@ -573,10 +577,10 @@
         functools.partial(join_kernel, groups, ex, ey),
         (
             shape(5, NODES, elems),
-            shape(5, 36, ey * height),
-            shape(5, 36, ey * height),
-            shape(5, 36, ex * height),
-            shape(5, 36, ex * height),
+            shape(180, ey * height),
+            shape(180, ey * height),
+            shape(180, ex * height),
+            shape(180, ex * height),
         ),
         flops=5_000_000,
         operands=(*given[1], wanted[1], part),
@@ -584,9 +588,7 @@
     xl = lax.ppermute(xhi, "gx", [(i, i + 1) for i in range(groups - 1)])
     xr = lax.ppermute(xlo, "gx", [(i + 1, i) for i in range(groups - 1)])
     yl, yr = turn_y(yhi, 1), turn_y(ylo, -1)
-    elo, ehi = call(
-        functools.partial(edge_kernel, ey), [shape(2, 5, 6, height)] * 2, flops=1_000_000, operands=(xl, xr)
-    )
+    elo, ehi = call(functools.partial(edge_kernel, ey), [shape(60, height)] * 2, flops=1_000_000, operands=(xl, xr))
     el, er = turn_y(ehi, 1), turn_y(elo, -1)
     out = call(
         functools.partial(finish_kernel, ex, ey),

time: 183 us -> 182 us (level)
  no operation moved by 1% of the time
where the time goes in v4:
time: 182 us; the launch traced here: 181 us
  starting transfers between devices  59.2 us (33%)
  Pallas kernels  53 us (29%)
  waiting for transfers between devices  48.1 us (26%)
  local copies, waits for them, and re-layouts  20.7 us (11%)
    pallas_call x11, Pallas kernels, call(): pl.pallas_call(kernel, out_shape=out_shape, in_specs=[pl.BlockSpec(memory...  53 us
    ppermute x14, waiting for transfers between devices, swap(): return lax.ppermute(x, 'gx', [(i, i ^ by) for i in range(groups)])  34 us
    ppermute x14, starting transfers between devices, swap(): return lax.ppermute(x, 'gx', [(i, i ^ by) for i in range(groups)])  28.9 us
    unnamed x73, local copies, waits for them, and re-layouts  19.4 us
    all_to_all x3, starting transfers between devices, exchange(): return lax.all_to_all(x, 'gx', 0, 0, tiled=True)  18.4 us
    all_to_all x3, waiting for transfers between devices, exchange(): return lax.all_to_all(x, 'gx', 0, 0, tiled=True)  7.64 us
    ppermute x4, starting transfers between devices, turn_y(): return lax.ppermute(x, 'gy', [(i, (i + by) % spans) for i in range(spans)])  5.72 us
    ppermute x1, starting transfers between devices, step(): xr = lax.ppermute(xlo, 'gx', [(i + 1, i) for i in range(groups - 1)])  4.26 us
  transfers between devices with their start and end apart: 23, of which 11 were waited for; matrix products, arithmetic and copies ran while one was open for 0% of the time, Pallas kernels for 17%

profile of v4, /device:TPU:9, one launch (start us, length us, event | category | flops | bytes accessed | tf_op | source)
XLA Modules:
  0.0 181.4 jit_solution(15738332508526646176)
XLA Ops:
  1.3 5.7 %all-to-all-start = ((s32[8,1,256]{2,1,0:T(1,128)}), s32[8,1,256]{2,1,0:T(1,128)S(1)}, u32[]{:S(2)}, u32[]{:S(2)}) async-start(s32[8,1,256]{2,1,0:T(1,128)} %broadcast_in_dim.2), calls=%async_computation | async-start | bytes 16384 | tf_op jit(solution)/shard_map/all_to_all | solution.py:494
  15.3 5.6 %all-to-all-start.1 = ((f32[8,272,128]{2,1,0:T(8,128)}), f32[8,272,128]{2,1,0:T(8,128)S(1)}, u32[]{:S(2)}, u32[]{:S(2)}) async-start(f32[8,272,128]{2,1,0:T(8,128)} %copy-done.11), calls=%async_computation.1 | async-start | bytes 2228224 | tf_op jit(solution)/shard_map/all_to_all | solution.py:494
  24.5 2.8 %shard_map.100 = (f32[23,128,128]{2,1,0:T(8,128)S(1)}, f32[23,128,128]{2,1,0:T(8,128)S(1)}, s32[8,128]{1,0:T(8,128)S(1)}, s32[8,128]{1,0:T(8,128)S(1)}) custom-call(s32[1,256]{1,0:T(1,128)S(1)} %bitcast.33, s32[1,256]{1,0:T(1,128)S(1)} %bitcast.34, f32[18,256,128]{2,1,0:T(8,128)S(1)} %bitcast.24, f32[3,256,128]{2,1,0:T(8,128)S(1)} %bitcast.29, ...), custom_call_target="tpu_custom_call" | custom-call | flops 10000000 | bytes 3016704 | tf_op jit(solution)/shard_map/pallas_call | solution.py:457
  37.2 7.6 %all-to-all-done.1.refs_0_ = f32[8,272,128]{2,1,0:T(8,128)S(1)} async-done(((f32[8,272,128]{2,1,0:T(8,128)}), f32[8,272,128]{2,1,0:T(8,128)S(1)}, u32[]{:S(2)}, u32[]{:S(2)}) %all-to-all-start.1) | async-done | bytes 1114144 | tf_op jit(solution)/shard_map/all_to_all | solution.py:494
  46.2 15.0 %shard_map.104.after_ref = f32[8,216,128]{2,1,0:T(8,128)} custom-call(s32[1]{0:T(128)} %bitcast.me_ref, s32[9]{0:T(128)S(1)} %convert_reduce_fusion.firsts_ref, f32[23,128,128]{2,1,0:T(8,128)S(1)} %copy-done.8, s32[8,128]{1,0:T(8,128)S(1)} %get-tuple-element.40.live_ref, s32[256,128]{1,0:T(8,128)S(1)} %get-tuple-element.44.after_ref.refs_8_, ...), custom_call_target="tpu_custom_call" | custom-call | flops 20000000 | bytes 2756648 | tf_op jit(solution)/shard_map/pallas_call | solution.py:457
  61.2 7.1 %all-to-all-start.2 = ((f32[8,216,128]{2,1,0:T(8,128)}), f32[8,216,128]{2,1,0:T(8,128)S(1)}, u32[]{:S(2)}, u32[]{:S(2)}) async-start(f32[8,216,128]{2,1,0:T(8,128)} %shard_map.104.after_ref), calls=%async_computation.2 | async-start | bytes 1769472 | tf_op jit(solution)/shard_map/all_to_all | solution.py:494
  74.3 4.0 %collective-permute-done.refs_1_ = f32[272,128]{1,0:T(8,128)S(1)} collective-permute-done((f32[272,128]{1,0:T(8,128)}, f32[272,128]{1,0:T(8,128)S(1)}, u32[]{:S(2)}, u32[]{:S(2)}) %collective-permute-start) | collective-permute-done | bytes 139296 | tf_op jit(solution)/shard_map/ppermute | solution.py:491
  78.3 2.3 %collective-permute-start.5 = (f32[272,128]{1,0:T(8,128)}, f32[272,128]{1,0:T(8,128)S(1)}, u32[]{:S(2)}, u32[]{:S(2)}) collective-permute-start(f32[272,128]{1,0:T(8,128)} %copy-done.30), channel_id=1, source_target_pairs={{0,24},{4,28},{8,16},{12,20},{16,8},{20,12},{24,0},{28,4},{1,25},{... | collective-permute-start | bytes 417800 | tf_op jit(solution)/shard_map/ppermute | solution.py:491
  80.5 5.2 %collective-permute-done.1.refs_2_ = f32[272,128]{1,0:T(8,128)S(1)} collective-permute-done((f32[272,128]{1,0:T(8,128)}, f32[272,128]{1,0:T(8,128)S(1)}, u32[]{:S(2)}, u32[]{:S(2)}) %collective-permute-start.1) | collective-permute-done | bytes 139296 | tf_op jit(solution)/shard_map/ppermute | solution.py:491
  85.7 3.3 %collective-permute-start.6 = (f32[272,128]{1,0:T(8,128)}, f32[272,128]{1,0:T(8,128)S(1)}, u32[]{:S(2)}, u32[]{:S(2)}) collective-permute-start(f32[272,128]{1,0:T(8,128)} %copy-done.29), channel_id=1, source_target_pairs={{0,28},{4,24},{8,20},{12,16},{16,12},{20,8},{24,4},{28,0},{1,29},{... | collective-permute-start | bytes 417800 | tf_op jit(solution)/shard_map/ppermute | solution.py:491
  89.9 12.7 %collective-permute-done.3.refs_4_ = f32[272,128]{1,0:T(8,128)S(1)} collective-permute-done((f32[272,128]{1,0:T(8,128)}, f32[272,128]{1,0:T(8,128)S(1)}, u32[]{:S(2)}, u32[]{:S(2)}) %collective-permute-start.3) | collective-permute-done | bytes 139296 | tf_op jit(solution)/shard_map/ppermute | solution.py:491
  102.6 3.0 %collective-permute-done.4.refs_5_ = f32[272,128]{1,0:T(8,128)S(1)} collective-permute-done((f32[272,128]{1,0:T(8,128)}, f32[272,128]{1,0:T(8,128)S(1)}, u32[]{:S(2)}, u32[]{:S(2)}) %collective-permute-start.4) | collective-permute-done | bytes 139296 | tf_op jit(solution)/shard_map/ppermute | solution.py:491
  105.6 4.4 %collective-permute-done.5.refs_6_ = f32[272,128]{1,0:T(8,128)S(1)} collective-permute-done((f32[272,128]{1,0:T(8,128)}, f32[272,128]{1,0:T(8,128)S(1)}, u32[]{:S(2)}, u32[]{:S(2)}) %collective-permute-start.5) | collective-permute-done | bytes 139296 | tf_op jit(solution)/shard_map/ppermute | solution.py:491
  109.9 3.8 %collective-permute-done.6.refs_7_ = f32[272,128]{1,0:T(8,128)S(1)} collective-permute-done((f32[272,128]{1,0:T(8,128)}, f32[272,128]{1,0:T(8,128)S(1)}, u32[]{:S(2)}, u32[]{:S(2)}) %collective-permute-start.6) | collective-permute-done | bytes 139296 | tf_op jit(solution)/shard_map/ppermute | solution.py:491
  113.8 14.7 %shard_map.105 = (f32[216,128]{1,0:T(8,128)S(1)}, f32[216,128]{1,0:T(8,128)}, f32[216,128]{1,0:T(8,128)}, f32[216,128]{1,0:T(8,128)}, f32[216,128]{1,0:T(8,128)S...) custom-call(s32[1]{0:T(128)} %bitcast.me_ref, s32[9]{0:T(128)S(1)} %convert_reduce_fusion.firsts_ref, ...), custom_call_target="tpu_custom_call" | custom-call | flops 20000000 | bytes 3510312 | tf_op jit(solution)/shard_map/pallas_call | solution.py:457
  129.2 2.4 %collective-permute-start.11 = (f32[216,128]{1,0:T(8,128)S(1)}, f32[216,128]{1,0:T(8,128)S(1)}, u32[]{:S(2)}, u32[]{:S(2)}) collective-permute-start(f32[216,128]{1,0:T(8,128)S(1)} %get-tuple-element.59), channel_id=1, source_target_pairs={{0,20},{4,16},{8,28},{12,24},{16,4},{20,0},{24,12},{28,8},{1,21},{... | collective-permute-start | bytes 331784 | tf_op jit(solution)/shard_map/ppermute | solution.py:491
  134.9 9.8 %collective-permute-start.8 = (f32[216,128]{1,0:T(8,128)}, f32[216,128]{1,0:T(8,128)}, u32[]{:S(2)}, u32[]{:S(2)}) collective-permute-start(f32[216,128]{1,0:T(8,128)} %get-tuple-element.56), channel_id=1, source_target_pairs={{0,8},{4,12},{8,0},{12,4},{16,24},{20,28},{24,16},{28,20},{1,9},{5... | collective-permute-start | bytes 331784 | tf_op jit(solution)/shard_map/ppermute | solution.py:491
  145.4 2.5 %collective-permute-start.9 = (f32[216,128]{1,0:T(8,128)}, f32[216,128]{1,0:T(8,128)}, u32[]{:S(2)}, u32[]{:S(2)}) collective-permute-start(f32[216,128]{1,0:T(8,128)} %get-tuple-element.57), channel_id=1, source_target_pairs={{0,12},{4,8},{8,4},{12,0},{16,28},{20,24},{24,20},{28,16},{1,13},{... | collective-permute-start | bytes 331784 | tf_op jit(solution)/shard_map/ppermute | solution.py:491
  147.9 7.3 %shard_map.106.refs_2_ = f32[5,216,512]{2,1,0:T(8,128)S(1)} custom-call(f32[216,648]{1,0:T(8,128)S(1)} %copy-done.12, f32[864,128]{1,0:T(8,128)S(1)} %bitcast.26, f32[2592,128]{1,0:T(8,128)S(1)} %bitcast.23, f32[864,128]{1,0:T(8,128)S(1)} %bitcast.28), custom_call_target="tpu_custom_call" | custom-call | flops 10000000 | bytes 2771712 | tf_op jit(solution)/shard_map/pallas_call | solution.py:457
  157.4 3.4 %shard_map.108 = (f32[5,216,512]{2,1,0:T(8,128)S(1)}, f32[180,256]{1,0:T(8,128)S(1)}, f32[180,256]{1,0:T(8,128)S(1)}, f32[180,256]{1,0:T(8,128)S(1)}, f32[180,256]{1,0:T(8,128)S(1)}) custom-call(f32[216,128]{1,0:T(8,128)S(1)} %copy-done.22, f32[216,128]{1,0:T(8,128)} %collective-permute-done.7.refs_1_, f32[216,128]{1,0:T(8,128)} %collective-permute-done.8.refs_2_, ...), custom_call_target="tpu_custom_call" | custom-call | flops 5000000 | bytes 3227648 | tf_op jit(solution)/shard_map/pallas_call | solution.py:457
  162.7 4.3 %collective-permute-start.15 = (f32[180,256]{1,0:T(8,128)S(1)}, f32[180,256]{1,0:T(8,128)S(1)}, u32[]{:S(2)}, u32[]{:S(2)}) collective-permute-start(f32[180,256]{1,0:T(8,128)S(1)} %get-tuple-element.64), channel_id=1, source_target_pairs={{4,0},{8,4},{12,8},{16,12},{20,16},{24,20},{28,24},{5,1},{9,5},{13... | collective-permute-start | bytes 552968 | tf_op jit(solution)/shard_map/ppermute | solution.py:589
  167.0 3.7 %collective-permute-start.16 = (f32[180,256]{1,0:T(8,128)S(1)}, f32[180,256]{1,0:T(8,128)S(1)}, u32[]{:S(2)}, u32[]{:S(2)}) collective-permute-start(f32[180,256]{1,0:T(8,128)S(1)} %get-tuple-element.65), channel_id=1, source_target_pairs={{0,1},{1,2},{2,3},{3,0},{4,5},{5,6},{6,7},{7,4},{8,9},{9,10},{10,1... | collective-permute-start | bytes 552968 | tf_op jit(solution)/shard_map/ppermute | solution.py:510
  170.8 3.2 %collective-permute-done.15.xr_ref = f32[180,256]{1,0:T(8,128)S(1)} collective-permute-done((f32[180,256]{1,0:T(8,128)S(1)}, f32[180,256]{1,0:T(8,128)S(1)}, u32[]{:S(2)}, u32[]{:S(2)}) %collective-permute-start.15) | collective-permute-done | bytes 184352 | tf_op jit(solution)/shard_map/ppermute | solution.py:589
  177.0 2.3 %collective-permute-done.19.er_ref = f32[60,128]{1,0:T(8,128)S(1)} collective-permute-done((f32[60,128]{1,0:T(8,128)S(1)}, f32[60,128]{1,0:T(8,128)S(1)}, u32[]{:S(2)}, u32[]{:S(2)}) %collective-permute-start.19) | collective-permute-done | bytes 30752 | tf_op jit(solution)/shard_map/ppermute | solution.py:510
  (109 shorter events, 45.0 us)
Async XLA Ops:
  1.3 10.1 %all-to-all-start = ((s32[8,1,256]{2,1,0:T(1,128)}), s32[8,1,256]{2,1,0:T(1,128)S(1)}, u32[]{:S(2)}, u32[]{:S(2)}) async-start(s32[8,1,256]{2,1,0:T(1,128)} %broadcast_in_dim.2), calls=%async_computation | async-start | bytes 16384 | tf_op jit(solution)/shard_map/all_to_all | solution.py:494
  15.3 29.5 %all-to-all-start.1 = ((f32[8,272,128]{2,1,0:T(8,128)}), f32[8,272,128]{2,1,0:T(8,128)S(1)}, u32[]{:S(2)}, u32[]{:S(2)}) async-start(f32[8,272,128]{2,1,0:T(8,128)} %copy-done.11), calls=%async_computation.1 | async-start | bytes 2228224 | tf_op jit(solution)/shard_map/all_to_all | solution.py:494
  61.2 52.5 %copy-start.18 = (f32[272,128]{1,0:T(8,128)S(1)}, f32[272,128]{1,0:T(8,128)}, u32[]{:S(2)}) copy-start(f32[272,128]{1,0:T(8,128)} %copy-done.17) | copy-start | bytes 417796
  61.2 94.0 %all-to-all-start.2 = ((f32[8,216,128]{2,1,0:T(8,128)}), f32[8,216,128]{2,1,0:T(8,128)S(1)}, u32[]{:S(2)}, u32[]{:S(2)}) async-start(f32[8,216,128]{2,1,0:T(8,128)} %shard_map.104.after_ref), calls=%async_computation.2 | async-start | bytes 1769472 | tf_op jit(solution)/shard_map/all_to_all | solution.py:494
  68.3 9.9 %collective-permute-start = (f32[272,128]{1,0:T(8,128)}, f32[272,128]{1,0:T(8,128)S(1)}, u32[]{:S(2)}, u32[]{:S(2)}) collective-permute-start(f32[272,128]{1,0:T(8,128)} %copy-done.35), channel_id=1, source_target_pairs={{0,4},{4,0},{8,12},{12,8},{16,20},{20,16},{24,28},{28,24},{1,5},{5... | collective-permute-start | bytes 417800 | tf_op jit(solution)/shard_map/ppermute | solution.py:491
  69.5 16.2 %collective-permute-start.1 = (f32[272,128]{1,0:T(8,128)}, f32[272,128]{1,0:T(8,128)S(1)}, u32[]{:S(2)}, u32[]{:S(2)}) collective-permute-start(f32[272,128]{1,0:T(8,128)} %copy-done.34), channel_id=1, source_target_pairs={{0,8},{4,12},{8,0},{12,4},{16,24},{20,28},{24,16},{28,20},{1,9},{5... | collective-permute-start | bytes 417800 | tf_op jit(solution)/shard_map/ppermute | solution.py:491
  69.8 20.1 %collective-permute-start.2 = (f32[272,128]{1,0:T(8,128)}, f32[272,128]{1,0:T(8,128)S(1)}, u32[]{:S(2)}, u32[]{:S(2)}) collective-permute-start(f32[272,128]{1,0:T(8,128)} %copy-done.33), channel_id=1, source_target_pairs={{0,12},{4,8},{8,4},{12,0},{16,28},{20,24},{24,20},{28,16},{1,13},{... | collective-permute-start | bytes 417800 | tf_op jit(solution)/shard_map/ppermute | solution.py:491
  71.0 31.6 %collective-permute-start.3 = (f32[272,128]{1,0:T(8,128)}, f32[272,128]{1,0:T(8,128)S(1)}, u32[]{:S(2)}, u32[]{:S(2)}) collective-permute-start(f32[272,128]{1,0:T(8,128)} %copy-done.32), channel_id=1, source_target_pairs={{0,16},{4,20},{8,24},{12,28},{16,0},{20,4},{24,8},{28,12},{1,17},{... | collective-permute-start | bytes 417800 | tf_op jit(solution)/shard_map/ppermute | solution.py:491
  73.1 32.5 %collective-permute-start.4 = (f32[272,128]{1,0:T(8,128)}, f32[272,128]{1,0:T(8,128)S(1)}, u32[]{:S(2)}, u32[]{:S(2)}) collective-permute-start(f32[272,128]{1,0:T(8,128)} %copy-done.31), channel_id=1, source_target_pairs={{0,20},{4,16},{8,28},{12,24},{16,4},{20,0},{24,12},{28,8},{1,21},{... | collective-permute-start | bytes 417800 | tf_op jit(solution)/shard_map/ppermute | solution.py:491
  78.3 31.7 %collective-permute-start.5 = (f32[272,128]{1,0:T(8,128)}, f32[272,128]{1,0:T(8,128)S(1)}, u32[]{:S(2)}, u32[]{:S(2)}) collective-permute-start(f32[272,128]{1,0:T(8,128)} %copy-done.30), channel_id=1, source_target_pairs={{0,24},{4,28},{8,16},{12,20},{16,8},{20,12},{24,0},{28,4},{1,25},{... | collective-permute-start | bytes 417800 | tf_op jit(solution)/shard_map/ppermute | solution.py:491
  85.7 28.0 %collective-permute-start.6 = (f32[272,128]{1,0:T(8,128)}, f32[272,128]{1,0:T(8,128)S(1)}, u32[]{:S(2)}, u32[]{:S(2)}) collective-permute-start(f32[272,128]{1,0:T(8,128)} %copy-done.29), channel_id=1, source_target_pairs={{0,28},{4,24},{8,20},{12,16},{16,12},{20,8},{24,4},{28,0},{1,29},{... | collective-permute-start | bytes 417800 | tf_op jit(solution)/shard_map/ppermute | solution.py:491
  129.2 5.1 %collective-permute-start.10 = (f32[216,128]{1,0:T(8,128)S(1)}, f32[216,128]{1,0:T(8,128)S(1)}, u32[]{:S(2)}, u32[]{:S(2)}) collective-permute-start(f32[216,128]{1,0:T(8,128)S(1)} %get-tuple-element.58), channel_id=1, source_target_pairs={{0,16},{4,20},{8,24},{12,28},{16,0},{20,4},{24,8},{28,12},{1,17},{... | collective-permute-start | bytes 331784 | tf_op jit(solution)/shard_map/ppermute | solution.py:491
  129.2 15.6 %collective-permute-start.11 = (f32[216,128]{1,0:T(8,128)S(1)}, f32[216,128]{1,0:T(8,128)S(1)}, u32[]{:S(2)}, u32[]{:S(2)}) collective-permute-start(f32[216,128]{1,0:T(8,128)S(1)} %get-tuple-element.59), channel_id=1, source_target_pairs={{0,20},{4,16},{8,28},{12,24},{16,4},{20,0},{24,12},{28,8},{1,21},{... | collective-permute-start | bytes 331784 | tf_op jit(solution)/shard_map/ppermute | solution.py:491
  131.6 25.7 %collective-permute-start.12 = (f32[216,128]{1,0:T(8,128)}, f32[216,128]{1,0:T(8,128)}, u32[]{:S(2)}, u32[]{:S(2)}) collective-permute-start(f32[216,128]{1,0:T(8,128)} %get-tuple-element.60), channel_id=1, source_target_pairs={{0,24},{4,28},{8,16},{12,20},{16,8},{20,12},{24,0},{28,4},{1,25},{... | collective-permute-start | bytes 331784 | tf_op jit(solution)/shard_map/ppermute | solution.py:491
  132.3 25.0 %collective-permute-start.13 = (f32[216,128]{1,0:T(8,128)}, f32[216,128]{1,0:T(8,128)}, u32[]{:S(2)}, u32[]{:S(2)}) collective-permute-start(f32[216,128]{1,0:T(8,128)} %get-tuple-element.61), channel_id=1, source_target_pairs={{0,28},{4,24},{8,20},{12,16},{16,12},{20,8},{24,4},{28,0},{1,29},{... | collective-permute-start | bytes 331784 | tf_op jit(solution)/shard_map/ppermute | solution.py:491
  133.9 23.5 %collective-permute-start.7 = (f32[216,128]{1,0:T(8,128)}, f32[216,128]{1,0:T(8,128)}, u32[]{:S(2)}, u32[]{:S(2)}) collective-permute-start(f32[216,128]{1,0:T(8,128)} %get-tuple-element.55), channel_id=1, source_target_pairs={{0,4},{4,0},{8,12},{12,8},{16,20},{20,16},{24,28},{28,24},{1,5},{5... | collective-permute-start | bytes 331784 | tf_op jit(solution)/shard_map/ppermute | solution.py:491
  134.9 22.5 %collective-permute-start.8 = (f32[216,128]{1,0:T(8,128)}, f32[216,128]{1,0:T(8,128)}, u32[]{:S(2)}, u32[]{:S(2)}) collective-permute-start(f32[216,128]{1,0:T(8,128)} %get-tuple-element.56), channel_id=1, source_target_pairs={{0,8},{4,12},{8,0},{12,4},{16,24},{20,28},{24,16},{28,20},{1,9},{5... | collective-permute-start | bytes 331784 | tf_op jit(solution)/shard_map/ppermute | solution.py:491
  145.4 12.0 %collective-permute-start.9 = (f32[216,128]{1,0:T(8,128)}, f32[216,128]{1,0:T(8,128)}, u32[]{:S(2)}, u32[]{:S(2)}) collective-permute-start(f32[216,128]{1,0:T(8,128)} %get-tuple-element.57), channel_id=1, source_target_pairs={{0,12},{4,8},{8,4},{12,0},{16,28},{20,24},{24,20},{28,16},{1,13},{... | collective-permute-start | bytes 331784 | tf_op jit(solution)/shard_map/ppermute | solution.py:491
  160.8 9.9 %collective-permute-start.14 = (f32[180,256]{1,0:T(8,128)S(1)}, f32[180,256]{1,0:T(8,128)S(1)}, u32[]{:S(2)}, u32[]{:S(2)}) collective-permute-start(f32[180,256]{1,0:T(8,128)S(1)} %get-tuple-element.63), channel_id=1, source_target_pairs={{0,4},{4,8},{8,12},{12,16},{16,20},{20,24},{24,28},{1,5},{5,9},{9,... | collective-permute-start | bytes 552968 | tf_op jit(solution)/shard_map/ppermute | solution.py:588
  162.7 11.2 %collective-permute-start.15 = (f32[180,256]{1,0:T(8,128)S(1)}, f32[180,256]{1,0:T(8,128)S(1)}, u32[]{:S(2)}, u32[]{:S(2)}) collective-permute-start(f32[180,256]{1,0:T(8,128)S(1)} %get-tuple-element.64), channel_id=1, source_target_pairs={{4,0},{8,4},{12,8},{16,12},{20,16},{24,20},{28,24},{5,1},{9,5},{13... | collective-permute-start | bytes 552968 | tf_op jit(solution)/shard_map/ppermute | solution.py:589
  167.0 8.9 %collective-permute-start.16 = (f32[180,256]{1,0:T(8,128)S(1)}, f32[180,256]{1,0:T(8,128)S(1)}, u32[]{:S(2)}, u32[]{:S(2)}) collective-permute-start(f32[180,256]{1,0:T(8,128)S(1)} %get-tuple-element.65), channel_id=1, source_target_pairs={{0,1},{1,2},{2,3},{3,0},{4,5},{5,6},{6,7},{7,4},{8,9},{9,10},{10,1... | collective-permute-start | bytes 552968 | tf_op jit(solution)/shard_map/ppermute | solution.py:510
  170.7 5.2 %collective-permute-start.17 = (f32[180,256]{1,0:T(8,128)S(1)}, f32[180,256]{1,0:T(8,128)S(1)}, u32[]{:S(2)}, u32[]{:S(2)}) collective-permute-start(f32[180,256]{1,0:T(8,128)S(1)} %get-tuple-element.66), channel_id=1, source_target_pairs={{0,3},{1,0},{2,1},{3,2},{4,7},{5,4},{6,5},{7,6},{8,11},{9,8},{10,9... | collective-permute-start | bytes 552968 | tf_op jit(solution)/shard_map/ppermute | solution.py:510
  174.0 3.0 %collective-permute-start.18 = (f32[60,128]{1,0:T(8,128)S(1)}, f32[60,128]{1,0:T(8,128)S(1)}, u32[]{:S(2)}, u32[]{:S(2)}) collective-permute-start(f32[60,128]{1,0:T(8,128)S(1)} %get-tuple-element.67), channel_id=1, source_target_pairs={{0,1},{1,2},{2,3},{3,0},{4,5},{5,6},{6,7},{7,4},{8,9},{9,10},{10,1... | collective-permute-start | bytes 92168 | tf_op jit(solution)/shard_map/ppermute | solution.py:510
  175.9 3.3 %collective-permute-start.19 = (f32[60,128]{1,0:T(8,128)S(1)}, f32[60,128]{1,0:T(8,128)S(1)}, u32[]{:S(2)}, u32[]{:S(2)}) collective-permute-start(f32[60,128]{1,0:T(8,128)S(1)} %get-tuple-element.68), channel_id=1, source_target_pairs={{0,3},{1,0},{2,1},{3,2},{4,7},{5,4},{6,5},{7,6},{8,11},{9,8},{10,9... | collective-permute-start | bytes 92168 | tf_op jit(solution)/shard_map/ppermute | solution.py:510
  (35 other events, 246.7 us)
